TPU v7x, 32 devices: a whole 2x2x4 slice. The times are simulated.
32 devices in a mesh: dp: 4 (over z), expert: 8 (over y, x, core).
Axes of the slice: x: 2, y: 2, z: 4, core: 2. Of those that a mesh axis runs over, the one named last changes fastest.
Arguments:
- inputs: bfloat16 [4096, 2048], P(('dp', 'expert')), may hold values from -6 to 6
- segments: int32 [32, 128], P(('dp', 'expert')), may hold values from 0 to 3, never falling along the last dimension, each value on 1 to 64 neighbouring positions
- routes: int32 [4096, 8], P(('dp', 'expert')), may hold values from 0 to 15, all different within a row; in each aligned block of 128 rows (0 to 127, 128 to 255, ...) at most 96 rows name the same one
- w_qkv: bfloat16 [2048, 3, 2048], P('dp'), may hold values from -0.125 to 0.125
- w_out: bfloat16 [2048, 2048], P('dp'), may hold values from -0.5 to 0.5
- w_router: bfloat16 [2048, 16], P('dp'), may hold values from -0.375 to 0.375
- gains: bfloat16 [2048, 4], P('dp'), may hold values from 0.5 to 1.5
- w_gate: bfloat16 [16, 2048, 1024], P('expert'), may hold values from -0.125 to 0.125
- w_up: bfloat16 [16, 2048, 1024], P('expert'), may hold values from -0.125 to 0.125
- w_down: bfloat16 [16, 1024, 2048], P('expert'), may hold values from -0.375 to 0.375
- cotangent: bfloat16 [4096, 2048], P(('dp', 'expert')), may hold values from -6 to 6
Outputs:
- output: bfloat16 [4096, 2048], P(('dp', 'expert'))
- grad_inputs: bfloat16 [4096, 2048], P(('dp', 'expert'))
- grad_w_qkv: float32 [2048, 3, 2048], P('dp')
- grad_w_out: float32 [2048, 2048], P('dp')
- grad_w_router: float32 [2048, 16], P('dp')
- grad_gains: float32 [2048, 4], P('dp')
- grad_w_gate: float32 [16, 2048, 1024], P('expert', 'dp')
- grad_w_up: float32 [16, 2048, 1024], P('expert', 'dp')
- grad_w_down: float32 [16, 1024, 2048], P('expert', 'dp')
Inputs may be any that keep to these rules, and one draw needn't show every extreme that they name: `routes`: each token names 8 different experts. Within the 128 rows of one device no expert is named more than 96 times, and in every draw some device's rows name some expert exactly 96 times. `segments`: segment numbers never fall along a sequence.
All inputs are finite; a program needn't handle non-finite values.
Results may differ from a plain program's by a relative error of at most 0.018.
The roundings to bfloat16 on the way count: a program that leaves them out, or rounds other values in their place, can miss the bound.
Values may be sent and summed in bfloat16 or wider, within the bound.
A program may use at most 512 MiB of HBM per device.

v0:
```python
import jax
import jax.numpy as jnp
from jax import lax
from jax.sharding import PartitionSpec as P

HD = 128


eps_norm = 1e-05
rope_base = 10000.0
masked_score = -1e30


def rms_forward(values, gain_col):
    inv_rms = lax.rsqrt(jnp.mean(values * values, axis=-1, keepdims=True) + eps_norm)
    return (values * inv_rms * gain_col, inv_rms)


def rms_backward(values, inv_rms, gain_col, grad_out):
    normed = values * inv_rms
    grad_gain = jnp.sum(grad_out * normed, axis=0)
    scaled = grad_out * gain_col
    grad_values = inv_rms * (scaled - normed * jnp.mean(scaled * normed, axis=-1, keepdims=True))
    return (grad_values, grad_gain)


def rope_tables(length, head_width):
    half_width = head_width // 2
    freqs = jnp.exp(
        -jnp.log(rope_base) * (2.0 * jnp.arange(half_width, dtype=jnp.float32) / head_width)
    )
    angles = jnp.arange(length, dtype=jnp.float32)[:, None] * freqs[None, :]
    return (jnp.cos(angles)[:, None, :], jnp.sin(angles)[:, None, :])


def rotate(values, cos_tab, sin_tab):
    half_width = values.shape[-1] // 2
    first_half = values[..., :half_width]
    second_half = values[..., half_width:]
    return jnp.concatenate(
        [
            first_half * cos_tab - second_half * sin_tab,
            second_half * cos_tab + first_half * sin_tab,
        ],
        axis=-1,
    )


def rotate_back(values, cos_tab, sin_tab):
    half_width = values.shape[-1] // 2
    first_half = values[..., :half_width]
    second_half = values[..., half_width:]
    return jnp.concatenate(
        [
            first_half * cos_tab + second_half * sin_tab,
            second_half * cos_tab - first_half * sin_tab,
        ],
        axis=-1,
    )


def attend_scores(query_rot, key_rot, seg_ids):
    places = jnp.arange(seg_ids.shape[0], dtype=jnp.int32)
    allowed = (places[:, None] >= places[None, :]) & (seg_ids[:, None] == seg_ids[None, :])
    scores = jnp.einsum("qhd,khd->hqk", query_rot, key_rot, preferred_element_type=jnp.float32)
    scores = scores * query_rot.shape[-1] ** (-0.5)
    return jnp.where(allowed[None], scores, masked_score)


def attend_forward(query_rot, key_rot, value_bf, seg_ids):
    scores = attend_scores(query_rot, key_rot, seg_ids)
    row_max = jnp.max(scores, axis=-1, keepdims=True)
    log_total = row_max + jnp.log(jnp.sum(jnp.exp(scores - row_max), axis=-1, keepdims=True))
    weights_bf = jnp.exp(scores - log_total).astype(jnp.bfloat16)
    mixed_heads = jnp.einsum(
        "hqk,khd->qhd", weights_bf, value_bf, preferred_element_type=jnp.float32
    )
    return (mixed_heads.astype(jnp.bfloat16), log_total)


def attend_backward(query_rot, key_rot, value_bf, seg_ids, log_total, grad_heads):
    scores = attend_scores(query_rot, key_rot, seg_ids)
    probs_full = jnp.exp(scores - log_total)
    probs_bf = probs_full.astype(jnp.bfloat16)
    grad_value = jnp.einsum(
        "hqk,qhd->khd", probs_bf, grad_heads, preferred_element_type=jnp.float32
    ).astype(jnp.bfloat16)
    grad_probs = jnp.einsum(
        "qhd,khd->hqk", grad_heads, value_bf, preferred_element_type=jnp.float32
    )
    delta_rows = jnp.sum(probs_full * grad_probs, axis=-1, keepdims=True)
    grad_scores = (probs_full * (grad_probs - delta_rows) * query_rot.shape[-1] ** (-0.5)).astype(
        jnp.bfloat16
    )
    grad_query = jnp.einsum(
        "hqk,khd->qhd", grad_scores, key_rot, preferred_element_type=jnp.float32
    )
    grad_key = jnp.einsum(
        "hqk,qhd->khd", grad_scores, query_rot, preferred_element_type=jnp.float32
    )
    return (grad_query, grad_key, grad_value)


def mixer_forward(inputs, seg_all, qkv_mat, out_mat, gain_mat):
    count, model_width = inputs.shape
    num_seqs, length = seg_all.shape
    head_count = model_width // HD
    shape_heads = (num_seqs, length, head_count, HD)
    inputs_f = inputs.astype(jnp.float32)
    normed_one, scale_one = rms_forward(inputs_f, gain_mat[:, 0])
    normed_one = normed_one.astype(jnp.bfloat16)
    projected = jnp.dot(
        normed_one,
        qkv_mat.reshape(model_width, 3 * model_width),
        preferred_element_type=jnp.float32,
    )
    query_raw = projected[:, :model_width]
    key_raw = projected[:, model_width : 2 * model_width]
    value_raw = projected[:, 2 * model_width :]
    query_norm, query_scale = rms_forward(query_raw, gain_mat[:, 1])
    key_norm, key_scale = rms_forward(key_raw, gain_mat[:, 2])
    cos_tab, sin_tab = rope_tables(length, HD)
    query_rot = rotate(query_norm.reshape(shape_heads), cos_tab, sin_tab).astype(jnp.bfloat16)
    key_rot = rotate(key_norm.reshape(shape_heads), cos_tab, sin_tab).astype(jnp.bfloat16)
    value_bf = value_raw.astype(jnp.bfloat16).reshape(shape_heads)
    mixed_heads, log_total = jax.vmap(attend_forward)(query_rot, key_rot, value_bf, seg_all)
    attn_flat = mixed_heads.reshape(count, model_width)
    after_attn = inputs_f + jnp.dot(attn_flat, out_mat, preferred_element_type=jnp.float32)
    saved = (
        inputs_f,
        scale_one,
        normed_one,
        query_raw,
        query_scale,
        key_raw,
        key_scale,
        query_rot,
        key_rot,
        value_bf,
        attn_flat,
        log_total,
    )
    return (after_attn, saved)


def mixer_backward(saved, seg_all, qkv_mat, out_mat, gain_mat, grad_mid):
    (
        inputs_f,
        scale_one,
        normed_one,
        query_raw,
        query_scale,
        key_raw,
        key_scale,
        query_rot,
        key_rot,
        value_bf,
        attn_flat,
        log_total,
    ) = saved
    count, model_width = inputs_f.shape
    num_seqs, length = seg_all.shape
    head_count = model_width // HD
    shape_heads = (num_seqs, length, head_count, HD)
    grad_mid_bf = grad_mid.astype(jnp.bfloat16)
    grad_out_mat = jnp.dot(attn_flat.T, grad_mid_bf, preferred_element_type=jnp.float32)
    grad_heads = (
        jnp.dot(grad_mid_bf, out_mat.T, preferred_element_type=jnp.float32)
        .astype(jnp.bfloat16)
        .reshape(shape_heads)
    )
    grad_query, grad_key, grad_value = jax.vmap(attend_backward)(
        query_rot, key_rot, value_bf, seg_all, log_total, grad_heads
    )
    cos_tab, sin_tab = rope_tables(length, HD)
    grad_qnorm = rotate_back(grad_query, cos_tab, sin_tab).reshape(count, model_width)
    grad_knorm = rotate_back(grad_key, cos_tab, sin_tab).reshape(count, model_width)
    grad_qraw, gain_query = rms_backward(query_raw, query_scale, gain_mat[:, 1], grad_qnorm)
    grad_kraw, gain_key = rms_backward(key_raw, key_scale, gain_mat[:, 2], grad_knorm)
    grad_proj = jnp.concatenate(
        [
            grad_qraw.astype(jnp.bfloat16),
            grad_kraw.astype(jnp.bfloat16),
            grad_value.reshape(count, model_width),
        ],
        axis=1,
    )
    grad_qkv_mat = jnp.dot(normed_one.T, grad_proj, preferred_element_type=jnp.float32).reshape(
        model_width, 3, model_width
    )
    grad_normed = jnp.dot(
        grad_proj,
        qkv_mat.reshape(model_width, 3 * model_width).T,
        preferred_element_type=jnp.float32,
    )
    grad_front, gain_attn = rms_backward(inputs_f, scale_one, gain_mat[:, 0], grad_normed)
    return (grad_mid + grad_front, grad_qkv_mat, grad_out_mat, gain_attn, gain_query, gain_key)


def router_forward(after_attn, router_mat, gain_mat, route_ids):
    normed_two, scale_two = rms_forward(after_attn, gain_mat[:, 3])
    normed_two = normed_two.astype(jnp.bfloat16)
    logits = jnp.dot(normed_two, router_mat, preferred_element_type=jnp.float32)
    probs = jax.nn.softmax(logits, axis=-1)
    expert_ids = jnp.arange(router_mat.shape[1], dtype=jnp.int32)
    picks = (route_ids[:, :, None] == expert_ids[None, None, :]).astype(jnp.float32)
    gate_vals = jnp.sum(picks * probs[:, None, :], axis=-1)
    return (normed_two, scale_two, probs, picks, gate_vals)


def router_backward(
    after_attn,
    scale_two,
    normed_two,
    probs,
    picks,
    grad_gates,
    router_mat,
    gain_mat,
    grad_from_experts,
):
    grad_probs = jnp.sum(picks * grad_gates[:, :, None], axis=1)
    grad_logits = probs * (grad_probs - jnp.sum(probs * grad_probs, axis=-1, keepdims=True))
    grad_logits = grad_logits.astype(jnp.bfloat16)
    grad_router_mat = jnp.dot(normed_two.T, grad_logits, preferred_element_type=jnp.float32)
    grad_normed = grad_from_experts + jnp.dot(
        grad_logits, router_mat.T, preferred_element_type=jnp.float32
    )
    grad_mid, gain_ffn = rms_backward(after_attn, scale_two, gain_mat[:, 3], grad_normed)
    return (grad_mid, grad_router_mat, gain_ffn)


def slot_positions(flat_routes, expert_count):
    marks = (flat_routes[:, None] == jnp.arange(expert_count, dtype=jnp.int32)[None, :]).astype(
        jnp.int32
    )
    return jnp.sum(marks * jnp.cumsum(marks, axis=0), axis=1) - 1


def body(inputs, segments, routes, w_qkv, w_out, w_router, gains, w_gate, w_up, w_down, cotangent):
    full_qkv, full_out, full_router, full_gains = (
        lax.all_gather(w_qkv, "dp", axis=0, tiled=True),
        lax.all_gather(w_out, "dp", axis=0, tiled=True),
        lax.all_gather(w_router, "dp", axis=0, tiled=True),
        lax.all_gather(gains, "dp", axis=0, tiled=True),
    )
    gain_mat = full_gains.astype(jnp.float32)
    after_attn, saved = mixer_forward(inputs, segments, full_qkv, full_out, gain_mat)
    normed_two, scale_two, probs, picks, gate_vals = router_forward(
        after_attn, full_router, gain_mat, routes
    )
    count, model_width = inputs.shape
    top_count = routes.shape[1]
    expert_count = full_router.shape[1]
    capacity = 3 * count * top_count // (2 * expert_count)
    flat_routes = routes.reshape(-1)
    slots = flat_routes * capacity + slot_positions(flat_routes, expert_count)

    def dispatch_rows(pair_rows):
        buffer = jnp.zeros((expert_count * capacity, model_width), jnp.bfloat16)
        buffer = buffer.at[slots].set(pair_rows.reshape(-1, model_width))
        return buffer.reshape(expert_count, capacity, model_width)

    def collect_rows(returned):
        return returned.reshape(-1, model_width)[slots].reshape(count, top_count, model_width)

    sent_rows = dispatch_rows(
        jnp.broadcast_to(normed_two[:, None, :], (count, top_count, model_width))
    )
    received = lax.all_to_all(sent_rows, "expert", split_axis=0, concat_axis=1, tiled=True)
    gate_pre = jnp.einsum("erd,edf->erf", received, w_gate, preferred_element_type=jnp.float32)
    up_pre = jnp.einsum("erd,edf->erf", received, w_up, preferred_element_type=jnp.float32)
    sig_gate = jax.nn.sigmoid(gate_pre)
    silu_gate = gate_pre * sig_gate
    act_bf = (silu_gate * up_pre).astype(jnp.bfloat16)
    expert_out = jnp.einsum(
        "erf,efd->erd", act_bf, w_down, preferred_element_type=jnp.float32
    ).astype(jnp.bfloat16)
    returned = lax.all_to_all(expert_out, "expert", split_axis=1, concat_axis=0, tiled=True)
    picked = collect_rows(returned).astype(jnp.float32)
    mixed = jnp.sum(gate_vals[:, :, None] * picked, axis=1)
    output = (after_attn + mixed).astype(jnp.bfloat16)
    grad_top = cotangent.astype(jnp.float32)
    grad_gates = jnp.sum(grad_top[:, None, :] * picked, axis=-1)
    grad_pairs = (gate_vals[:, :, None] * grad_top[:, None, :]).astype(jnp.bfloat16)
    grad_received = lax.all_to_all(
        dispatch_rows(grad_pairs), "expert", split_axis=0, concat_axis=1, tiled=True
    )
    grad_act = jnp.einsum("erd,efd->erf", grad_received, w_down, preferred_element_type=jnp.float32)
    grad_gate_bf = (grad_act * up_pre * (sig_gate * (1.0 + gate_pre * (1.0 - sig_gate)))).astype(
        jnp.bfloat16
    )
    grad_up_bf = (grad_act * silu_gate).astype(jnp.bfloat16)
    local_down = jnp.einsum(
        "erf,erd->efd", act_bf, grad_received, preferred_element_type=jnp.float32
    )
    local_gate = jnp.einsum(
        "erd,erf->edf", received, grad_gate_bf, preferred_element_type=jnp.float32
    )
    local_up = jnp.einsum("erd,erf->edf", received, grad_up_bf, preferred_element_type=jnp.float32)
    grad_rows_in = jnp.einsum(
        "erf,edf->erd", grad_gate_bf, w_gate, preferred_element_type=jnp.float32
    ) + jnp.einsum("erf,edf->erd", grad_up_bf, w_up, preferred_element_type=jnp.float32)
    grad_back = lax.all_to_all(
        grad_rows_in.astype(jnp.bfloat16), "expert", split_axis=1, concat_axis=0, tiled=True
    )
    grad_from_experts = jnp.sum(collect_rows(grad_back).astype(jnp.float32), axis=1)
    grad_w_gate, grad_w_up, grad_w_down = (
        lax.psum_scatter(
            local_gate.astype(jnp.bfloat16), "dp", scatter_dimension=1, tiled=True
        ).astype(jnp.float32),
        lax.psum_scatter(
            local_up.astype(jnp.bfloat16), "dp", scatter_dimension=1, tiled=True
        ).astype(jnp.float32),
        lax.psum_scatter(
            local_down.astype(jnp.bfloat16), "dp", scatter_dimension=1, tiled=True
        ).astype(jnp.float32),
    )
    back_qkv, back_out, back_router, back_gains = (
        lax.all_gather(w_qkv, "dp", axis=0, tiled=True),
        lax.all_gather(w_out, "dp", axis=0, tiled=True),
        lax.all_gather(w_router, "dp", axis=0, tiled=True),
        lax.all_gather(gains, "dp", axis=0, tiled=True),
    )
    back_gain_mat = back_gains.astype(jnp.float32)
    grad_ffn, local_router, gain_ffn = router_backward(
        after_attn,
        scale_two,
        normed_two,
        probs,
        picks,
        grad_gates,
        back_router,
        back_gain_mat,
        grad_from_experts,
    )
    grad_mid = grad_top + grad_ffn
    grad_all, local_qkv, local_out, gain_attn, gain_query, gain_key = mixer_backward(
        saved, segments, back_qkv, back_out, back_gain_mat, grad_mid
    )
    local_gains = jnp.stack([gain_attn, gain_query, gain_key, gain_ffn], axis=1)
    shares = (
        lax.psum_scatter(local_qkv, ("dp", "expert"), scatter_dimension=0, tiled=True),
        lax.psum_scatter(local_out, ("dp", "expert"), scatter_dimension=0, tiled=True),
        lax.psum_scatter(local_router, ("dp", "expert"), scatter_dimension=0, tiled=True),
        lax.psum_scatter(local_gains, ("dp", "expert"), scatter_dimension=0, tiled=True),
    )
    grad_w_qkv, grad_w_out, grad_w_router, grad_gains = (
        lax.all_gather(shares[0].astype(jnp.bfloat16), "expert", axis=0, tiled=True).astype(
            jnp.float32
        ),
        lax.all_gather(shares[1].astype(jnp.bfloat16), "expert", axis=0, tiled=True).astype(
            jnp.float32
        ),
        lax.all_gather(shares[2].astype(jnp.bfloat16), "expert", axis=0, tiled=True).astype(
            jnp.float32
        ),
        lax.all_gather(shares[3].astype(jnp.bfloat16), "expert", axis=0, tiled=True).astype(
            jnp.float32
        ),
    )
    return (
        output,
        grad_all.astype(jnp.bfloat16),
        grad_w_qkv,
        grad_w_out,
        grad_w_router,
        grad_gains,
        grad_w_gate,
        grad_w_up,
        grad_w_down,
    )


def solution(mesh):
    return jax.shard_map(
        body,
        mesh=mesh,
        in_specs=(
            P(("dp", "expert"), None),
            P(("dp", "expert"), None),
            P(("dp", "expert"), None),
            P("dp", None, None),
            P("dp", None),
            P("dp", None),
            P("dp", None),
            P("expert", None, None),
            P("expert", None, None),
            P("expert", None, None),
            P(("dp", "expert"), None),
        ),
        out_specs=(
            P(("dp", "expert"), None),
            P(("dp", "expert"), None),
            P("dp", None, None),
            P("dp", None),
            P("dp", None),
            P("dp", None),
            P("expert", "dp", None),
            P("expert", "dp", None),
            P("expert", "dp", None),
        ),
        check_vma=False,
    )
```

profile of v0, /device:TPU:0, one launch (start us, length us, event | category | flops | bytes accessed | tf_op | source)
XLA Modules:
  0.0 2814.0 jit_solution(4152275836891686152)
XLA Ops:
  23.1 14.9 all_gather.28
  38.0 37.5 %all_gather.31 = bf16[2048,16]{0,1:T(8,128)(2,1)S(1)} all-gather(bf16[512,16]{0,1:T(8,128)(2,1)S(1)} %copy-done.44), channel_id=1, replica_groups=mesh['dp'=4,'expert'=8] {'dp'}, dimensions={0}, use_global_device_ids=true | all-gather | bytes 81920 | tf_op jit(solution)/shard_map/all_gather | solution.py:244
  76.3 368.6 %all-gather.7.cloned.1.call-done = bf16[2048,3,2048]{0,2,1:T(8,128)(2,1)} async-done(((bf16[512,3,2048]{0,2,1:T(8,128)(2,1)}), bf16[2048,3,2048]{0,2,1:T(8,128)(2,1)}) %all-gather.7.cloned.1.call-update) | async-done | bytes 25165840 | tf_op jit(solution)/shard_map/all_gather | solution.py:242
  444.9 13.6 fusion.61
  465.6 128.7 %all-gather.9.cloned.1.call-done = bf16[2048,2048]{1,0:T(8,128)(2,1)} async-done(((bf16[512,2048]{1,0:T(8,128)(2,1)}), bf16[2048,2048]{1,0:T(8,128)(2,1)}) %all-gather.9.cloned.1.call-update) | async-done | bytes 8388624 | tf_op jit(solution)/shard_map/all_gather | solution.py:243
  627.1 61.3 %all-to-all-done.2 = bf16[16,96,2048]{2,1,0:T(8,128)(2,1)} async-done(((bf16[16,96,2048]{2,1,0:T(8,128)(2,1)}), bf16[16,96,2048]{2,1,0:T(8,128)(2,1)}, u32[]{:S(2)}, u32[]{:S(2)}) %all-to-all-start.2) | async-done | bytes 6291488 | tf_op jit(solution)/shard_map/all_to_all | solution.py:286
  700.0 65.0 %all-to-all-done = bf16[16,96,2048]{2,1,0:T(8,128)(2,1)} async-done(((bf16[16,96,2048]{2,1,0:T(8,128)(2,1)}), bf16[16,96,2048]{2,1,0:T(8,128)(2,1)}, u32[]{:S(2)}, u32[]{:S(2)}) %all-to-all-start) | async-done | bytes 6291488 | tf_op jit(solution)/shard_map/all_to_all | solution.py:270
  768.5 13.0 fusion.88
  790.1 17.2 multiply_convert_fusion
  818.2 18.7 copy.262
  841.7 13.5 fusion.89
  855.2 14.3 add_convert_fusion
  869.5 12.6 copy.266
  882.1 31.2 %all-to-all-done.1 = bf16[2,768,2048]{2,0,1:T(2,128)(2,1)} async-done(((bf16[2,768,2048]{2,0,1:T(2,128)(2,1)}), bf16[2,768,2048]{2,0,1:T(2,128)(2,1)}, u32[]{:S(2)}, u32[]{:S(2)}) %all-to-all-start.1) | async-done | bytes 6291488 | tf_op jit(solution)/shard_map/all_to_all | solution.py:279
  926.9 12.4 gather_fusion
  944.3 45.3 %all-to-all-done.3 = bf16[2,768,2048]{2,0,1:T(2,128)(2,1)} async-done(((bf16[2,768,2048]{2,0,1:T(2,128)(2,1)}), bf16[2,768,2048]{2,0,1:T(2,128)(2,1)}, u32[]{:S(2)}, u32[]{:S(2)}) %all-to-all-start.3) | async-done | bytes 6291488 | tf_op jit(solution)/shard_map/all_to_all | solution.py:304
  998.0 12.6 gather_fusion.1
  1072.2 21.3 fusion.39
  1094.9 71.4 %copy.283 = f32[2048,3,2048]{2,1,0:T(4,128)} copy(f32[2048,3,2048]{0,2,1:T(8,128)} %bitcast.174) | data formatting | bytes 100663296 | tf_op jit(solution)/shard_map/reshape | solution.py:188
  1166.4 1116.6 %all-reduce.2 = bf16[2048,3,2048]{2,1,0:T(4,128)(2,1)} all-reduce(f32[2048,3,2048]{2,1,0:T(4,128)} %copy.283), channel_id=2, replica_groups=mesh['dp'=4,'expert'=8] {'dp','expert'}, use_global_device_ids=true, to_apply=%region_24.25.clone | all-reduce | flops 12582912 | bytes 75497472
  2355.2 121.7 %reduce-scatter.17.cloned.1.call-done = bf16[2,256,2048]{2,1,0:T(8,128)(2,1)} async-done(((bf16[2,1024,2048]{2,1,0:T(8,128)(2,1)}), bf16[2,256,2048]{2,1,0:T(8,128)(2,1)}) %reduce-scatter.17.cloned.1.call-update) | async-done | bytes 2097168 | tf_op jit(solution)/shard_map/reduce_scatter | solution.py:315
  2481.0 143.5 %reduce-scatter.15.cloned.1.call-done = bf16[2,512,1024]{2,1,0:T(8,128)(2,1)} async-done(((bf16[2,2048,1024]{2,1,0:T(8,128)(2,1)}), bf16[2,512,1024]{2,1,0:T(8,128)(2,1)}) %reduce-scatter.15.cloned.1.call-update) | async-done | bytes 2097168 | tf_op jit(solution)/shard_map/reduce_scatter | solution.py:312
  2628.6 143.6 %reduce-scatter.13.cloned.1.call-done = bf16[2,512,1024]{2,1,0:T(8,128)(2,1)} async-done(((bf16[2,2048,1024]{2,1,0:T(8,128)(2,1)}), bf16[2,512,1024]{2,1,0:T(8,128)(2,1)}) %reduce-scatter.13.cloned.1.call-update) | async-done | bytes 2097168 | tf_op jit(solution)/shard_map/reduce_scatter | solution.py:309
  2776.2 26.7 all-gather.13.cloned.1.call-done
  (246 shorter events, 273.4 us)
Async XLA Ops:
  7.2 437.8 %all-gather.7.cloned.1.call-start = ((), (), s32[]{:S(2)}) async-start(), calls=%async_computation.10 | async-start | bytes 31457280 | tf_op jit(solution)/shard_map/all_gather | solution.py:242
  15.9 60.0 %copy-start.52 = (s32[1,128]{1,0:T(1,128)S(1)}, s32[1,128]{1,0:T(1,128)}, u32[]{:S(2)}) copy-start(s32[1,128]{1,0:T(1,128)} %param.12) | copy-start | bytes 1540
  15.9 578.4 %all-gather.9.cloned.1.call-start = ((), (), s32[]{:S(2)}) async-start(), calls=%async_computation.11 | async-start | bytes 10485760 | tf_op jit(solution)/shard_map/all_gather | solution.py:243
  75.5 525.1 %copy-start.31 = (bf16[2048,16]{0,1:T(8,128)(2,1)}, bf16[2048,16]{0,1:T(8,128)(2,1)S(1)}, u32[]{:S(2)}) copy-start(bf16[2048,16]{0,1:T(8,128)(2,1)S(1)} %all_gather.31) | copy-start | bytes 196612
  75.8 382.8 %copy-start.42 = (f32[128]{0:T(128)}, f32[128]{0:T(128)S(1)}, u32[]{:S(2)}) copy-start(f32[128]{0:T(128)S(1)} %add_rsqrt_fusion.3) | copy-start | bytes 1540
  76.2 384.2 %copy-start.27 = (f32[128,64]{1,0:T(8,128)}, f32[128,64]{1,0:T(8,128)S(1)}, u32[]{:S(2)}) copy-start(f32[128,64]{1,0:T(8,128)S(1)} %get-tuple-element.70) | copy-start | bytes 98308
  76.2 384.2 %copy-start.29 = (f32[128,64]{1,0:T(8,128)}, f32[128,64]{1,0:T(8,128)S(1)}, u32[]{:S(2)}) copy-start(f32[128,64]{1,0:T(8,128)S(1)} %get-tuple-element.71) | copy-start | bytes 98308
  76.3 382.3 %copy-start.25 = (f32[2048,1]{0,1:T(1,128)}, f32[2048,1]{0,1:T(1,128)S(1)}, u32[]{:S(2)}) copy-start(f32[2048,1]{0,1:T(1,128)S(1)} %get-tuple-element.69) | copy-start | bytes 24580
  76.3 382.6 %copy-start.33 = (f32[2048,1]{0,1:T(1,128)}, f32[2048,1]{0,1:T(1,128)S(1)}, u32[]{:S(2)}) copy-start(f32[2048,1]{0,1:T(1,128)S(1)} %get-tuple-element.67) | copy-start | bytes 24580
  76.3 382.6 %copy-start.35 = (f32[2048,1]{0,1:T(1,128)}, f32[2048,1]{0,1:T(1,128)S(1)}, u32[]{:S(2)}) copy-start(f32[2048,1]{0,1:T(1,128)S(1)} %get-tuple-element.68) | copy-start | bytes 24580
  76.3 523.1 %copy-start.37 = (f32[2048,1]{0,1:T(1,128)}, f32[2048,1]{0,1:T(1,128)S(1)}, u32[]{:S(2)}) copy-start(f32[2048,1]{0,1:T(1,128)S(1)} %get-tuple-element.66) | copy-start | bytes 24580
  464.4 134.9 %copy-start.39 = (f32[16,128]{1,0:T(8,128)}, f32[16,128]{1,0:T(8,128)S(1)}, u32[]{:S(2)}) copy-start(f32[16,128]{1,0:T(8,128)S(1)} %log_add_fusion) | copy-start | bytes 24580
  612.1 76.3 %all-to-all-start.2 = ((bf16[16,96,2048]{2,1,0:T(8,128)(2,1)}), bf16[16,96,2048]{2,1,0:T(8,128)(2,1)}, u32[]{:S(2)}, u32[]{:S(2)}) async-start(bf16[16,96,2048]{2,1,0:T(8,128)(2,1)} %bitcast.178), calls=%async_computation.2 | async-start | bytes 12582912 | tf_op jit(solution)/shard_map/all_to_all | solution.py:286
  688.4 76.5 %all-to-all-start = ((bf16[16,96,2048]{2,1,0:T(8,128)(2,1)}), bf16[16,96,2048]{2,1,0:T(8,128)(2,1)}, u32[]{:S(2)}, u32[]{:S(2)}) async-start(bf16[16,96,2048]{2,1,0:T(8,128)(2,1)} %bitcast.177), calls=%async_computation | async-start | bytes 12582912 | tf_op jit(solution)/shard_map/all_to_all | solution.py:270
  837.0 76.3 %all-to-all-start.1 = ((bf16[2,768,2048]{2,0,1:T(2,128)(2,1)}), bf16[2,768,2048]{2,0,1:T(2,128)(2,1)}, u32[]{:S(2)}, u32[]{:S(2)}) async-start(bf16[2,768,2048]{2,0,1:T(2,128)(2,1)} %copy.262), calls=%async_computation.1 | async-start | bytes 12582912 | tf_op jit(solution)/shard_map/all_to_all | solution.py:279
  913.3 76.4 %all-to-all-start.3 = ((bf16[2,768,2048]{2,0,1:T(2,128)(2,1)}), bf16[2,768,2048]{2,0,1:T(2,128)(2,1)}, u32[]{:S(2)}, u32[]{:S(2)}) async-start(bf16[2,768,2048]{2,0,1:T(2,128)(2,1)} %copy.266), calls=%async_computation.3 | async-start | bytes 12582912 | tf_op jit(solution)/shard_map/all_to_all | solution.py:304
  918.1 1404.6 %reduce-scatter.11.cloned.1.call-start = ((), (), s32[]{:S(2)}) async-start(), calls=%async_computation.13 | async-start | bytes 17301504 | tf_op jit(solution)/shard_map/reduce_scatter | solution.py:344
  1026.7 1299.0 %reduce-scatter.21.cloned.1.call-start = ((), (), s32[]{:S(2)}) async-start(), calls=%async_computation.19 | async-start | bytes 1081344
  1093.6 1242.2 %reduce-scatter.19.cloned.1.call-start = ((), (), s32[]{:S(2)}) async-start(), calls=%async_computation.18 | async-start | bytes 1081344
  1166.4 1179.6 %all-gather.11.cloned.1.call-start = ((), (), s32[]{:S(2)}) async-start(), calls=%async_computation.12 | async-start | bytes 7077888 | tf_op jit(solution)/shard_map/all_gather | solution.py:349
  2286.2 190.7 %reduce-scatter.17.cloned.1.call-start = ((), (), s32[]{:S(2)}) async-start(), calls=%async_computation.17 | async-start | bytes 10485760 | tf_op jit(solution)/shard_map/reduce_scatter | solution.py:315
  2298.6 325.9 %reduce-scatter.15.cloned.1.call-start = ((), (), s32[]{:S(2)}) async-start(), calls=%async_computation.16 | async-start | bytes 10485760 | tf_op jit(solution)/shard_map/reduce_scatter | solution.py:312
  2310.8 461.3 %reduce-scatter.13.cloned.1.call-start = ((), (), s32[]{:S(2)}) async-start(), calls=%async_computation.15 | async-start | bytes 10485760 | tf_op jit(solution)/shard_map/reduce_scatter | solution.py:309
  2322.6 480.2 %all-gather.13.cloned.1.call-start = ((), (), s32[]{:S(2)}) async-start(), calls=%async_computation.14 | async-start | bytes 2359296 | tf_op jit(solution)/shard_map/all_gather | solution.py:352
  (45 other events, 414.4 us)
Sparse Core Ops, SparseCore 0:
  16.0 428.8 all-gather.6
  446.5 147.7 all-gather.8
  1026.8 207.0 reduce-scatter.10
  1236.0 149.5 reduce-scatter.20
  1388.2 136.5 reduce-scatter.18
  2286.3 43.4 all-gather.10
  2332.2 144.6 reduce-scatter.16
  2479.2 145.2 reduce-scatter.14
  2626.9 145.2 reduce-scatter.12
  2774.4 28.3 all-gather.12
where the time goes:
time: 2830 us; the launch traced here: 2810 us
  blocking collectives  1190 us (42%)
  waiting for transfers between devices  1140 us (40%)
  matrix products  198 us (7%)
  local copies, waits for them, and re-layouts  192 us (7%)
  other arithmetic  65.7 us (2%)
    unnamed x1, blocking collectives  1120 us
    all_gather x1, waiting for transfers between devices, body(): lax.all_gather(w_qkv, 'dp', axis=0, tiled=True)  369 us
    reduce_scatter x1, waiting for transfers between devices, body(): lax.psum_scatter(local_gate.astype(jnp.bfloat16), 'dp', scatter_dimension...  144 us
    reduce_scatter x1, waiting for transfers between devices, body(): lax.psum_scatter(local_up.astype(jnp.bfloat16), 'dp', scatter_dimension=1...  143 us
    all_gather x1, waiting for transfers between devices, body(): lax.all_gather(w_out, 'dp', axis=0, tiled=True)  129 us
    reduce_scatter x1, waiting for transfers between devices, body(): lax.psum_scatter(local_down.astype(jnp.bfloat16), 'dp', scatter_dimension...  122 us
    reshape x1, local copies, waits for them, and re-layouts, mixer_backward(): jnp.dot(normed_one.T, grad_proj, preferred_element_type=jnp.float32)  71.4 us
    all_to_all x1, waiting for transfers between devices, body(): lax.all_to_all(sent_rows, 'expert', split_axis=0, concat_axis=1, tiled=True)  65 us
  transfers between devices with their start and end apart: 14, of which 10 were waited for; matrix products, arithmetic and copies ran while one was open for 11% of the time, Pallas kernels for 0%

commit v1 on v0

v1 whole, which is shorter than its diff:
```python
import functools

import jax
import jax.numpy as jnp
from jax import lax
from jax.experimental import pallas as pl
from jax.experimental.pallas import tpu as pltpu
from jax.sharding import PartitionSpec as P

HD = 128
EPS = 1e-05
ROPE_BASE = 10000.0
MASKED = -1e30
BF = jnp.bfloat16
F32 = jnp.float32


def dot(a, b, dims):
    return lax.dot_general(a, b, (dims, ((), ())), preferred_element_type=F32)


NN = ((1,), (0,))
NT = ((1,), (1,))
TN = ((0,), (0,))


def rms_scale(values):
    return lax.rsqrt(jnp.mean(values * values, axis=-1, keepdims=True) + EPS)


def rms_backward(values, inv_rms, gain_col, grad_out):
    normed = values * inv_rms
    grad_gain = jnp.sum(grad_out * normed, axis=0)
    scaled = grad_out * gain_col
    grad_values = inv_rms * (scaled - normed * jnp.mean(scaled * normed, axis=-1, keepdims=True))
    return (grad_values, grad_gain)


def rope_tables(length):
    half = HD // 2
    freqs = jnp.exp(-jnp.log(ROPE_BASE) * (2.0 * jnp.arange(half, dtype=F32) / HD))
    angles = jnp.arange(length, dtype=F32)[:, None] * freqs[None, :]
    return (jnp.cos(angles)[:, None, :], jnp.sin(angles)[:, None, :])


def rotate(values, cos_tab, sin_tab):
    first, second = jnp.split(values, 2, axis=-1)
    return jnp.concatenate(
        [first * cos_tab - second * sin_tab, second * cos_tab + first * sin_tab], axis=-1
    )


def attend_scores(query_rot, key_rot, seg_ids):
    places = jnp.arange(seg_ids.shape[0], dtype=jnp.int32)
    allowed = (places[:, None] >= places[None, :]) & (seg_ids[:, None] == seg_ids[None, :])
    scores = jnp.einsum("qhd,khd->hqk", query_rot, key_rot, preferred_element_type=F32)
    scores = scores * query_rot.shape[-1] ** (-0.5)
    return jnp.where(allowed[None], scores, MASKED)


def attend_forward(query_rot, key_rot, value_bf, seg_ids):
    scores = attend_scores(query_rot, key_rot, seg_ids)
    row_max = jnp.max(scores, axis=-1, keepdims=True)
    log_total = row_max + jnp.log(jnp.sum(jnp.exp(scores - row_max), axis=-1, keepdims=True))
    weights_bf = jnp.exp(scores - log_total).astype(BF)
    mixed = jnp.einsum("hqk,khd->qhd", weights_bf, value_bf, preferred_element_type=F32)
    return (mixed.astype(BF), log_total)


def attend_backward(query_rot, key_rot, value_bf, seg_ids, log_total, grad_heads):
    scores = attend_scores(query_rot, key_rot, seg_ids)
    probs = jnp.exp(scores - log_total)
    grad_value = jnp.einsum(
        "hqk,qhd->khd", probs.astype(BF), grad_heads, preferred_element_type=F32
    ).astype(BF)
    grad_probs = jnp.einsum("qhd,khd->hqk", grad_heads, value_bf, preferred_element_type=F32)
    delta = jnp.sum(probs * grad_probs, axis=-1, keepdims=True)
    grad_scores = (probs * (grad_probs - delta) * query_rot.shape[-1] ** (-0.5)).astype(BF)
    grad_query = jnp.einsum("hqk,khd->qhd", grad_scores, key_rot, preferred_element_type=F32)
    grad_key = jnp.einsum("hqk,qhd->khd", grad_scores, query_rot, preferred_element_type=F32)
    return (grad_query, grad_key, grad_value)


def moe_kernel(
    fl, h_ref, g_ref, gate_ref, win_ref, wdt_ref, wd_ref, wint_ref,
    mix_ref, gh_ref, gg_ref, dwin_ref, dwd_ref, acc_in, acc_d,
):
    step = pl.program_id(0)
    h = h_ref[...]
    g = g_ref[...]
    gates = gate_ref[...]
    pre = dot(h, win_ref[...], NN)
    graw = dot(g, wdt_ref[...], NN)
    scaled_act, grad_gate, grad_up, gg = [], [], [], []
    for i in range(2):
        u = pre[:, i * fl : (i + 1) * fl]
        w = pre[:, (2 + i) * fl : (3 + i) * fl]
        gr = graw[:, i * fl : (i + 1) * fl]
        gate = gates[:, i : i + 1]
        sig = 1.0 / (1.0 + jnp.exp(-u))
        silu = u * sig
        act = silu * w
        gg.append(jnp.sum(act.astype(BF).astype(F32) * gr, axis=-1, keepdims=True))
        scaled_act.append((gate * act).astype(BF))
        gact = gate * gr
        grad_gate.append((gact * w * (sig * (1.0 + u * (1.0 - sig)))).astype(BF))
        grad_up.append((gact * silu).astype(BF))
    a = jnp.concatenate(scaled_act, axis=1)
    gin = jnp.concatenate(grad_gate + grad_up, axis=1)
    mix_ref[...] = dot(a, wd_ref[...], NN).astype(BF)
    gh_ref[...] = dot(gin, wint_ref[...], NN).astype(BF)
    gg_ref[...] = jnp.concatenate(gg, axis=1)

    @pl.when(step == 0)
    def _():
        acc_in[...] = jnp.zeros_like(acc_in)
        acc_d[...] = jnp.zeros_like(acc_d)

    acc_in[...] += dot(h, gin, TN)
    acc_d[...] += dot(a, g, TN)

    @pl.when(step == pl.num_programs(0) - 1)
    def _():
        dwin_ref[...] = acc_in[...].astype(BF)
        dwd_ref[...] = acc_d[...]


def moe(h_all, g_all, gates2, w_in, wd_t, wd, w_in_t, tile):
    count, width = h_all.shape
    hid4 = w_in.shape[1]
    hid2 = wd.shape[0]
    fl = hid2 // 2
    rows = lambda n: pl.BlockSpec((tile, n), lambda i: (i, 0))
    whole = lambda s: pl.BlockSpec(s, lambda i: (0, 0), pipeline_mode=pl.Buffered(1))
    return pl.pallas_call(
        functools.partial(moe_kernel, fl),
        grid=(count // tile,),
        in_specs=[
            rows(width), rows(width), rows(2),
            whole(w_in.shape), whole(wd_t.shape), whole(wd.shape), whole(w_in_t.shape),
        ],
        out_specs=[
            rows(width), rows(width), rows(2), whole((width, hid4)), whole((hid2, width)),
        ],
        out_shape=[
            jax.ShapeDtypeStruct((count, width), BF),
            jax.ShapeDtypeStruct((count, width), BF),
            jax.ShapeDtypeStruct((count, 2), F32),
            jax.ShapeDtypeStruct((width, hid4), BF),
            jax.ShapeDtypeStruct((hid2, width), F32),
        ],
        scratch_shapes=[pltpu.VMEM((width, hid4), F32), pltpu.VMEM((hid2, width), F32)],
        compiler_params=pltpu.CompilerParams(vmem_limit_bytes=66_000_000),
        cost_estimate=pl.CostEstimate(
            flops=2 * count * width * hid2 * 9,
            bytes_accessed=8 * count * width + 24 * hid4 * width,
            transcendentals=count * hid2,
        ),
        name="moe",
    )(h_all, g_all, gates2, w_in, wd_t, wd, w_in_t)


def body(inputs, segments, routes, w_qkv, w_out, w_router, gains, w_gate, w_up, w_down, cotangent):
    z = lax.axis_index("dp")
    e = lax.axis_index("expert")
    nz = lax.axis_size("dp")
    ne = lax.axis_size("expert")
    count, width = inputs.shape
    num_seqs, length = segments.shape
    heads = width // HD // ne
    hw = heads * HD
    expert_count = w_router.shape[1]
    per_dev = w_gate.shape[0]
    hidden = w_gate.shape[2]
    fl = hidden // nz
    both = ("dp", "expert")

    qkv_cols = lax.dynamic_slice_in_dim(w_qkv, e * hw, hw, axis=2)
    wq = lax.all_gather(qkv_cols, "dp", axis=0, tiled=True).reshape(width, 3 * hw)
    out_cols = lax.dynamic_slice_in_dim(w_out, e * hw, hw, axis=1)
    out_cols = lax.all_gather(out_cols, "dp", axis=0, tiled=True)
    wo = lax.all_to_all(
        out_cols.reshape(ne, hw, hw), "expert", split_axis=0, concat_axis=0, tiled=True
    )
    wo = wo.transpose(1, 0, 2).reshape(hw, width)
    small = lax.all_gather(
        jnp.concatenate([gains, w_router], axis=1), "dp", axis=0, tiled=True
    )
    gain_mat = small[:, :4].astype(F32)
    router = small[:, 4:]
    my_gains = lax.dynamic_slice_in_dim(gain_mat, e * hw, hw, axis=0)

    g_all = lax.all_gather(cotangent, both, axis=0, tiled=True)
    inputs_f = inputs.astype(F32)
    scale_one = rms_scale(inputs_f)
    h1 = (inputs_f * scale_one * gain_mat[:, 0]).astype(BF)
    h1_all = lax.all_gather(h1, "expert", axis=0, tiled=True)
    seg_all = lax.all_gather(segments, "expert", axis=0, tiled=True)
    plane = h1_all.shape[0]
    shape_heads = (ne * num_seqs, length, heads, HD)

    proj = dot(h1_all, wq, NN)
    q, k, v = proj[:, :hw], proj[:, hw : 2 * hw], proj[:, 2 * hw :]
    sums = jnp.stack([jnp.sum(q * q, axis=-1), jnp.sum(k * k, axis=-1)])
    scales = lax.rsqrt(lax.psum(sums, "expert") / width + EPS)
    aq, ak = scales[0][:, None], scales[1][:, None]
    cos_tab, sin_tab = rope_tables(length)
    rq = rotate((q * aq * my_gains[:, 1]).reshape(shape_heads), cos_tab, sin_tab).astype(BF)
    rk = rotate((k * ak * my_gains[:, 2]).reshape(shape_heads), cos_tab, sin_tab).astype(BF)
    vb = v.astype(BF).reshape(shape_heads)
    o, lse = jax.vmap(attend_forward)(rq, rk, vb, seg_all)
    o = o.reshape(plane, hw)
    x1_part = dot(o, wo, NN).astype(BF)
    x1 = inputs_f + lax.psum_scatter(
        x1_part, "expert", scatter_dimension=0, tiled=True
    ).astype(F32)

    a2 = rms_scale(x1)
    h2 = (x1 * a2 * gain_mat[:, 3]).astype(BF)
    probs = jax.nn.softmax(dot(h2, router, NN), axis=-1)
    picks = jnp.sum(
        (routes[:, :, None] == jnp.arange(expert_count, dtype=jnp.int32)).astype(F32), axis=1
    )
    gates = picks * probs

    h2_all = lax.all_gather(h2, both, axis=0, tiled=True)
    gates_all = lax.all_gather(gates, both, axis=0, tiled=True)
    gates2 = lax.dynamic_slice_in_dim(gates_all, e * per_dev, per_dev, axis=1)
    wg = lax.dynamic_slice_in_dim(w_gate, z * fl, fl, axis=2)
    wu = lax.dynamic_slice_in_dim(w_up, z * fl, fl, axis=2)
    wd = lax.dynamic_slice_in_dim(w_down, z * fl, fl, axis=1)
    w_in_t = jnp.concatenate(
        [wg.transpose(0, 2, 1), wu.transpose(0, 2, 1)], axis=0
    ).reshape(2 * per_dev * fl, width)
    w_in = jnp.concatenate([wg[0], wg[1], wu[0], wu[1]], axis=1)
    wd = wd.reshape(per_dev * fl, width)
    mix, gh, gg, dwin, dwd = moe(h2_all, g_all, gates2, w_in, wd.T, wd, w_in_t, 512)

    gg_full = lax.dynamic_update_slice_in_dim(
        jnp.zeros((gg.shape[0], expert_count), F32), gg, e * per_dev, axis=1
    )
    grad_gates = lax.psum_scatter(gg_full, both, scatter_dimension=0, tiled=True)

    def scatter_tokens(part):
        part = part.reshape(nz, ne, count, width).transpose(1, 0, 2, 3).reshape(-1, width)
        part = lax.psum_scatter(part, "expert", scatter_dimension=0, tiled=True)
        return lax.psum_scatter(part, "dp", scatter_dimension=0, tiled=True).astype(F32)

    grad_from_experts = scatter_tokens(gh)
    mixed = scatter_tokens(mix)
    output = (x1 + mixed).astype(BF)

    dwin = lax.all_to_all(
        dwin.reshape(nz, width // nz, 2 * per_dev * fl), "dp", split_axis=0, concat_axis=0, tiled=True
    )
    dwin = dwin.reshape(nz, width // nz, 2, per_dev, fl).transpose(2, 3, 1, 0, 4)
    dwin = dwin.reshape(2, per_dev, width // nz, hidden).astype(F32)
    grad_w_down = dwd.reshape(per_dev, fl, width)

    grad_top = cotangent.astype(F32)
    grad_probs = picks * grad_gates
    glog = (probs * (grad_probs - jnp.sum(probs * grad_probs, axis=-1, keepdims=True))).astype(BF)
    local_router = dot(h2, glog, TN)
    gh2 = grad_from_experts + dot(glog, router, NT)
    grad_ffn, gain_ffn = rms_backward(x1, a2, gain_mat[:, 3], gh2)
    gx1 = grad_top + grad_ffn
    gab = gx1.astype(BF)

    gab_all = lax.all_gather(gab, "expert", axis=0, tiled=True)
    go = dot(gab_all, wo, NT).astype(BF).reshape(shape_heads)
    grad_q, grad_k, gv = jax.vmap(attend_backward)(rq, rk, vb, seg_all, lse, go)
    gqn = rotate(grad_q, cos_tab, -sin_tab).reshape(plane, hw)
    gkn = rotate(grad_k, cos_tab, -sin_tab).reshape(plane, hw)
    nq, nk = q * aq, k * ak
    sq, sk = gqn * my_gains[:, 1], gkn * my_gains[:, 2]
    sums = jnp.stack([jnp.sum(sq * nq, axis=-1), jnp.sum(sk * nk, axis=-1)])
    means = lax.psum(sums, "expert") / width
    gq = (aq * (sq - nq * means[0][:, None])).astype(BF)
    gk = (ak * (sk - nk * means[1][:, None])).astype(BF)
    gproj = jnp.concatenate([gq, gk, gv.reshape(plane, hw)], axis=1)
    gain_q, gain_k = jnp.sum(gqn * nq, axis=0), jnp.sum(gkn * nk, axis=0)

    gh1_part = dot(gproj, wq, NT).astype(BF)
    gh1 = lax.psum_scatter(gh1_part, "expert", scatter_dimension=0, tiled=True).astype(F32)
    grad_front, gain_attn = rms_backward(inputs_f, scale_one, gain_mat[:, 0], gh1)
    grad_inputs = (gx1 + grad_front).astype(BF)

    part_qkv = dot(h1_all, gproj, TN).astype(BF)
    part_out = dot(o, gab_all, TN).astype(BF)
    part_out = lax.all_to_all(
        part_out.reshape(hw, ne, hw).transpose(1, 0, 2),
        "expert", split_axis=0, concat_axis=0, tiled=True,
    ).reshape(width, hw)
    parts = jnp.concatenate([part_qkv, part_out], axis=1)
    mine = lax.psum_scatter(parts, "dp", scatter_dimension=0, tiled=True)
    wide = lax.all_gather(mine, "expert", axis=0)
    wide = wide.reshape(ne, width // nz, 4, hw).transpose(1, 2, 0, 3)
    wide = wide.reshape(width // nz, 4, width).astype(F32)
    grad_w_qkv, grad_w_out = wide[:, :3], wide[:, 3]

    place = lambda part: lax.dynamic_update_slice_in_dim(
        jnp.zeros((width,), F32), part, e * hw, axis=0
    )
    tiny = jnp.concatenate(
        [
            local_router,
            jnp.stack([gain_attn, place(gain_q), place(gain_k), gain_ffn], axis=1),
        ],
        axis=1,
    )
    tiny = lax.psum(tiny, both)
    tiny = lax.dynamic_slice_in_dim(tiny, z * (width // nz), width // nz, axis=0)
    grad_w_router, grad_gains = tiny[:, :expert_count], tiny[:, expert_count:]
    return (
        output,
        grad_inputs,
        grad_w_qkv,
        grad_w_out,
        grad_w_router,
        grad_gains,
        dwin[0],
        dwin[1],
        grad_w_down,
    )


def solution(mesh):
    tokens = P(("dp", "expert"), None)
    rows = P("dp", None)
    rows3 = P("dp", None, None)
    owned = P("expert", None, None)
    return jax.shard_map(
        body,
        mesh=mesh,
        in_specs=(tokens, tokens, tokens, rows3, rows, rows, rows, owned, owned, owned, tokens),
        out_specs=(tokens, tokens, rows3, rows, rows, rows)
        + (P("expert", "dp", None),) * 3,
        check_vma=False,
    )
```

time: 2830 us -> 1470 us (0.52)
  blocking collectives: 1190 us -> 114 us
  waiting for transfers between devices: 1140 us -> 890 us
  matrix products: 198 us -> 45.6 us
  Pallas kernels: 0 us -> 96.4 us
    unnamed x1 -> x0, blocking collectives: 1120 us -> none
    all_gather x4 -> x7, waiting for transfers between devices: 524 us -> 221 us  [the longest x1 108 us: body(): h2_all = lax.all_gather(h2, both, axis=0, tiled=True)]
    dot_general x22 -> x14, matrix products: 193 us -> 41.8 us  [the longest x9 33.2 us: dot(): return lax.dot_general(a, b, (dims, ((), ())), preferred_element_type=F32)]
    pallas_call x0 -> x1, Pallas kernels: none -> 96.4 us  [moe(): pl.pallas_call(functools.partial(moe_kernel, fl), grid=(count // tile,),...]
    reduce_scatter x4 -> x8, waiting for transfers between devices: 409 us -> 493 us  [the longest x1 132 us: body(): lax.psum_scatter(gg_full, both, scatter_dimension=0, tiled=True)]
    all_to_all x4 -> x3, waiting for transfers between devices: 203 us -> 147 us  [the longest x1 128 us: body(): lax.all_to_all(dwin.reshape(nz, width // nz, 2 * per_dev * fl), 'dp', spl...]
    reshape x2 -> x7, local copies, waits for them, and re-layouts: 73.5 us -> 32.4 us  [the longest x2 28.3 us: scatter_tokens(): part.reshape(nz, ne, count, width).transpose(1, 0, 2, 3).reshape(-1, width)]
    convert_element_type x5 -> x6, local copies, waits for them, and re-layouts: 32.7 us -> 62.8 us  [the longest x2 38.2 us: body(): wide = wide.reshape(width // nz, 4, width).astype(F32)]
  transfers between devices with their start and end apart: 14 -> 19, of which waited for: 10 -> 15; matrix products, arithmetic and copies ran while one was open for 11% -> 12% of each run, Pallas kernels for 0% -> 0%
where the time goes in v1:
time: 1470 us; the launch traced here: 1460 us
  waiting for transfers between devices  890 us (61%)
  local copies, waits for them, and re-layouts  218 us (15%)
  blocking collectives  114 us (8%)
  Pallas kernels  96.4 us (7%)
  other arithmetic  53.2 us (4%)
  matrix products  45.6 us (3%)
  starting transfers between devices  22 us (1%)
  between operations  16.9 us (1%)
    reduce_scatter x1, waiting for transfers between devices, body(): lax.psum_scatter(gg_full, both, scatter_dimension=0, tiled=True)  132 us
    reduce_scatter x2, waiting for transfers between devices, scatter_tokens(): part = lax.psum_scatter(part, 'expert', scatter_dimension=0, tiled=True)  131 us
    all_to_all x1, waiting for transfers between devices, body(): lax.all_to_all(dwin.reshape(nz, width // nz, 2 * per_dev * fl), 'dp', spl...  128 us
    all_gather x1, waiting for transfers between devices, body(): h2_all = lax.all_gather(h2, both, axis=0, tiled=True)  108 us
    pallas_call x1, Pallas kernels, moe(): pl.pallas_call(functools.partial(moe_kernel, fl), grid=(count // tile,),...  96.4 us
    reduce_scatter x1, waiting for transfers between devices, body(): mine = lax.psum_scatter(parts, 'dp', scatter_dimension=0, tiled=True)  77.4 us
    reduce_scatter x1, waiting for transfers between devices, body(): lax.psum_scatter(x1_part, 'expert', scatter_dimension=0, tiled=True)  56.7 us
    reduce_scatter x1, waiting for transfers between devices, body(): lax.psum_scatter(gh1_part, 'expert', scatter_dimension=0, tiled=True)  54.5 us
  transfers between devices with their start and end apart: 19, of which 15 were waited for; matrix products, arithmetic and copies ran while one was open for 12% of the time, Pallas kernels for 0%

profile of v1, /device:TPU:0, one launch (start us, length us, event | category | flops | bytes accessed | tf_op | source)
XLA Modules:
  0.0 1455.9 jit_solution(11685475000130730819)
XLA Ops:
  12.4 15.4 %all_gather.33 = bf16[2048,20]{0,1:T(8,128)(2,1)S(1)} all-gather(bf16[512,20]{0,1:T(8,128)(2,1)S(1)} %pad_maximum_fusion.14), channel_id=1, replica_groups=mesh['dp'=4,'expert'=8] {'dp'}, dimensions={0}, use_global_device_ids=true | all-gather | bytes 102400 | tf_op jit(solution)/shard_map/all_gather | solution.py:186
  46.1 18.3 %all-gather.1 = s32[8,1,128]{2,1,0:T(1,128)S(1)} all-gather(s32[1,1,128]{2,1,0:T(1,128)S(1)} %bitcast.219), channel_id=1, replica_groups=mesh['dp'=4,'expert'=8] {'expert'}, dimensions={0}, use_global_device_ids=true | all-gather | bytes 4608 | tf_op jit(solution)/shard_map/all_gather | solution.py:198
  66.9 40.2 %all-gather.12.cloned.1.call-done = bf16[2048,3,256]{0,2,1:T(8,128)(2,1)} async-done(((bf16[512,3,256]{0,2,1:T(8,128)(2,1)}), bf16[2048,3,256]{0,2,1:T(8,128)(2,1)}) %all-gather.12.cloned.1.call-update) | async-done | bytes 3145744 | tf_op jit(solution)/shard_map/all_gather | solution.py:179
  107.1 37.7 %all-gather.10.cloned.1.call-done = bf16[1024,2048]{1,0:T(8,128)(2,1)} async-done(((bf16[128,2048]{1,0:T(8,128)(2,1)}), bf16[1024,2048]{1,0:T(8,128)(2,1)}) %all-gather.10.cloned.1.call-update) | async-done | bytes 4194320 | tf_op jit(solution)/shard_map/all_gather | solution.py:197
  188.5 56.7 %reduce-scatter.9.cloned.1.call-done = bf16[128,2048]{1,0:T(8,128)(2,1)} async-done(((bf16[1024,2048]{1,0:T(8,128)(2,1)}), bf16[128,2048]{1,0:T(8,128)(2,1)}) %reduce-scatter.9.cloned.1.call-update) | async-done | bytes 524304 | tf_op jit(solution)/shard_map/reduce_scatter | solution.py:214
  270.5 54.0 %all_gather.40 = f32[4096,16]{1,0:T(8,128)S(1)} all-gather(f32[128,16]{1,0:T(8,128)S(1)} %fusion.58), channel_id=1, replica_groups=mesh['dp'=4,'expert'=8] {'dp','expert'}, dimensions={0}, use_global_device_ids=true | all-gather | bytes 270336 | tf_op jit(solution)/shard_map/all_gather | solution.py:227
  326.5 108.2 %all-gather.16.cloned.1.call-done.h_ref = bf16[4096,2048]{1,0:T(8,128)(2,1)} async-done(((bf16[128,2048]{1,0:T(8,128)(2,1)}), bf16[4096,2048]{1,0:T(8,128)(2,1)}) %all-gather.16.cloned.1.call-update) | async-done | bytes 16777232 | tf_op jit(solution)/shard_map/all_gather | solution.py:226
  434.7 96.4 %moe.1 = (bf16[4096,2048]{1,0:T(8,128)(2,1)}, bf16[4096,2048]{1,0:T(8,128)(2,1)}, f32[4096,2]{1,0:T(8,128)}, bf16[2048,1024]{1,0:T(8,128)(2,1)}, f32[512,2048]{1,0:T(8,128)}) custom-call(bf16[4096,2048]{1,0:T(8,128)(2,1)} %all-gather.16.cloned.1.call-done.h_ref, bf16[4096,2048]{1,0:T(8,128)(2,1)} %all-gather.18.cloned.1.call-done.g_ref, ...), custom_call_target="tpu_custom_call" | custom-call | flops 77309411328 | bytes 117440512 | tf_op jit(solution)/shard_map/moe/pallas_call | solution.py:135
  531.1 14.1 copy.189
  545.4 15.5 %dynamic_update_slice.11 = f32[4096,16]{1,0:T(8,128)S(1)} dynamic-update-slice(f32[4096,16]{1,0:T(8,128)S(1)} %broadcast_in_dim.20, f32[4096,2]{1,0:T(8,128)} %get-tuple-element.16, s32[]{:T(128)} %constant.19.clone.1, s32[]{:T(128)S(6)} %select_n.26) | dynamic-update-slice | bytes 65540 | tf_op jit(solution)/shard_map/dynamic_update_slice | solution.py:239
  562.3 97.5 %reduce-scatter.15.cloned.1.call-done = bf16[512,2048]{1,0:T(8,128)(2,1)} async-done(((bf16[4096,2048]{1,0:T(8,128)(2,1)}), bf16[512,2048]{1,0:T(8,128)(2,1)}) %reduce-scatter.15.cloned.1.call-update) | async-done | bytes 2097168 | tf_op jit(solution)/shard_map/reduce_scatter | solution.py:246
  668.5 132.3 %reduce-scatter.19.cloned.1.call-done = f32[128,16]{1,0:T(8,128)} async-done(((f32[4096,16]{1,0:T(8,128)}), f32[128,16]{1,0:T(8,128)}) %reduce-scatter.19.cloned.1.call-update) | async-done | bytes 8208 | tf_op jit(solution)/shard_map/reduce_scatter | solution.py:242
  801.9 40.8 %reduce-scatter.17.cloned.1.call-done = bf16[128,2048]{1,0:T(8,128)(2,1)} async-done(((bf16[512,2048]{1,0:T(8,128)(2,1)}), bf16[128,2048]{1,0:T(8,128)(2,1)}) %reduce-scatter.17.cloned.1.call-update) | async-done | bytes 524304 | tf_op jit(solution)/shard_map/reduce_scatter | solution.py:247
  848.1 14.2 copy.188
  862.4 21.6 %all-gather.20.cloned.1.call-done = bf16[1024,2048]{1,0:T(8,128)(2,1)} async-done(((bf16[128,2048]{1,0:T(8,128)(2,1)}), bf16[1024,2048]{1,0:T(8,128)(2,1)}) %all-gather.20.cloned.1.call-update) | async-done | bytes 4194320 | tf_op jit(solution)/shard_map/all_gather | solution.py:269
  957.8 19.1 %all-to-all-done.1 = bf16[8,256,256]{1,2,0:T(8,128)(2,1)S(1)} async-done(((bf16[8,256,256]{1,2,0:T(8,128)(2,1)}), bf16[8,256,256]{1,2,0:T(8,128)(2,1)S(1)}, u32[]{:S(2)}, u32[]{:S(2)}) %all-to-all-start.1) | async-done | bytes 1048608 | tf_op jit(solution)/shard_map/all_to_all | solution.py:290
  981.7 33.6 %reduce-scatter.11.cloned.1.call-done = bf16[512,2048]{1,0:T(8,128)(2,1)} async-done(((bf16[4096,2048]{1,0:T(8,128)(2,1)}), bf16[512,2048]{1,0:T(8,128)(2,1)}) %reduce-scatter.11.cloned.1.call-update) | async-done | bytes 2097168 | tf_op jit(solution)/shard_map/reduce_scatter | solution.py:246
  1015.7 54.5 %reduce-scatter.21.cloned.1.call-done = bf16[128,2048]{1,0:T(8,128)(2,1)} async-done(((bf16[1024,2048]{1,0:T(8,128)(2,1)}), bf16[128,2048]{1,0:T(8,128)(2,1)}) %reduce-scatter.21.cloned.1.call-update) | async-done | bytes 524304 | tf_op jit(solution)/shard_map/reduce_scatter | solution.py:284
  1073.1 77.4 %reduce-scatter.23.cloned.1.call-done = bf16[512,1024]{0,1:T(8,128)(2,1)} async-done(((bf16[2048,1024]{0,1:T(8,128)(2,1)}), bf16[512,1024]{0,1:T(8,128)(2,1)}) %reduce-scatter.23.cloned.1.call-update) | async-done | bytes 1048592 | tf_op jit(solution)/shard_map/reduce_scatter | solution.py:295
  1155.4 128.3 %all-to-all-done.2 = bf16[4,512,1024]{2,1,0:T(8,128)(2,1)} async-done(((bf16[4,512,1024]{2,1,0:T(8,128)(2,1)}), bf16[4,512,1024]{2,1,0:T(8,128)(2,1)}, u32[]{:S(2)}, u32[]{:S(2)}) %all-to-all-start.2) | async-done | bytes 4194336 | tf_op jit(solution)/shard_map/all_to_all | solution.py:253
  1330.7 27.6 %all-reduce.2.cloned.1.call-done = f32[2048,20]{0,1:T(8,128)} async-done(((f32[2048,20]{0,1:T(8,128)}), f32[2048,20]{0,1:T(8,128)}) %all-reduce.2.cloned.1.call-update) | async-done | bytes 163856 | tf_op jit(solution)/shard_map/psum | solution.py:311
  1372.4 21.2 %copy.230 = f32[128,8,8,512]{3,2,1,0:T(8,128)} copy(f32[128,8,8,512]{3,1,2,0:T(8,128)} %bitcast.156) | data formatting | bytes 33554432
  1393.6 20.2 %copy.206 = f32[512,4,8,256]{3,2,0,1:T(8,128)} copy(f32[512,4,8,256]{0,2,3,1:T(8,128)} %bitcast.157) | data formatting | bytes 33554432 | tf_op jit(solution)/shard_map/convert_element_type | solution.py:298
  1413.8 18.0 %reshape.249 = f32[512,4,2048]{2,0,1:T(8,128)} reshape(f32[512,4,8,256]{3,2,0,1:T(8,128)} %copy.206) | data formatting | bytes 33554432 | tf_op jit(solution)/shard_map/convert_element_type | solution.py:298
  (239 shorter events, 276.1 us)
Async XLA Ops:
  8.0 34.2 %all-gather.14.cloned.1.call-start = ((), (), s32[]{:S(2)}) async-start(), calls=%async_computation.13 | async-start | bytes 1310720 | tf_op jit(solution)/shard_map/all_gather | solution.py:181
  9.9 97.3 %all-gather.12.cloned.1.call-start = ((), (), s32[]{:S(2)}) async-start(), calls=%async_computation.12 | async-start | bytes 3932160 | tf_op jit(solution)/shard_map/all_gather | solution.py:179
  12.3 132.6 %all-gather.10.cloned.1.call-start = ((), (), s32[]{:S(2)}) async-start(), calls=%async_computation.11 | async-start | bytes 4718592 | tf_op jit(solution)/shard_map/all_gather | solution.py:197
  42.3 23.3 %all-to-all-start = ((bf16[8,256,256]{2,1,0:T(8,128)(2,1)}), bf16[8,256,256]{2,1,0:T(8,128)(2,1)S(1)}, u32[]{:S(2)}, u32[]{:S(2)}) async-start(bf16[8,256,256]{2,1,0:T(8,128)(2,1)} %bitcast.180), calls=%async_computation | async-start | bytes 2097152 | tf_op jit(solution)/shard_map/all_to_all | solution.py:182
  46.0 199.2 %reduce-scatter.9.cloned.1.call-start = ((), (), s32[]{:S(2)}) async-start(), calls=%async_computation.14 | async-start | bytes 4718592 | tf_op jit(solution)/shard_map/reduce_scatter | solution.py:214
  64.5 101.8 %copy-start.36 = (f32[256,1]{0,1:T(1,128)}, f32[256,1]{0,1:T(1,128)S(1)}, u32[]{:S(2)}) copy-start(f32[256,1]{0,1:T(1,128)S(1)} %get-tuple-element.63) | copy-start | bytes 3076
  64.5 101.8 %copy-start.38 = (f32[256,1]{0,1:T(1,128)}, f32[256,1]{0,1:T(1,128)S(1)}, u32[]{:S(2)}) copy-start(f32[256,1]{0,1:T(1,128)S(1)} %get-tuple-element.64) | copy-start | bytes 3076
  187.8 61.1 %copy-start.42 = (s32[128,8]{0,1:T(8,128)S(1)}, s32[128,8]{0,1:T(8,128)}, u32[]{:S(2)}) copy-start(s32[128,8]{0,1:T(8,128)} %param.13) | copy-start | bytes 12292
  187.9 138.6 %all-gather.18.cloned.1.call-start = ((), (), s32[]{:S(2)}) async-start(), calls=%async_computation.16 | async-start | bytes 17301504 | tf_op jit(solution)/shard_map/all_gather | solution.py:193
  188.4 246.2 %all-gather.16.cloned.1.call-start = ((), (), s32[]{:S(2)}) async-start(), calls=%async_computation.15 | async-start | bytes 17301504 | tf_op jit(solution)/shard_map/all_gather | solution.py:226
  248.6 411.1 %reduce-scatter.15.cloned.1.call-start = ((), (), s32[]{:S(2)}) async-start(), calls=%async_computation.19 | async-start | bytes 18874368 | tf_op jit(solution)/shard_map/reduce_scatter | solution.py:246
  545.2 255.7 %reduce-scatter.19.cloned.1.call-start = ((), (), s32[]{:S(2)}) async-start(), calls=%async_computation.21 | async-start | bytes 2162688 | tf_op jit(solution)/shard_map/reduce_scatter | solution.py:242
  562.2 280.5 %reduce-scatter.17.cloned.1.call-start = ((), (), s32[]{:S(2)}) async-start(), calls=%async_computation.20 | async-start | bytes 2621440 | tf_op jit(solution)/shard_map/reduce_scatter | solution.py:247
  659.8 224.2 %all-gather.20.cloned.1.call-start = ((), (), s32[]{:S(2)}) async-start(), calls=%async_computation.22 | async-start | bytes 4718592 | tf_op jit(solution)/shard_map/all_gather | solution.py:269
  848.0 167.2 %reduce-scatter.11.cloned.1.call-start = ((), (), s32[]{:S(2)}) async-start(), calls=%async_computation.17 | async-start | bytes 18874368 | tf_op jit(solution)/shard_map/reduce_scatter | solution.py:246
  862.3 207.9 %reduce-scatter.21.cloned.1.call-start = ((), (), s32[]{:S(2)}) async-start(), calls=%async_computation.23 | async-start | bytes 4718592 | tf_op jit(solution)/shard_map/reduce_scatter | solution.py:284
  946.2 30.7 %all-to-all-start.1 = ((bf16[8,256,256]{1,2,0:T(8,128)(2,1)}), bf16[8,256,256]{1,2,0:T(8,128)(2,1)S(1)}, u32[]{:S(2)}, u32[]{:S(2)}) async-start(bf16[8,256,256]{1,2,0:T(8,128)(2,1)} %bitcast.38), calls=%async_computation.8 | async-start | bytes 2097152 | tf_op jit(solution)/shard_map/all_to_all | solution.py:290
  950.0 200.5 %reduce-scatter.23.cloned.1.call-start = ((), (), s32[]{:S(2)}) async-start(), calls=%async_computation.24 | async-start | bytes 5242880 | tf_op jit(solution)/shard_map/reduce_scatter | solution.py:295
  981.6 88.6 %copy-start.30 = (f32[2048,1]{0,1:T(1,128)S(1)}, f32[2048,1]{0,1:T(1,128)}, u32[]{:S(2)}) copy-start(f32[2048,1]{0,1:T(1,128)} %copy-done.29) | copy-start | bytes 24580
  981.6 88.6 %copy-start.41 = (f32[128]{0:T(128)S(1)}, f32[128]{0:T(128)}, u32[]{:S(2)}) copy-start(f32[128]{0:T(128)} %copy-done.40) | copy-start | bytes 1540
  981.6 346.1 %reduce-scatter.13.cloned.1.call-start = ((), (), s32[]{:S(2)}) async-start(), calls=%async_computation.18 | async-start | bytes 2621440 | tf_op jit(solution)/shard_map/reduce_scatter | solution.py:247
  1015.3 343.0 %all-reduce.2.cloned.1.call-start = ((), (), s32[]{:S(2)}) async-start(), calls=%async_computation.25 | async-start | bytes 393216 | tf_op jit(solution)/shard_map/psum | solution.py:311
  1073.1 288.0 %all-gather.22.cloned.1.call-start = ((), (), s32[]{:S(2)}) async-start(), calls=%async_computation.26 | async-start | bytes 9437184 | tf_op jit(solution)/shard_map/all_gather | solution.py:296
  1150.5 133.2 %all-to-all-start.2 = ((bf16[4,512,1024]{2,1,0:T(8,128)(2,1)}), bf16[4,512,1024]{2,1,0:T(8,128)(2,1)}, u32[]{:S(2)}, u32[]{:S(2)}) async-start(bf16[4,512,1024]{2,1,0:T(8,128)(2,1)} %bitcast.167), calls=%async_computation.10 | async-start | bytes 8388608 | tf_op jit(solution)/shard_map/all_to_all | solution.py:253
  (41 other events, 363.5 us)
Sparse Core Ops, SparseCore 0:
  11.0 31.2 all-gather.13
  44.4 62.6 all-gather.11
  109.6 35.2 all-gather.9
  188.0 57.2 reduce-scatter.8
  545.3 114.3 reduce-scatter.14
  662.4 138.4 reduce-scatter.18
  803.2 39.4 reduce-scatter.16
  848.2 35.7 all-gather.19
  887.6 127.6 reduce-scatter.10
  1019.1 51.1 reduce-scatter.20
  1073.1 77.3 reduce-scatter.22
  1152.7 81.8 reduce-scatter.12
  1236.5 89.9 all-gather.21
Sparse Core Ops, SparseCore 1:
  191.2 126.1 all-gather.17
  320.7 113.9 all-gather.15
  1073.1 285.1 all-reduce.1

commit v2 on v1

--- a/solution.py
+++ b/solution.py
@@ -81,35 +81,610 @@
     return (grad_query, grad_key, grad_value)
 
 
+MESH = pl.DeviceIdType.MESH
+ANY = pl.BlockSpec(memory_space=pl.ANY)
+VMEM = pl.BlockSpec(memory_space=pltpu.VMEM)
+DMA = pltpu.SemaphoreType.DMA
+
+
+def flip(index, bit):
+    return index + bit * (1 - 2 * ((index // bit) % 2))
+
+
+def flips(index, bits):
+    out = [index]
+    for bit in bits:
+        out = out + [flip(i, bit) for i in out]
+    return out
+
+
+def bit_orders(ne):
+    bits = [1 << b for b in range(ne.bit_length() - 1)]
+    return [bits[:1] + bits[1:], bits[:1] + bits[1:][::-1]]
+
+
+def nearest(z, r, nz):
+    low = jnp.minimum(z, nz - 1 - z)
+    near = z - (r + 1) // 2 if r % 2 else z + r // 2
+    far = jnp.where(2 * z < nz, z + (r - low), z - (r - low))
+    return jnp.where(r <= 2 * low, near, far)
+
+
+def remote(src, dst, send, recv, peer):
+    return pltpu.make_async_remote_copy(
+        src_ref=src, dst_ref=dst, send_sem=send, recv_sem=recv, device_id=peer, device_id_type=MESH
+    )
+
+
+def for_others(nz, ne, z, e, act):
+    def step(i, carry):
+        flat = lax.rem(z * ne + e + i, nz * ne)
+        act(flat // ne, lax.rem(flat, ne), flat)
+        return carry
+
+    lax.fori_loop(1, nz * ne, step, 0)
+
+
+def meet_all(nz, ne, z, e):
+    sem = pltpu.get_barrier_semaphore()
+
+    def greet(zz, ee, flat):
+        pl.semaphore_signal(sem, inc=1, device_id=(zz, ee), device_id_type=MESH)
+
+    for_others(nz, ne, z, e, greet)
+    pl.semaphore_wait(sem, nz * ne - 1)
+
+
+def meet_column_and_plane(nz, ne, z, e, spread):
+    sem = pltpu.get_barrier_semaphore()
+    peers = [(z, flip(e, 1 << b)) for b in range(ne.bit_length() - 1)]
+    if spread:
+        peers += [(lax.rem(z + r, nz), e) for r in range(1, nz)]
+    for peer in peers:
+        pl.semaphore_signal(sem, inc=1, device_id=peer, device_id_type=MESH)
+    pl.semaphore_wait(sem, len(peers))
+
+
+class PlaneGather:
+    def __init__(self, nz, ne, z, e, spread, x_ref, out_ref, zsend, zrecv, send, recv, local):
+        self.nz, self.ne, self.z, self.e, self.spread = nz, ne, z, e, spread
+        self.x, self.out = x_ref, out_ref
+        self.zsend, self.zrecv, self.send, self.recv = zsend, zrecv, send, recv
+        self.rounds = nz if spread else 1
+        self.half = x_ref.shape[0] // 2
+        self.orders = [o[1:] + o[:1] for o in bit_orders(ne)]
+        self.planes = [z if spread else 0] + [nearest(z, r, nz) for r in range(1, self.rounds)]
+        self.pending, self.arrivals = [], {}
+        own = self.slot(0, e)
+        keep = pltpu.make_async_copy(x_ref, out_ref.at[own], local)
+        keep.start()
+        self.pending.append(keep.wait)
+
+    @staticmethod
+    def scratch(nz, ne, spread):
+        rounds = nz if spread else 1
+        return [DMA((nz,)), DMA((nz,)), DMA((rounds, 2, ne - 1)), DMA((rounds, 2, ne - 1)), DMA]
+
+    def slot(self, r, ee):
+        return self.planes[r] * self.ne + ee
+
+    def spread_own(self):
+        for r in range(1, self.rounds):
+            to = self.planes[r]
+            copy = remote(
+                self.x, self.out.at[self.slot(0, self.e)],
+                self.zsend.at[r], self.zrecv.at[self.z], (to, self.e),
+            )
+            copy.start()
+            self.pending.append(copy.wait_send)
+
+    def forward(self, r, s, stage, subset):
+        order = self.orders[s]
+        rows = pl.ds(s * self.half, self.half)
+        peer_e = flip(self.e, order[stage])
+        n = (1 << stage) - 1 + subset
+        block = self.slot(r, flips(self.e, order[:stage])[subset])
+        dst = self.out.at[block, rows]
+        src = self.x.at[rows] if r == 0 and subset == 0 else dst
+        sems = self.send.at[r, s, n], self.recv.at[r, s, n]
+        copy = remote(src, dst, *sems, (self.z, peer_e))
+        copy.start()
+        self.pending.append(copy.wait_send)
+        got = self.out.at[self.slot(r, flips(peer_e, order[:stage])[subset]), rows]
+        self.arrivals[(r, s, stage, subset)] = remote(got, got, *sems, (self.z, peer_e)).wait_recv
+
+    def start_round(self, r):
+        if r > 0:
+            here = self.out.at[self.slot(r, self.e)]
+            remote(
+                here, here, self.zsend.at[r], self.zrecv.at[self.planes[r]], (self.planes[r], self.e)
+            ).wait_recv()
+        for stage in range(len(self.orders[0])):
+            for s in range(2):
+                self.forward(r, s, stage, 0)
+
+    def finish_round(self, r, last=False):
+        stages = len(self.orders[0])
+        for stage in range(stages):
+            for subset in range(1 << stage):
+                for s in range(2):
+                    self.arrivals.pop((r, s, stage, subset))()
+                    for later in range(stage + 1, stages):
+                        self.forward(r, s, later, subset + (1 << stage))
+
+    def finish(self):
+        for wait in self.pending:
+            wait()
+
+
+def gather_kernel(nz, ne, spread, small, *refs):
+    z, e = lax.axis_index("dp"), lax.axis_index("expert")
+    if small:
+        x_ref, small_ref, out_ref, small_out, *sems, small_send, small_recv = refs
+        meet_all(nz, ne, z, e)
+    else:
+        x_ref, out_ref, *sems = refs
+        meet_column_and_plane(nz, ne, z, e, spread)
+    net = PlaneGather(nz, ne, z, e, spread, x_ref, out_ref, *sems)
+    net.spread_own()
+    net.start_round(0)
+    if small:
+        me = z * ne + e
+        small_out[me] = small_ref[...]
+
+        def give(zz, ee, flat):
+            remote(small_ref, small_out.at[me], small_send, small_recv, (zz, ee)).start()
+
+        for_others(nz, ne, z, e, give)
+    for r in range(1, net.rounds):
+        net.start_round(r)
+        net.finish_round(r - 1)
+    net.finish_round(net.rounds - 1)
+    net.finish()
+    if small:
+        most = small_out.at[pl.ds(0, nz * ne - 1)]
+        everyone = remote(most, most, small_send, small_recv, (z, flip(e, 1)))
+        everyone.wait_send()
+        everyone.wait_recv()
+
+
+def gather_tokens(x, nz, ne, spread, cid, small=None):
+    rounds = nz if spread else 1
+    out = [jax.ShapeDtypeStruct((rounds * ne, *x.shape), x.dtype)]
+    scratch = PlaneGather.scratch(nz, ne, spread)
+    args = [x]
+    if small is not None:
+        out.append(jax.ShapeDtypeStruct((nz * ne, *small.shape), small.dtype))
+        scratch += [DMA, DMA]
+        args.append(small)
+    return pl.pallas_call(
+        functools.partial(gather_kernel, nz, ne, spread, small is not None),
+        out_shape=out,
+        in_specs=[VMEM] * len(args),
+        out_specs=[ANY, VMEM][: len(args)],
+        scratch_shapes=scratch,
+        compiler_params=pltpu.CompilerParams(collective_id=cid, has_side_effects=True),
+        name="gather_tokens",
+    )(*args)
+
+
+def add_rows(dst, src, tile=16):
+    def step(i, carry):
+        rows = pl.ds(pl.multiple_of(i * tile, tile), tile)
+        dst[rows, :] = (dst[rows, :].astype(F32) + src[rows, :].astype(F32)).astype(dst.dtype)
+        return carry
+
+    lax.fori_loop(0, dst.shape[0] // tile, step, 0)
+
+
+def scatter_kernel(nz, ne, spread, small, *refs):
+    z, e = lax.axis_index("dp"), lax.axis_index("expert")
+    if small:
+        x_ref, small_ref, out_ref, small_out, *rest, small_send, small_recv = refs
+        meet_all(nz, ne, z, e)
+        me = z * ne + e
+        small_out[me] = small_ref[me]
+
+        def give(zz, ee, flat):
+            remote(small_ref.at[flat], small_out.at[me], small_send, small_recv, (zz, ee)).start()
+
+        for_others(nz, ne, z, e, give)
+    else:
+        x_ref, out_ref, *rest = refs
+        meet_column_and_plane(nz, ne, z, e, spread)
+    acc, got, zgot, loads, send, recv, zsend, zrecv = rest
+    rounds = nz if spread else 1
+    stages = ne.bit_length() - 1
+    half = out_ref.shape[0] // 2
+    orders = bit_orders(ne)
+    pending, arrivals, zwait = [], {}, {}
+    ranks = list(range(1, rounds)) + [0]
+    first = [0] * (stages + 1)
+    for j in range(stages):
+        first[j + 1] = first[j] + (ne >> (j + 1))
+
+    def plane_of(r):
+        return lax.rem(z + r, nz) * ne if spread else 0
+
+    def push(r, s, j):
+        order = orders[s]
+        peer = (z, flip(e, order[j]))
+        rest = ne >> (j + 1)
+        for i in range(rest):
+            n = first[j] + i
+            if j == 0:
+                block = flips(peer[1], order[:0:-1])[i]
+                src = x_ref.at[plane_of(r) + block, pl.ds(s * half, half)]
+            else:
+                src = acc.at[r, s, rest + i]
+            copy = remote(src, got.at[r, s, n], send.at[r, s, n], recv.at[r, s, n], peer)
+            copy.start()
+            pending.append(copy.wait_send)
+            arrivals.setdefault((r, s, j), []).append((copy.wait_recv, i, n))
+
+    for r in ranks:
+        for s in range(2):
+            push(r, s, 0)
+            for i, block in enumerate(flips(e, orders[s][:0:-1])):
+                copy = pltpu.make_async_copy(
+                    x_ref.at[plane_of(r) + block, pl.ds(s * half, half)],
+                    acc.at[r, s, i],
+                    loads.at[r, s, i],
+                )
+                copy.start()
+                arrivals.setdefault((r, s, -1), []).append(copy.wait)
+    for t in range(rounds + stages):
+        for place, r in enumerate(ranks):
+            j = t - place
+            if not 0 <= j < stages:
+                continue
+            for s in range(2):
+                if j == 0:
+                    for wait in arrivals.pop((r, s, -1)):
+                        wait()
+                for wait, i, n in arrivals.pop((r, s, j)):
+                    wait()
+                    add_rows(acc.at[r, s, i], got.at[r, s, n])
+                if j + 1 < stages:
+                    push(r, s, j + 1)
+                elif r > 0:
+                    copy = remote(
+                        acc.at[r, s, 0], zgot.at[r, s], zsend.at[r, s], zrecv.at[r, s],
+                        (lax.rem(z + r, nz), e),
+                    )
+                    copy.start()
+                    pending.append(copy.wait_send)
+                    zwait[(r, s)] = copy.wait_recv
+    for s in range(2):
+        for r in range(1, rounds):
+            zwait[(r, s)]()
+
+        def step(i, carry):
+            rows = pl.ds(pl.multiple_of(i * 16, 16), 16)
+            total = acc[0, s, 0, rows, :].astype(F32)
+            for r in range(1, rounds):
+                total = total + zgot[r, s, rows, :].astype(F32)
+            out_ref[pl.ds(pl.multiple_of(s * half + i * 16, 16), 16), :] = total.astype(out_ref.dtype)
+            return carry
+
+        lax.fori_loop(0, half // 16, step, 0)
+    for wait in pending:
+        wait()
+    if small:
+        most = small_out.at[pl.ds(0, nz * ne - 1)]
+        everyone = remote(most, most, small_send, small_recv, (z, flip(e, 1)))
+        everyone.wait_send()
+        everyone.wait_recv()
+
+
+def scatter_tokens(parts, nz, ne, spread, cid, small=None):
+    rounds = nz if spread else 1
+    _, count, width = parts.shape
+    half = count // 2
+    held = (2 * rounds * (ne // 2 + ne - 1) + 2 * nz) * half * width * 2
+    if held > 56_000_000:
+        left = scatter_tokens(parts[..., : width // 2], nz, ne, spread, cid, small)
+        right = scatter_tokens(parts[..., width // 2 :], nz, ne, spread, cid + 16)
+        return [jnp.concatenate([left[0], right[0]], axis=1), *left[1:]]
+    out = [jax.ShapeDtypeStruct((count, width), F32)]
+    args = [parts]
+    scratch = [
+        pltpu.VMEM((rounds, 2, ne // 2, half, width), BF),
+        pltpu.VMEM((rounds, 2, ne - 1, half, width), BF),
+        pltpu.VMEM((nz, 2, half, width), BF),
+        DMA((rounds, 2, ne // 2)),
+        DMA((rounds, 2, ne - 1)),
+        DMA((rounds, 2, ne - 1)),
+        DMA((nz, 2)),
+        DMA((nz, 2)),
+    ]
+    if small is not None:
+        out.append(jax.ShapeDtypeStruct(small.shape, small.dtype))
+        args.append(small)
+        scratch += [DMA, DMA]
+    return pl.pallas_call(
+        functools.partial(scatter_kernel, nz, ne, spread, small is not None),
+        out_shape=out,
+        in_specs=[ANY, VMEM][: len(args)],
+        out_specs=[VMEM, VMEM][: len(args)],
+        scratch_shapes=scratch,
+        compiler_params=pltpu.CompilerParams(
+            collective_id=cid, has_side_effects=True, vmem_limit_bytes=64_000_000
+        ),
+        name="scatter_tokens",
+    )(*args)
+
+
+def start_kernel(
+    nz, ne, x_ref, wqkv_ref, wout_ref, small_ref, seg_ref,
+    out_ref, wq_ref, wo_ref, small_out, seg_out,
+    wbuf, pbuf, zsend, zrecv, send, recv, local,
+    up_send, up_recv, dn_send, dn_recv, wload, wkeep, pload, psend, precv, pkeep,
+    small_send, small_recv, seg_send, seg_recv,
+):
+    z, e = lax.axis_index("dp"), lax.axis_index("expert")
+    kinds, depth, hw = wbuf.shape
+    per = ne // nz
+    loads = [
+        pltpu.make_async_copy(wqkv_ref.at[j, :, pl.ds(e * hw, hw)], wbuf.at[j], wload.at[j])
+        for j in range(kinds)
+    ]
+    for copy in loads:
+        copy.start()
+    pieces = [
+        pltpu.make_async_copy(
+            wout_ref.at[pl.ds(i * hw, hw), pl.ds(e * hw, hw)], pbuf.at[i], pload.at[i]
+        )
+        for i in range(per)
+    ]
+    for copy in pieces:
+        copy.start()
+    meet_all(nz, ne, z, e)
+
+    def rows_of(zz):
+        return pl.ds(pl.multiple_of(zz * depth, depth), depth)
+
+    def hop(j, zz, dist, up):
+        send, recv = (up_send, up_recv) if up else (dn_send, dn_recv)
+        here = wq_ref.at[j, rows_of(zz)]
+        src = wbuf.at[j] if dist == 1 else here
+        to = z + 1 if up else z - 1
+        return remote(src, here, send.at[dist, j], recv.at[dist, j], (to, e))
+
+    keeps = []
+    for j in range(kinds):
+        loads[j].wait()
+
+        @pl.when(z + 1 < nz)
+        def _():
+            hop(j, z, 1, True).start()
+
+        @pl.when(z > 0)
+        def _():
+            hop(j, z, 1, False).start()
+
+        keep = pltpu.make_async_copy(wbuf.at[j], wq_ref.at[j, rows_of(z)], wkeep.at[j])
+        keep.start()
+        keeps.append(keep)
+
+    def wait_all(ref, send, recv, count):
+        most = ref.at[pl.ds(0, count)]
+        both = remote(most, most, send, recv, (z, flip(e, 1)))
+        both.wait_send()
+        both.wait_recv()
+
+    small_out[z] = small_ref[...]
+    for r in range(1, nz):
+        remote(
+            small_ref, small_out.at[z], small_send, small_recv, (lax.rem(z + r, nz), e)
+        ).start()
+    seg_out[e] = seg_ref[...]
+    for r in range(1, ne):
+        remote(seg_ref, seg_out.at[e], seg_send, seg_recv, (z, lax.rem(e + r, ne))).start()
+    net = PlaneGather(nz, ne, z, e, False, x_ref, out_ref, zsend, zrecv, send, recv, local)
+    net.start_round(0)
+
+    columns = pl.ds(e * hw, hw)
+    for i in range(per):
+        pieces[i].wait()
+    for r in range(nz):
+        for i in range(per):
+            to = (lax.rem(z + r, nz), z * per + i)
+            give = remote(pbuf.at[i], wo_ref.at[:, columns], psend.at[r, i], precv, to)
+            if r > 0:
+                give.start()
+            else:
+                own = pltpu.make_async_copy(pbuf.at[i], wo_ref.at[:, columns], pkeep)
+
+                @pl.when(to[1] == e)
+                def _():
+                    own.start()
+
+                @pl.when(to[1] != e)
+                def _():
+                    give.start()
+    net.finish_round(0)
+    for dist in range(1, nz):
+        for j in range(kinds):
+
+            @pl.when(z - dist >= 0)
+            def _():
+                got = wq_ref.at[j, rows_of(z - dist)]
+                remote(got, got, up_send.at[dist, j], up_recv.at[dist, j], (z, e)).wait_recv()
+
+                @pl.when(z + 1 < nz)
+                def _():
+                    if dist + 1 < nz:
+                        hop(j, z - dist, dist + 1, True).start()
+
+            @pl.when(z + dist < nz)
+            def _():
+                got = wq_ref.at[j, rows_of(z + dist)]
+                remote(got, got, dn_send.at[dist, j], dn_recv.at[dist, j], (z, e)).wait_recv()
+
+                @pl.when(z > 0)
+                def _():
+                    if dist + 1 < nz:
+                        hop(j, z + dist, dist + 1, False).start()
+
+    net.finish()
+    for keep in keeps:
+        keep.wait()
+    for dist in range(1, nz):
+        for j in range(kinds):
+
+            @pl.when((z - dist + 1 >= 0) & (z + 1 < nz))
+            def _():
+                hop(j, z - dist + 1, dist, True).wait_send()
+
+            @pl.when((z + dist - 1 < nz) & (z > 0))
+            def _():
+                hop(j, z + dist - 1, dist, False).wait_send()
+
+    for r in range(nz):
+        for i in range(per):
+            to = (lax.rem(z + r, nz), z * per + i)
+            give = remote(pbuf.at[i], wo_ref.at[:, columns], psend.at[r, i], precv, to)
+            if r > 0:
+                give.wait_send()
+            else:
+                own = pltpu.make_async_copy(pbuf.at[i], wo_ref.at[:, columns], pkeep)
+
+                @pl.when(to[1] == e)
+                def _():
+                    own.wait()
+
+                @pl.when(to[1] != e)
+                def _():
+                    give.wait_send()
+
+    def wait_pieces(count):
+        most = wo_ref.at[:, pl.ds(0, count * hw)]
+        remote(most, most, psend.at[0, 0], precv, (z, e)).wait_recv()
+
+    @pl.when(z == e // per)
+    def _():
+        wait_pieces(ne - 1)
+
+    @pl.when(z != e // per)
+    def _():
+        wait_pieces(ne)
+
+    wait_all(small_out, small_send, small_recv, nz - 1)
+    wait_all(seg_out, seg_send, seg_recv, ne - 1)
+
+
+def start_gather(x, w_qkv, w_out, small, seg, nz, ne, hw, cid):
+    kinds, depth, width = w_qkv.shape
+    per = ne // nz
+    return pl.pallas_call(
+        functools.partial(start_kernel, nz, ne),
+        out_shape=[
+            jax.ShapeDtypeStruct((ne, *x.shape), x.dtype),
+            jax.ShapeDtypeStruct((kinds, nz * depth, hw), BF),
+            jax.ShapeDtypeStruct((hw, width), BF),
+            jax.ShapeDtypeStruct((nz, *small.shape), small.dtype),
+            jax.ShapeDtypeStruct((ne, *seg.shape), seg.dtype),
+        ],
+        in_specs=[VMEM, ANY, ANY, VMEM, VMEM],
+        out_specs=[ANY, ANY, ANY, VMEM, VMEM],
+        scratch_shapes=[
+            pltpu.VMEM((kinds, depth, hw), BF),
+            pltpu.VMEM((per, hw, hw), BF),
+            *PlaneGather.scratch(nz, ne, False),
+            DMA((nz, kinds)), DMA((nz, kinds)), DMA((nz, kinds)), DMA((nz, kinds)),
+            DMA((kinds,)), DMA((kinds,)), DMA((per,)), DMA((nz, per)), DMA, DMA,
+            DMA, DMA, DMA, DMA,
+        ],
+        compiler_params=pltpu.CompilerParams(collective_id=cid, has_side_effects=True),
+        name="start_gather",
+    )(x, w_qkv, w_out, small, seg)
+
+
+def lay_kernel(kinds, hw, x_ref, *outs):
+    for k in range(kinds):
+        piece = x_ref[0, :, k * hw : (k + 1) * hw].astype(F32)
+        if k < kinds - 1:
+            outs[0][k] = piece
+        else:
+            outs[1][...] = piece
+
+
+def lay_mixer(wide, kinds, hw):
+    ne, rows, _ = wide.shape
+    return pl.pallas_call(
+        functools.partial(lay_kernel, kinds, hw),
+        grid=(ne,),
+        in_specs=[pl.BlockSpec((1, rows, kinds * hw), lambda i: (i, 0, 0))],
+        out_specs=[
+            pl.BlockSpec((kinds - 1, rows, hw), lambda i: (0, 0, i)),
+            pl.BlockSpec((rows, hw), lambda i: (0, i)),
+        ],
+        out_shape=[
+            jax.ShapeDtypeStruct((kinds - 1, rows, ne * hw), F32),
+            jax.ShapeDtypeStruct((rows, ne * hw), F32),
+        ],
+        name="lay_mixer",
+    )(wide)
+
+
+def lay_experts_kernel(per_dev, fl, x_ref, gate_ref, up_ref):
+    for i in range(per_dev):
+        gate_ref[i] = x_ref[0, :, i * fl : (i + 1) * fl].astype(F32)
+        up_ref[i] = x_ref[0, :, (per_dev + i) * fl : (per_dev + i + 1) * fl].astype(F32)
+
+
+def lay_experts(wide, per_dev, fl):
+    nz, rows, _ = wide.shape
+    out = jax.ShapeDtypeStruct((per_dev, rows, nz * fl), F32)
+    spec = pl.BlockSpec((per_dev, rows, fl), lambda i: (0, 0, i))
+    return pl.pallas_call(
+        functools.partial(lay_experts_kernel, per_dev, fl),
+        grid=(nz,),
+        in_specs=[pl.BlockSpec((1, rows, 2 * per_dev * fl), lambda i: (i, 0, 0))],
+        out_specs=[spec, spec],
+        out_shape=[out, out],
+        name="lay_experts",
+    )(wide)
+
+
 def moe_kernel(
     fl, h_ref, g_ref, gate_ref, win_ref, wdt_ref, wd_ref, wint_ref,
     mix_ref, gh_ref, gg_ref, dwin_ref, dwd_ref, acc_in, acc_d,
 ):
     step = pl.program_id(0)
+    tile, width = h_ref.shape
+    per_dev = gate_ref.shape[1]
     h = h_ref[...]
     g = g_ref[...]
     gates = gate_ref[...]
     pre = dot(h, win_ref[...], NN)
     graw = dot(g, wdt_ref[...], NN)
-    scaled_act, grad_gate, grad_up, gg = [], [], [], []
-    for i in range(2):
+    scaled_act, grad_gate, grad_up = [], [], []
+    lanes = lax.broadcasted_iota(jnp.int32, (tile, 128), 1)
+    gg = jnp.zeros((tile, 128), F32)
+    for i in range(per_dev):
         u = pre[:, i * fl : (i + 1) * fl]
-        w = pre[:, (2 + i) * fl : (3 + i) * fl]
+        w = pre[:, (per_dev + i) * fl : (per_dev + 1 + i) * fl]
         gr = graw[:, i * fl : (i + 1) * fl]
         gate = gates[:, i : i + 1]
         sig = 1.0 / (1.0 + jnp.exp(-u))
         silu = u * sig
         act = silu * w
-        gg.append(jnp.sum(act.astype(BF).astype(F32) * gr, axis=-1, keepdims=True))
+        total = jnp.sum(act.astype(BF).astype(F32) * gr, axis=-1, keepdims=True)
+        gg = jnp.where(lanes == i, total, gg)
         scaled_act.append((gate * act).astype(BF))
         gact = gate * gr
         grad_gate.append((gact * w * (sig * (1.0 + u * (1.0 - sig)))).astype(BF))
         grad_up.append((gact * silu).astype(BF))
     a = jnp.concatenate(scaled_act, axis=1)
     gin = jnp.concatenate(grad_gate + grad_up, axis=1)
-    mix_ref[...] = dot(a, wd_ref[...], NN).astype(BF)
+    blocks, rows = mix_ref.shape[0], mix_ref.shape[2]
+    mix_ref[...] = dot(a, wd_ref[...], NN).astype(BF).reshape(blocks, 1, rows, width)
     gh_ref[...] = dot(gin, wint_ref[...], NN).astype(BF)
-    gg_ref[...] = jnp.concatenate(gg, axis=1)
+    turned = gg.T[:8]
+    for i in range(blocks):
+        gg_ref[i] = turned[:, i * rows : (i + 1) * rows]
 
     @pl.when(step == 0)
     def _():
@@ -125,27 +700,33 @@
         dwd_ref[...] = acc_d[...]
 
 
-def moe(h_all, g_all, gates2, w_in, wd_t, wd, w_in_t, tile):
+def moe(h_all, g_all, gates2, w_in, wd_t, wd, w_in_t, nz, ne, rows_dev, blocks):
     count, width = h_all.shape
     hid4 = w_in.shape[1]
     hid2 = wd.shape[0]
-    fl = hid2 // 2
+    per_dev = gates2.shape[1]
+    fl = hid2 // per_dev
+    tile = blocks * rows_dev
+    turns = ne // blocks
     rows = lambda n: pl.BlockSpec((tile, n), lambda i: (i, 0))
     whole = lambda s: pl.BlockSpec(s, lambda i: (0, 0), pipeline_mode=pl.Buffered(1))
     return pl.pallas_call(
         functools.partial(moe_kernel, fl),
         grid=(count // tile,),
         in_specs=[
-            rows(width), rows(width), rows(2),
+            rows(width), rows(width), rows(per_dev),
             whole(w_in.shape), whole(wd_t.shape), whole(wd.shape), whole(w_in_t.shape),
         ],
         out_specs=[
-            rows(width), rows(width), rows(2), whole((width, hid4)), whole((hid2, width)),
+            pl.BlockSpec((blocks, 1, rows_dev, width), lambda i: (i % turns, i // turns, 0, 0)),
+            rows(width),
+            pl.BlockSpec((blocks, 8, rows_dev), lambda i: (i, 0, 0)),
+            whole((width, hid4)), whole((hid2, width)),
         ],
         out_shape=[
+            jax.ShapeDtypeStruct((ne, nz, rows_dev, width), BF),
             jax.ShapeDtypeStruct((count, width), BF),
-            jax.ShapeDtypeStruct((count, width), BF),
-            jax.ShapeDtypeStruct((count, 2), F32),
+            jax.ShapeDtypeStruct((nz * ne, 8, rows_dev), F32),
             jax.ShapeDtypeStruct((width, hid4), BF),
             jax.ShapeDtypeStruct((hid2, width), F32),
         ],
@@ -175,57 +756,55 @@
     fl = hidden // nz
     both = ("dp", "expert")
 
-    qkv_cols = lax.dynamic_slice_in_dim(w_qkv, e * hw, hw, axis=2)
-    wq = lax.all_gather(qkv_cols, "dp", axis=0, tiled=True).reshape(width, 3 * hw)
-    out_cols = lax.dynamic_slice_in_dim(w_out, e * hw, hw, axis=1)
-    out_cols = lax.all_gather(out_cols, "dp", axis=0, tiled=True)
-    wo = lax.all_to_all(
-        out_cols.reshape(ne, hw, hw), "expert", split_axis=0, concat_axis=0, tiled=True
-    )
-    wo = wo.transpose(1, 0, 2).reshape(hw, width)
-    small = lax.all_gather(
-        jnp.concatenate([gains, w_router], axis=1), "dp", axis=0, tiled=True
-    )
-    gain_mat = small[:, :4].astype(F32)
-    router = small[:, 4:]
-    my_gains = lax.dynamic_slice_in_dim(gain_mat, e * hw, hw, axis=0)
-
-    g_all = lax.all_gather(cotangent, both, axis=0, tiled=True)
+    pad = -(expert_count + 4) % 16
+    small = jnp.concatenate(
+        [w_router.T, gains.T, jnp.zeros((pad, gains.shape[0]), BF)], axis=0
+    )
+    seg8 = jnp.broadcast_to(segments[:, None, :], (num_seqs, 8, length)).reshape(-1, length)
+    in_all, wq, wo, small, seg_all = start_gather(
+        inputs, w_qkv.transpose(1, 0, 2), w_out, small, seg8, nz, ne, hw, 0
+    )
+    small = small.transpose(1, 0, 2).reshape(-1, width)
+    router_t = small[:expert_count]
+    gain_mat = small[expert_count : expert_count + 4].astype(F32)
+    my_gains = lax.dynamic_slice_in_dim(gain_mat, e * hw, hw, axis=1)
+    seg_all = seg_all.reshape(ne * num_seqs, 8, length)[:, 0]
+
+    cot, _ = lax.optimization_barrier((cotangent, small))
+    g_all = lax.all_gather(cot, both, axis=0, tiled=True)
+    in_all = in_all.reshape(ne * count, width).astype(F32)
+    h1_all = (in_all * rms_scale(in_all) * gain_mat[0]).astype(BF)
     inputs_f = inputs.astype(F32)
     scale_one = rms_scale(inputs_f)
-    h1 = (inputs_f * scale_one * gain_mat[:, 0]).astype(BF)
-    h1_all = lax.all_gather(h1, "expert", axis=0, tiled=True)
-    seg_all = lax.all_gather(segments, "expert", axis=0, tiled=True)
     plane = h1_all.shape[0]
     shape_heads = (ne * num_seqs, length, heads, HD)
 
-    proj = dot(h1_all, wq, NN)
-    q, k, v = proj[:, :hw], proj[:, hw : 2 * hw], proj[:, 2 * hw :]
+    q, k, v = [dot(h1_all, wq[j], NN) for j in range(3)]
     sums = jnp.stack([jnp.sum(q * q, axis=-1), jnp.sum(k * k, axis=-1)])
     scales = lax.rsqrt(lax.psum(sums, "expert") / width + EPS)
     aq, ak = scales[0][:, None], scales[1][:, None]
     cos_tab, sin_tab = rope_tables(length)
-    rq = rotate((q * aq * my_gains[:, 1]).reshape(shape_heads), cos_tab, sin_tab).astype(BF)
-    rk = rotate((k * ak * my_gains[:, 2]).reshape(shape_heads), cos_tab, sin_tab).astype(BF)
+    rq = rotate((q * aq * my_gains[1]).reshape(shape_heads), cos_tab, sin_tab).astype(BF)
+    rk = rotate((k * ak * my_gains[2]).reshape(shape_heads), cos_tab, sin_tab).astype(BF)
     vb = v.astype(BF).reshape(shape_heads)
     o, lse = jax.vmap(attend_forward)(rq, rk, vb, seg_all)
     o = o.reshape(plane, hw)
     x1_part = dot(o, wo, NN).astype(BF)
-    x1 = inputs_f + lax.psum_scatter(
-        x1_part, "expert", scatter_dimension=0, tiled=True
-    ).astype(F32)
+    (x1_sum,) = scatter_tokens(x1_part.reshape(ne, count, width), nz, ne, False, 1)
+    x1 = inputs_f + x1_sum
 
     a2 = rms_scale(x1)
-    h2 = (x1 * a2 * gain_mat[:, 3]).astype(BF)
-    probs = jax.nn.softmax(dot(h2, router, NN), axis=-1)
+    h2 = (x1 * a2 * gain_mat[3]).astype(BF)
+    probs = jax.nn.softmax(dot(h2, router_t, NT), axis=-1)
     picks = jnp.sum(
         (routes[:, :, None] == jnp.arange(expert_count, dtype=jnp.int32)).astype(F32), axis=1
     )
     gates = picks * probs
 
-    h2_all = lax.all_gather(h2, both, axis=0, tiled=True)
-    gates_all = lax.all_gather(gates, both, axis=0, tiled=True)
+    h2_all, gates_all = gather_tokens(h2, nz, ne, True, 2, small=gates.T)
+    h2_all = h2_all.reshape(-1, width)
     gates2 = lax.dynamic_slice_in_dim(gates_all, e * per_dev, per_dev, axis=1)
+    gates2 = gates2.transpose(0, 2, 1).reshape(-1, per_dev)
     wg = lax.dynamic_slice_in_dim(w_gate, z * fl, fl, axis=2)
     wu = lax.dynamic_slice_in_dim(w_up, z * fl, fl, axis=2)
     wd = lax.dynamic_slice_in_dim(w_down, z * fl, fl, axis=1)
@@ -234,69 +813,65 @@
     ).reshape(2 * per_dev * fl, width)
     w_in = jnp.concatenate([wg[0], wg[1], wu[0], wu[1]], axis=1)
     wd = wd.reshape(per_dev * fl, width)
-    mix, gh, gg, dwin, dwd = moe(h2_all, g_all, gates2, w_in, wd.T, wd, w_in_t, 512)
-
-    gg_full = lax.dynamic_update_slice_in_dim(
-        jnp.zeros((gg.shape[0], expert_count), F32), gg, e * per_dev, axis=1
-    )
-    grad_gates = lax.psum_scatter(gg_full, both, scatter_dimension=0, tiled=True)
-
-    def scatter_tokens(part):
-        part = part.reshape(nz, ne, count, width).transpose(1, 0, 2, 3).reshape(-1, width)
-        part = lax.psum_scatter(part, "expert", scatter_dimension=0, tiled=True)
-        return lax.psum_scatter(part, "dp", scatter_dimension=0, tiled=True).astype(F32)
-
-    grad_from_experts = scatter_tokens(gh)
-    mixed = scatter_tokens(mix)
-    output = (x1 + mixed).astype(BF)
+    mix, gh, gg, dwin, dwd = moe(
+        h2_all, g_all, gates2, w_in, wd.T, wd, w_in_t, nz, ne, count, min(4, ne)
+    )
+    grad_from_experts, gg = scatter_tokens(
+        gh.reshape(nz * ne, count, width), nz, ne, True, 3, small=gg
+    )
+    grad_gates = jnp.sum(gg.reshape(nz, ne, 8, count), axis=0)[:, :per_dev]
+    grad_gates = grad_gates.reshape(expert_count, count).T
+
+    mix = lax.psum_scatter(mix.reshape(-1, width), "expert", scatter_dimension=0, tiled=True)
+    mix = lax.psum_scatter(mix, "dp", scatter_dimension=0, tiled=True)
+    output = (x1 + mix.astype(F32)).astype(BF)
 
     dwin = lax.all_to_all(
         dwin.reshape(nz, width // nz, 2 * per_dev * fl), "dp", split_axis=0, concat_axis=0, tiled=True
     )
-    dwin = dwin.reshape(nz, width // nz, 2, per_dev, fl).transpose(2, 3, 1, 0, 4)
-    dwin = dwin.reshape(2, per_dev, width // nz, hidden).astype(F32)
+    grad_w_gate, grad_w_up = lay_experts(dwin, per_dev, fl)
     grad_w_down = dwd.reshape(per_dev, fl, width)
 
     grad_top = cotangent.astype(F32)
     grad_probs = picks * grad_gates
     glog = (probs * (grad_probs - jnp.sum(probs * grad_probs, axis=-1, keepdims=True))).astype(BF)
     local_router = dot(h2, glog, TN)
-    gh2 = grad_from_experts + dot(glog, router, NT)
-    grad_ffn, gain_ffn = rms_backward(x1, a2, gain_mat[:, 3], gh2)
+    gh2 = grad_from_experts + dot(glog, router_t, NN)
+    grad_ffn, gain_ffn = rms_backward(x1, a2, gain_mat[3], gh2)
     gx1 = grad_top + grad_ffn
     gab = gx1.astype(BF)
 
-    gab_all = lax.all_gather(gab, "expert", axis=0, tiled=True)
+    gab_all = gather_tokens(gab, nz, ne, False, 4)[0].reshape(-1, width)
     go = dot(gab_all, wo, NT).astype(BF).reshape(shape_heads)
     grad_q, grad_k, gv = jax.vmap(attend_backward)(rq, rk, vb, seg_all, lse, go)
     gqn = rotate(grad_q, cos_tab, -sin_tab).reshape(plane, hw)
     gkn = rotate(grad_k, cos_tab, -sin_tab).reshape(plane, hw)
     nq, nk = q * aq, k * ak
-    sq, sk = gqn * my_gains[:, 1], gkn * my_gains[:, 2]
+    sq, sk = gqn * my_gains[1], gkn * my_gains[2]
     sums = jnp.stack([jnp.sum(sq * nq, axis=-1), jnp.sum(sk * nk, axis=-1)])
     means = lax.psum(sums, "expert") / width
     gq = (aq * (sq - nq * means[0][:, None])).astype(BF)
     gk = (ak * (sk - nk * means[1][:, None])).astype(BF)
-    gproj = jnp.concatenate([gq, gk, gv.reshape(plane, hw)], axis=1)
+    gproj = [gq, gk, gv.reshape(plane, hw)]
     gain_q, gain_k = jnp.sum(gqn * nq, axis=0), jnp.sum(gkn * nk, axis=0)
 
-    gh1_part = dot(gproj, wq, NT).astype(BF)
-    gh1 = lax.psum_scatter(gh1_part, "expert", scatter_dimension=0, tiled=True).astype(F32)
-    grad_front, gain_attn = rms_backward(inputs_f, scale_one, gain_mat[:, 0], gh1)
+    gh1_part = sum(dot(part, wq[j], NT) for j, part in enumerate(gproj)).astype(BF)
+    (gh1,) = scatter_tokens(gh1_part.reshape(ne, count, width), nz, ne, False, 5)
+    grad_front, gain_attn = rms_backward(inputs_f, scale_one, gain_mat[0], gh1)
     grad_inputs = (gx1 + grad_front).astype(BF)
 
-    part_qkv = dot(h1_all, gproj, TN).astype(BF)
     part_out = dot(o, gab_all, TN).astype(BF)
     part_out = lax.all_to_all(
         part_out.reshape(hw, ne, hw).transpose(1, 0, 2),
         "expert", split_axis=0, concat_axis=0, tiled=True,
     ).reshape(width, hw)
-    parts = jnp.concatenate([part_qkv, part_out], axis=1)
-    mine = lax.psum_scatter(parts, "dp", scatter_dimension=0, tiled=True)
-    wide = lax.all_gather(mine, "expert", axis=0)
-    wide = wide.reshape(ne, width // nz, 4, hw).transpose(1, 2, 0, 3)
-    wide = wide.reshape(width // nz, 4, width).astype(F32)
-    grad_w_qkv, grad_w_out = wide[:, :3], wide[:, 3]
+    parts = [dot(h1_all, part, TN).astype(BF) for part in gproj] + [part_out]
+    mine = lax.psum_scatter(
+        jnp.concatenate(parts, axis=1), "dp", scatter_dimension=0, tiled=True
+    )
+    wide = gather_tokens(mine, nz, ne, False, 6)[0]
+    grad_w_qkv, grad_w_out = lay_mixer(wide, 4, hw)
+    grad_w_qkv = grad_w_qkv.transpose(1, 0, 2)
 
     place = lambda part: lax.dynamic_update_slice_in_dim(
         jnp.zeros((width,), F32), part, e * hw, axis=0
@@ -318,8 +893,8 @@
         grad_w_out,
         grad_w_router,
         grad_gains,
-        dwin[0],
-        dwin[1],
+        grad_w_gate,
+        grad_w_up,
         grad_w_down,
     )
 

time: 1470 us -> 1090 us (0.74)
  waiting for transfers between devices: 890 us -> 249 us
  Pallas kernels: 96.4 us -> 638 us
  local copies, waits for them, and re-layouts: 218 us -> 49.2 us
  blocking collectives: 114 us -> 26.3 us
    pallas_call x0 -> x9, Pallas kernels: none -> 541 us  [the longest x3 184 us: scatter_tokens(): pl.pallas_call(functools.partial(scatter_kernel, nz, ne, spread, small is...]
    reduce_scatter x8 -> x3, waiting for transfers between devices: 493 us -> 71.9 us  [the longest x1 71.9 us: body(): lax.psum_scatter(jnp.concatenate(parts, axis=1), 'dp', scatter_dimension=...]
    all_gather x7 -> x1, waiting for transfers between devices: 221 us -> 0.01 us  [body(): g_all = lax.all_gather(cot, both, axis=0, tiled=True)]
    psum x1, waiting for transfers between devices: 27.6 us -> 176 us  [body(): tiny = lax.psum(tiny, both)]
    all_to_all x1, waiting for transfers between devices: 128 us -> 0.01 us  [body(): lax.all_to_all(dwin.reshape(nz, width // nz, 2 * per_dev * fl), 'dp', spl...]
    all_gather x3 -> x0, blocking collectives: 87.7 us -> none  [the longest x1 54 us: body(): gates_all = lax.all_gather(gates, both, axis=0, tiled=True)]
    convert_element_type x4 -> x0, local copies, waits for them, and re-layouts: 62.1 us -> none  [the longest x2 38.2 us: body(): wide = wide.reshape(width // nz, 4, width).astype(F32)]
    reshape x3 -> x1, local copies, waits for them, and re-layouts: 28.4 us -> 1.25 us  [body(): jnp.broadcast_to(segments[:, None, :], (num_seqs, 8, length))]
  transfers between devices with their start and end apart: 19 -> 7, of which waited for: 15 -> 3; matrix products, arithmetic and copies ran while one was open for 12% -> 13% of each run, Pallas kernels for 0% -> 50%
where the time goes in v2:
time: 1090 us
  Pallas kernels  638 us (59%)
  waiting for transfers between devices  249 us (23%)
  matrix products  51.8 us (5%)
  local copies, waits for them, and re-layouts  49.2 us (5%)
  other arithmetic  48.5 us (4%)
  blocking collectives  26.3 us (2%)
  between operations  15.1 us (1%)
    pallas_call x3, Pallas kernels, scatter_tokens(): pl.pallas_call(functools.partial(scatter_kernel, nz, ne, spread, small is...  184 us
    pallas_call x3, Pallas kernels, gather_tokens(): pl.pallas_call(functools.partial(gather_kernel, nz, ne, spread, small is...  181 us
    psum x1, waiting for transfers between devices, body(): tiny = lax.psum(tiny, both)  176 us
    pallas_call x1, Pallas kernels, start_gather(): pl.pallas_call(functools.partial(start_kernel, nz, ne), out_shape=[jax.Sh...  159 us
    pallas_call x1, Pallas kernels, moe(): pl.pallas_call(functools.partial(moe_kernel, fl), grid=(count // tile,),...  96.9 us
    reduce_scatter x1, waiting for transfers between devices, body(): lax.psum_scatter(jnp.concatenate(parts, axis=1), 'dp', scatter_dimension=...  71.9 us
    dot_general x15, matrix products, dot(): return lax.dot_general(a, b, (dims, ((), ())), preferred_element_type=F32)  39.3 us
  transfers between devices with their start and end apart: 7, of which 3 were waited for; matrix products, arithmetic and copies ran while one was open for 13% of the time, Pallas kernels for 50%

profile of v2, /device:TPU:0, one launch (start us, length us, event | category | flops | bytes accessed | tf_op | source)
XLA Modules:
  0.0 1087.0 jit_solution(12707361441097352740)
XLA Ops:
  10.7 159.4 %start_gather.1 = (bf16[8,128,2048]{2,1,0:T(8,128)(2,1)}, bf16[3,2048,256]{2,1,0:T(8,128)(2,1)}, bf16[256,2048]{1,0:T(8,128)(2,1)}, bf16[4,32,512]{2,1,0:T(8,128)(2,1)}, s32[8,8,128]{2,1,0:T(8,128)}) custom-call(bf16[128,2048]{1,0:T(8,128)(2,1)} %x_ref.1, bf16[3,512,2048]{2,1,0:T(8,128)(2,1)} %bitcast.195, bf16[512,2048]{1,0:T(8,128)(2,1)} %wout_ref.1, ...), custom_call_target="tpu_custom_call" | custom-call | tf_op jit(solution)/shard_map/start_gather/pallas_call | solution.py:580
  179.0 12.6 %psum.21 = f32[2,1024]{1,0:T(2,128)S(1)} all-reduce(f32[2,1024]{1,0:T(2,128)S(1)} %pad_maximum_fusion.11), channel_id=1, replica_groups=mesh['dp'=4,'expert'=8] {'expert'}, use_global_device_ids=true, to_apply=%region_3.0 | all-reduce | flops 2048 | bytes 16384 | tf_op jit(solution)/shard_map/psum | solution.py:784
  214.1 26.0 %scatter_tokens.3 = f32[128,2048]{1,0:T(8,128)} custom-call(bf16[8,128,2048]{2,1,0:T(8,128)(2,1)} %bitcast.185), custom_call_target="tpu_custom_call" | custom-call | tf_op jit(solution)/shard_map/scatter_tokens/pallas_call | solution.py:405
  243.8 106.4 %gather_tokens.3 = (bf16[32,128,2048]{2,1,0:T(8,128)(2,1)}, f32[32,16,128]{2,1,0:T(8,128)}) custom-call(bf16[128,2048]{1,0:T(8,128)(2,1)} %copy-done.12, f32[16,128]{1,0:T(8,128)} %multiply_bitcast_fusion.2.refs_1_), custom_call_target="tpu_custom_call" | custom-call | tf_op jit(solution)/shard_map/gather_tokens/pallas_call | solution.py:260
  358.1 6.2 copy.84
  373.6 96.9 %moe.1 = (bf16[8,4,128,2048]{3,2,1,0:T(8,128)(2,1)}, bf16[4096,2048]{1,0:T(8,128)(2,1)}, f32[32,8,128]{2,1,0:T(8,128)}, bf16[2048,1024]{1,0:T(8,128)(2,1)}, f32[512,2048]{1,0:T(8,128)}) custom-call(bf16[4096,2048]{1,0:T(8,128)(2,1)} %bitcast.260, bf16[4096,2048]{1,0:T(8,128)(2,1)} %all-gather.2.cloned.1.call-done.g_ref, f32[4096,2]{1,0:T(8,128)} %bitcast.211, ...), custom_call_target="tpu_custom_call" | custom-call | flops 77309411328 | bytes 117440512 | tf_op jit(solution)/shard_map/moe/pallas_call | solution.py:713
  470.5 5.2 fusion.2
  475.7 131.7 %scatter_tokens.4 = (f32[128,2048]{1,0:T(8,128)}, f32[32,8,128]{2,1,0:T(8,128)}) custom-call(bf16[32,128,2048]{2,1,0:T(8,128)(2,1)} %bitcast.187, f32[32,8,128]{2,1,0:T(8,128)} %get-tuple-element.36.refs_1_), custom_call_target="tpu_custom_call" | custom-call | tf_op jit(solution)/shard_map/scatter_tokens/pallas_call | solution.py:405
  612.4 34.1 %gather_tokens.4 = bf16[8,128,2048]{2,1,0:T(8,128)(2,1)} custom-call(bf16[128,2048]{1,0:T(8,128)(2,1)} %fusion.75.refs_0_), custom_call_target="tpu_custom_call" | custom-call | tf_op jit(solution)/shard_map/gather_tokens/pallas_call | solution.py:260
  646.5 4.7 convolution_convert_fusion.7
  667.6 4.4 multiply_subtract_fusion
  684.9 13.7 %psum.22 = f32[2,1024]{1,0:T(2,128)S(1)} all-reduce(f32[2,1024]{1,0:T(2,128)S(1)} %pad_maximum_fusion.12), channel_id=1, replica_groups=mesh['dp'=4,'expert'=8] {'expert'}, use_global_device_ids=true, to_apply=%region_19.20 | all-reduce | flops 2048 | bytes 16384 | tf_op jit(solution)/shard_map/psum | solution.py:852
  705.2 4.7 add_convert_fusion
  709.9 26.1 %scatter_tokens.5 = f32[128,2048]{1,0:T(8,128)} custom-call(bf16[8,128,2048]{2,1,0:T(8,128)(2,1)} %bitcast.188), custom_call_target="tpu_custom_call" | custom-call | tf_op jit(solution)/shard_map/scatter_tokens/pallas_call | solution.py:405
  740.6 4.3 all-to-all-start
  746.6 4.7 convolution_convert_fusion.3
  752.7 4.7 convolution_convert_fusion.4
  760.2 3.8 pad_maximum_fusion.2
  764.1 4.9 all-to-all-start.1
  769.6 175.5 %all-reduce.2.cloned.1.call-done = f32[2048,20]{0,1:T(8,128)} async-done(((f32[2048,20]{0,1:T(8,128)}), f32[2048,20]{0,1:T(8,128)}) %all-reduce.2.cloned.1.call-update) | async-done | bytes 163856 | tf_op jit(solution)/shard_map/psum | solution.py:886
  947.8 5.9 lay_experts.1
  953.7 71.9 %reduce-scatter.8.cloned.1.call-done.refs_0_ = bf16[512,1024]{1,0:T(8,128)(2,1)} async-done(((bf16[2048,1024]{1,0:T(8,128)(2,1)}), bf16[512,1024]{1,0:T(8,128)(2,1)}) %reduce-scatter.8.cloned.1.call-update) | async-done | bytes 1048592 | tf_op jit(solution)/shard_map/reduce_scatter | solution.py:869
  1025.6 41.0 %gather_tokens.5.x_ref = bf16[8,512,1024]{2,1,0:T(8,128)(2,1)} custom-call(bf16[512,1024]{1,0:T(8,128)(2,1)} %reduce-scatter.8.cloned.1.call-done.refs_0_), custom_call_target="tpu_custom_call" | custom-call | tf_op jit(solution)/shard_map/gather_tokens/pallas_call | solution.py:260
  1066.6 10.3 lay_mixer.1
  (189 shorter events, 113.0 us)
Async XLA Ops:
  7.2 366.4 %all-gather.2.cloned.1.call-start = ((), (), s32[]{:S(2)}) async-start(), calls=%async_computation.5 | async-start | bytes 17301504 | tf_op jit(solution)/shard_map/all_gather | solution.py:774
  7.9 761.1 %reduce-scatter.4.cloned.1.call-start = ((), (), s32[]{:S(2)}) async-start(), calls=%async_computation.6 | async-start | bytes 18874368 | tf_op jit(solution)/shard_map/reduce_scatter | solution.py:825
  177.7 19.7 %copy-start.7 = (f32[1024,256]{0,1:T(8,128)}, f32[1024,256]{0,1:T(8,128)S(1)}, u32[]{:S(2)}) copy-start(f32[1024,256]{0,1:T(8,128)S(1)} %get-tuple-element.94) | copy-start | bytes 3145732
  179.0 17.9 %copy-start.5 = (f32[1024,256]{0,1:T(8,128)}, f32[1024,256]{0,1:T(8,128)S(1)}, u32[]{:S(2)}) copy-start(f32[1024,256]{0,1:T(8,128)S(1)} %get-tuple-element.96) | copy-start | bytes 3145732
  207.5 6.7 copy-start.29
  214.1 26.0 %copy-start.36 = (bf16[4,32,512]{2,1,0:T(8,128)(2,1)S(1)}, bf16[4,32,512]{2,1,0:T(8,128)(2,1)}, u32[]{:S(2)}) copy-start(bf16[4,32,512]{2,1,0:T(8,128)(2,1)} %get-tuple-element.28) | copy-start | bytes 393220
  214.1 26.0 %copy-start.14 = (bf16[128,2048]{1,0:T(8,128)(2,1)S(1)}, bf16[128,2048]{1,0:T(8,128)(2,1)}, u32[]{:S(2)}) copy-start(bf16[128,2048]{1,0:T(8,128)(2,1)} %x_ref.1) | copy-start | bytes 1572868
  214.1 29.0 %copy-start.37 = (s32[128,8]{0,1:T(8,128)S(1)}, s32[128,8]{0,1:T(8,128)}, u32[]{:S(2)}) copy-start(s32[128,8]{0,1:T(8,128)} %param.13) | copy-start | bytes 12292
  475.7 132.7 %copy-start.2 = (f32[128,2048]{1,0:T(8,128)S(1)}, f32[128,2048]{1,0:T(8,128)}, u32[]{:S(2)}) copy-start(f32[128,2048]{1,0:T(8,128)} %copy-done.1) | copy-start | bytes 3145732
  475.7 135.5 %copy-start.18 = (bf16[128,2048]{1,0:T(8,128)(2,1)S(1)}, bf16[128,2048]{1,0:T(8,128)(2,1)}, u32[]{:S(2)}) copy-start(bf16[128,2048]{1,0:T(8,128)(2,1)} %param.21) | copy-start | bytes 1572868
  646.5 8.6 copy-start.4
  651.2 6.7 copy-start.17
  673.3 8.1 copy-start.6
  709.9 26.1 %copy-start.23 = (bf16[8,128,2,128]{1,0,3,2:T(8,128)(2,1)S(1)}, bf16[8,128,2,128]{1,0,3,2:T(8,128)(2,1)}, u32[]{:S(2)}) copy-start(bf16[8,128,2,128]{1,0,3,2:T(8,128)(2,1)} %copy-done.22) | copy-start | bytes 1572868
  736.0 8.9 copy-start.10
  739.5 6.8 copy-start.13
  740.6 19.7 %all-to-all-start = ((bf16[8,256,256]{2,1,0:T(8,128)(2,1)}), bf16[8,256,256]{2,1,0:T(8,128)(2,1)}, u32[]{:S(2)}, u32[]{:S(2)}) async-start(bf16[8,256,256]{2,1,0:T(8,128)(2,1)} %bitcast.204), calls=%async_computation.2 | async-start | bytes 2097152 | tf_op jit(solution)/shard_map/all_to_all | solution.py:864
  744.8 200.3 %all-reduce.2.cloned.1.call-start = ((), (), s32[]{:S(2)}) async-start(), calls=%async_computation.9 | async-start | bytes 393216 | tf_op jit(solution)/shard_map/psum | solution.py:886
  746.6 6.2 copy-start.27
  752.7 272.9 %reduce-scatter.8.cloned.1.call-start = ((), (), s32[]{:S(2)}) async-start(), calls=%async_computation.8 | async-start | bytes 5242880 | tf_op jit(solution)/shard_map/reduce_scatter | solution.py:869
  764.1 183.7 %all-to-all-start.1 = ((bf16[4,512,1024]{2,1,0:T(8,128)(2,1)}), bf16[4,512,1024]{2,1,0:T(8,128)(2,1)}, u32[]{:S(2)}, u32[]{:S(2)}) async-start(bf16[4,512,1024]{2,1,0:T(8,128)(2,1)} %bitcast.202), calls=%async_computation.4 | async-start | bytes 8388608 | tf_op jit(solution)/shard_map/all_to_all | solution.py:829
  769.0 308.0 %reduce-scatter.6.cloned.1.call-start = ((), (), s32[]{:S(2)}) async-start(), calls=%async_computation.7 | async-start | bytes 2621440 | tf_op jit(solution)/shard_map/reduce_scatter | solution.py:826
  1066.6 10.4 copy-start.9
  1066.6 10.3 copy-start.15
  (21 other events, 57.7 us)
Sparse Core Ops, SparseCore 0:
  10.8 163.7 all-gather.1
  470.6 169.3 reduce-scatter.3
  752.8 192.2 all-reduce.1
  947.8 77.7 reduce-scatter.7
  1027.7 44.1 reduce-scatter.5

commit v3 on v2

--- a/solution.py
+++ b/solution.py
@@ -6,6 +6,7 @@
 from jax.experimental import pallas as pl
 from jax.experimental.pallas import tpu as pltpu
 from jax.sharding import PartitionSpec as P
+
 
 HD = 128
 EPS = 1e-05
@@ -203,7 +204,7 @@
             for s in range(2):
                 self.forward(r, s, stage, 0)
 
-    def finish_round(self, r, last=False):
+    def finish_round(self, r):
         stages = len(self.orders[0])
         for stage in range(stages):
             for subset in range(1 << stage):
@@ -217,55 +218,30 @@
             wait()
 
 
-def gather_kernel(nz, ne, spread, small, *refs):
+def gather_kernel(nz, ne, spread, x_ref, out_ref, *sems):
     z, e = lax.axis_index("dp"), lax.axis_index("expert")
-    if small:
-        x_ref, small_ref, out_ref, small_out, *sems, small_send, small_recv = refs
-        meet_all(nz, ne, z, e)
-    else:
-        x_ref, out_ref, *sems = refs
-        meet_column_and_plane(nz, ne, z, e, spread)
+    meet_column_and_plane(nz, ne, z, e, spread)
     net = PlaneGather(nz, ne, z, e, spread, x_ref, out_ref, *sems)
     net.spread_own()
     net.start_round(0)
-    if small:
-        me = z * ne + e
-        small_out[me] = small_ref[...]
-
-        def give(zz, ee, flat):
-            remote(small_ref, small_out.at[me], small_send, small_recv, (zz, ee)).start()
-
-        for_others(nz, ne, z, e, give)
     for r in range(1, net.rounds):
         net.start_round(r)
         net.finish_round(r - 1)
     net.finish_round(net.rounds - 1)
     net.finish()
-    if small:
-        most = small_out.at[pl.ds(0, nz * ne - 1)]
-        everyone = remote(most, most, small_send, small_recv, (z, flip(e, 1)))
-        everyone.wait_send()
-        everyone.wait_recv()
-
-
-def gather_tokens(x, nz, ne, spread, cid, small=None):
+
+
+def gather_tokens(x, nz, ne, spread, cid):
     rounds = nz if spread else 1
-    out = [jax.ShapeDtypeStruct((rounds * ne, *x.shape), x.dtype)]
-    scratch = PlaneGather.scratch(nz, ne, spread)
-    args = [x]
-    if small is not None:
-        out.append(jax.ShapeDtypeStruct((nz * ne, *small.shape), small.dtype))
-        scratch += [DMA, DMA]
-        args.append(small)
     return pl.pallas_call(
-        functools.partial(gather_kernel, nz, ne, spread, small is not None),
-        out_shape=out,
-        in_specs=[VMEM] * len(args),
-        out_specs=[ANY, VMEM][: len(args)],
-        scratch_shapes=scratch,
+        functools.partial(gather_kernel, nz, ne, spread),
+        out_shape=jax.ShapeDtypeStruct((rounds * ne, *x.shape), x.dtype),
+        in_specs=[VMEM],
+        out_specs=ANY,
+        scratch_shapes=PlaneGather.scratch(nz, ne, spread),
         compiler_params=pltpu.CompilerParams(collective_id=cid, has_side_effects=True),
         name="gather_tokens",
-    )(*args)
+    )(x)
 
 
 def add_rows(dst, src, tile=16):
@@ -277,22 +253,10 @@
     lax.fori_loop(0, dst.shape[0] // tile, step, 0)
 
 
-def scatter_kernel(nz, ne, spread, small, *refs):
+def scatter_kernel(nz, ne, spread, x_ref, *refs):
+    out_ref, acc, got, zgot, loads, send, recv, zsend, zrecv = refs[-9:]
     z, e = lax.axis_index("dp"), lax.axis_index("expert")
-    if small:
-        x_ref, small_ref, out_ref, small_out, *rest, small_send, small_recv = refs
-        meet_all(nz, ne, z, e)
-        me = z * ne + e
-        small_out[me] = small_ref[me]
-
-        def give(zz, ee, flat):
-            remote(small_ref.at[flat], small_out.at[me], small_send, small_recv, (zz, ee)).start()
-
-        for_others(nz, ne, z, e, give)
-    else:
-        x_ref, out_ref, *rest = refs
-        meet_column_and_plane(nz, ne, z, e, spread)
-    acc, got, zgot, loads, send, recv, zsend, zrecv = rest
+    meet_column_and_plane(nz, ne, z, e, spread)
     rounds = nz if spread else 1
     stages = ne.bit_length() - 1
     half = out_ref.shape[0] // 2
@@ -370,54 +334,126 @@
         lax.fori_loop(0, half // 16, step, 0)
     for wait in pending:
         wait()
-    if small:
-        most = small_out.at[pl.ds(0, nz * ne - 1)]
-        everyone = remote(most, most, small_send, small_recv, (z, flip(e, 1)))
-        everyone.wait_send()
-        everyone.wait_recv()
-
-
-def scatter_tokens(parts, nz, ne, spread, cid, small=None):
+
+
+def scatter_tokens(parts, nz, ne, spread, cid, after=None):
     rounds = nz if spread else 1
     _, count, width = parts.shape
     half = count // 2
     held = (2 * rounds * (ne // 2 + ne - 1) + 2 * nz) * half * width * 2
     if held > 56_000_000:
-        left = scatter_tokens(parts[..., : width // 2], nz, ne, spread, cid, small)
-        right = scatter_tokens(parts[..., width // 2 :], nz, ne, spread, cid + 16)
+        cut = width // 256 * 128
+        left = scatter_tokens(parts[..., :cut], nz, ne, spread, cid, after)
+        right = scatter_tokens(parts[..., cut:], nz, ne, spread, cid + 16)
         return [jnp.concatenate([left[0], right[0]], axis=1), *left[1:]]
-    out = [jax.ShapeDtypeStruct((count, width), F32)]
-    args = [parts]
-    scratch = [
-        pltpu.VMEM((rounds, 2, ne // 2, half, width), BF),
-        pltpu.VMEM((rounds, 2, ne - 1, half, width), BF),
-        pltpu.VMEM((nz, 2, half, width), BF),
-        DMA((rounds, 2, ne // 2)),
-        DMA((rounds, 2, ne - 1)),
-        DMA((rounds, 2, ne - 1)),
-        DMA((nz, 2)),
-        DMA((nz, 2)),
-    ]
-    if small is not None:
-        out.append(jax.ShapeDtypeStruct(small.shape, small.dtype))
-        args.append(small)
-        scratch += [DMA, DMA]
+    more = [] if after is None else [after]
     return pl.pallas_call(
-        functools.partial(scatter_kernel, nz, ne, spread, small is not None),
-        out_shape=out,
-        in_specs=[ANY, VMEM][: len(args)],
-        out_specs=[VMEM, VMEM][: len(args)],
-        scratch_shapes=scratch,
+        functools.partial(scatter_kernel, nz, ne, spread),
+        out_shape=[jax.ShapeDtypeStruct(m.shape, m.dtype) for m in more]
+        + [jax.ShapeDtypeStruct((count, width), F32)],
+        in_specs=[ANY] * (1 + len(more)),
+        out_specs=[ANY] * len(more) + [VMEM],
+        scratch_shapes=[
+            pltpu.VMEM((rounds, 2, ne // 2, half, width), BF),
+            pltpu.VMEM((rounds, 2, ne - 1, half, width), BF),
+            pltpu.VMEM((nz, 2, half, width), BF),
+            DMA((rounds, 2, ne // 2)),
+            DMA((rounds, 2, ne - 1)),
+            DMA((rounds, 2, ne - 1)),
+            DMA((nz, 2)),
+            DMA((nz, 2)),
+        ],
+        input_output_aliases={1: 0} if more else {},
         compiler_params=pltpu.CompilerParams(
             collective_id=cid, has_side_effects=True, vmem_limit_bytes=64_000_000
         ),
         name="scatter_tokens",
-    )(*args)
+    )(parts, *more)[::-1]
+
+
+def reduce_kernel(nz, ne, x_ref, out_ref, got, total, far, send1, recv1, send2, recv2):
+    z, e = lax.axis_index("dp"), lax.axis_index("expert")
+    per = ne // nz
+    meet_all(nz, ne, z, e)
+    first = []
+    for r in range(1, ne):
+        to = lax.rem(e + r, ne)
+        copy = remote(x_ref.at[to], got.at[r], send1.at[r], recv1.at[r], (z, to))
+        copy.start()
+        first.append(copy)
+    acc = x_ref[e]
+    for r, copy in enumerate(first):
+        copy.wait_recv()
+        acc = acc + got[r + 1]
+    total[...] = acc
+    home, place = e // per, lax.rem(e, per)
+    for r in range(ne):
+        to = lax.rem(e + r, ne)
+        copy = remote(total, far.at[z, place], send2.at[r], recv2, (home, to))
+        if r > 0:
+            copy.start()
+        else:
+
+            @pl.when(home != z)
+            def _():
+                copy.start()
+
+            @pl.when(home == z)
+            def _():
+                far[z, place] = total[...]
+
+    for copy in first:
+        copy.wait_send()
+    for r in range(ne):
+        copy = remote(total, far.at[z, place], send2.at[r], recv2, (home, e))
+        if r > 0:
+            copy.wait_send()
+        else:
+
+            @pl.when(home != z)
+            def _():
+                copy.wait_send()
+
+    def arrive(count):
+        flat = got.at[pl.ds(0, count)]
+        remote(flat, flat, send2.at[0], recv2, (z, e)).wait_recv()
+
+    @pl.when(home == z)
+    def _():
+        arrive(nz * per - 1)
+
+    @pl.when(home != z)
+    def _():
+        arrive(nz * per)
+
+    for i in range(per):
+        out_ref[i] = sum(far[k, i] for k in range(nz))
+
+
+def reduce_columns(x, nz, ne, cid):
+    rows, width = x.shape
+    per = ne // nz
+    x = x.reshape(rows, ne, width // ne).transpose(1, 0, 2)
+    out = pl.pallas_call(
+        functools.partial(reduce_kernel, nz, ne),
+        out_shape=jax.ShapeDtypeStruct((per, rows, width // ne), F32),
+        in_specs=[VMEM],
+        out_specs=VMEM,
+        scratch_shapes=[
+            pltpu.VMEM((ne, rows, width // ne), F32),
+            pltpu.VMEM((rows, width // ne), F32),
+            pltpu.VMEM((nz, per, rows, width // ne), F32),
+            DMA((ne,)), DMA((ne,)), DMA((ne,)), DMA,
+        ],
+        compiler_params=pltpu.CompilerParams(collective_id=cid, has_side_effects=True),
+        name="reduce_columns",
+    )(x)
+    return out.transpose(1, 0, 2).reshape(rows, per * (width // ne))
 
 
 def start_kernel(
-    nz, ne, x_ref, wqkv_ref, wout_ref, small_ref, seg_ref,
-    out_ref, wq_ref, wo_ref, small_out, seg_out,
+    nz, ne, x_ref, wqkv_ref, wout_ref, small_ref, seg_ref, _,
+    out_ref, wq_ref, wo_ref, small_out, seg_out, _2,
     wbuf, pbuf, zsend, zrecv, send, recv, local,
     up_send, up_recv, dn_send, dn_recv, wload, wkeep, pload, psend, precv, pkeep,
     small_send, small_recv, seg_send, seg_recv,
@@ -574,7 +610,7 @@
     wait_all(seg_out, seg_send, seg_recv, ne - 1)
 
 
-def start_gather(x, w_qkv, w_out, small, seg, nz, ne, hw, cid):
+def start_gather(x, w_qkv, w_out, small, seg, after, nz, ne, hw, cid):
     kinds, depth, width = w_qkv.shape
     per = ne // nz
     return pl.pallas_call(
@@ -585,9 +621,11 @@
             jax.ShapeDtypeStruct((hw, width), BF),
             jax.ShapeDtypeStruct((nz, *small.shape), small.dtype),
             jax.ShapeDtypeStruct((ne, *seg.shape), seg.dtype),
+            jax.ShapeDtypeStruct(after.shape, after.dtype),
         ],
-        in_specs=[VMEM, ANY, ANY, VMEM, VMEM],
-        out_specs=[ANY, ANY, ANY, VMEM, VMEM],
+        in_specs=[VMEM, ANY, ANY, VMEM, VMEM, ANY],
+        out_specs=[ANY, ANY, ANY, VMEM, VMEM, ANY],
+        input_output_aliases={5: 5},
         scratch_shapes=[
             pltpu.VMEM((kinds, depth, hw), BF),
             pltpu.VMEM((per, hw, hw), BF),
@@ -598,7 +636,42 @@
         ],
         compiler_params=pltpu.CompilerParams(collective_id=cid, has_side_effects=True),
         name="start_gather",
-    )(x, w_qkv, w_out, small, seg)
+    )(x, w_qkv, w_out, small, seg, after)
+
+
+def swap_kernel(ne, x_ref, out_ref, send, recv):
+    z, e = lax.axis_index("dp"), lax.axis_index("expert")
+    hw = x_ref.shape[0]
+    sem = pltpu.get_barrier_semaphore()
+    for r in range(1, ne):
+        to = (z, lax.rem(e + r, ne))
+        pl.semaphore_signal(sem, inc=1, device_id=to, device_id_type=MESH)
+    pl.semaphore_wait(sem, ne - 1)
+    mine = pl.ds(pl.multiple_of(e * hw, hw), hw)
+    copies = []
+    for r in range(1, ne):
+        to = lax.rem(e + r, ne)
+        src = x_ref.at[:, pl.ds(pl.multiple_of(to * hw, hw), hw)]
+        copy = remote(src, out_ref.at[mine, :], send.at[r], recv.at[r], (z, to))
+        copy.start()
+        copies.append(copy)
+    out_ref[mine, :] = x_ref[:, mine]
+    for copy in copies:
+        copy.wait_send()
+        copy.wait_recv()
+
+
+def swap_in_plane(x, ne, cid):
+    hw, width = x.shape
+    return pl.pallas_call(
+        functools.partial(swap_kernel, ne),
+        out_shape=jax.ShapeDtypeStruct((width, hw), x.dtype),
+        in_specs=[VMEM],
+        out_specs=VMEM,
+        scratch_shapes=[DMA((ne,)), DMA((ne,))],
+        compiler_params=pltpu.CompilerParams(collective_id=cid, has_side_effects=True),
+        name="swap_in_plane",
+    )(x)
 
 
 def lay_kernel(kinds, hw, x_ref, *outs):
@@ -649,30 +722,36 @@
 
 
 def moe_kernel(
-    fl, h_ref, g_ref, gate_ref, win_ref, wdt_ref, wd_ref, wint_ref,
-    mix_ref, gh_ref, gg_ref, dwin_ref, dwd_ref, acc_in, acc_d,
+    fl, h_ref, g_ref, win_ref, wdt_ref, wd_ref, wint_ref,
+    mix_ref, gh_ref, dwin_ref, dwd_ref, acc_in, acc_d,
 ):
     step = pl.program_id(0)
-    tile, width = h_ref.shape
-    per_dev = gate_ref.shape[1]
-    h = h_ref[...]
+    tile, width = g_ref.shape
+    per_dev = wd_ref.shape[0] // fl
+    e = lax.axis_index("expert")
+    h = h_ref[:, :width]
     g = g_ref[...]
-    gates = gate_ref[...]
+    extra = h_ref[:, width:].astype(F32)
     pre = dot(h, win_ref[...], NN)
     graw = dot(g, wdt_ref[...], NN)
     scaled_act, grad_gate, grad_up = [], [], []
     lanes = lax.broadcasted_iota(jnp.int32, (tile, 128), 1)
     gg = jnp.zeros((tile, 128), F32)
+    split = 64
     for i in range(per_dev):
         u = pre[:, i * fl : (i + 1) * fl]
         w = pre[:, (per_dev + i) * fl : (per_dev + 1 + i) * fl]
         gr = graw[:, i * fl : (i + 1) * fl]
-        gate = gates[:, i : i + 1]
+        mine = e * per_dev + i
+        picked = (lanes == mine) | (lanes == mine + split)
+        gate = jnp.sum(jnp.where(picked, extra, 0.0), axis=-1, keepdims=True)
         sig = 1.0 / (1.0 + jnp.exp(-u))
         silu = u * sig
         act = silu * w
         total = jnp.sum(act.astype(BF).astype(F32) * gr, axis=-1, keepdims=True)
-        gg = jnp.where(lanes == i, total, gg)
+        rounded = total.astype(BF).astype(F32)
+        gg = jnp.where(lanes == mine, rounded, gg)
+        gg = jnp.where(lanes == mine + split, total - rounded, gg)
         scaled_act.append((gate * act).astype(BF))
         gact = gate * gr
         grad_gate.append((gact * w * (sig * (1.0 + u * (1.0 - sig)))).astype(BF))
@@ -681,10 +760,8 @@
     gin = jnp.concatenate(grad_gate + grad_up, axis=1)
     blocks, rows = mix_ref.shape[0], mix_ref.shape[2]
     mix_ref[...] = dot(a, wd_ref[...], NN).astype(BF).reshape(blocks, 1, rows, width)
-    gh_ref[...] = dot(gin, wint_ref[...], NN).astype(BF)
-    turned = gg.T[:8]
-    for i in range(blocks):
-        gg_ref[i] = turned[:, i * rows : (i + 1) * rows]
+    gh_ref[:, :width] = dot(gin, wint_ref[...], NN).astype(BF)
+    gh_ref[:, width:] = gg.astype(BF)
 
     @pl.when(step == 0)
     def _():
@@ -700,11 +777,11 @@
         dwd_ref[...] = acc_d[...]
 
 
-def moe(h_all, g_all, gates2, w_in, wd_t, wd, w_in_t, nz, ne, rows_dev, blocks):
-    count, width = h_all.shape
+def moe(h_all, g_all, w_in, wd_t, wd, w_in_t, per_dev, nz, ne, rows_dev, blocks):
+    count, width = g_all.shape
+    wide = h_all.shape[1]
     hid4 = w_in.shape[1]
     hid2 = wd.shape[0]
-    per_dev = gates2.shape[1]
     fl = hid2 // per_dev
     tile = blocks * rows_dev
     turns = ne // blocks
@@ -714,19 +791,17 @@
         functools.partial(moe_kernel, fl),
         grid=(count // tile,),
         in_specs=[
-            rows(width), rows(width), rows(per_dev),
+            rows(wide), rows(width),
             whole(w_in.shape), whole(wd_t.shape), whole(wd.shape), whole(w_in_t.shape),
         ],
         out_specs=[
             pl.BlockSpec((blocks, 1, rows_dev, width), lambda i: (i % turns, i // turns, 0, 0)),
-            rows(width),
-            pl.BlockSpec((blocks, 8, rows_dev), lambda i: (i, 0, 0)),
+            rows(wide),
             whole((width, hid4)), whole((hid2, width)),
         ],
         out_shape=[
             jax.ShapeDtypeStruct((ne, nz, rows_dev, width), BF),
-            jax.ShapeDtypeStruct((count, width), BF),
-            jax.ShapeDtypeStruct((nz * ne, 8, rows_dev), F32),
+            jax.ShapeDtypeStruct((count, wide), BF),
             jax.ShapeDtypeStruct((width, hid4), BF),
             jax.ShapeDtypeStruct((hid2, width), F32),
         ],
@@ -738,7 +813,7 @@
             transcendentals=count * hid2,
         ),
         name="moe",
-    )(h_all, g_all, gates2, w_in, wd_t, wd, w_in_t)
+    )(h_all, g_all, w_in, wd_t, wd, w_in_t)
 
 
 def body(inputs, segments, routes, w_qkv, w_out, w_router, gains, w_gate, w_up, w_down, cotangent):
@@ -761,8 +836,8 @@
         [w_router.T, gains.T, jnp.zeros((pad, gains.shape[0]), BF)], axis=0
     )
     seg8 = jnp.broadcast_to(segments[:, None, :], (num_seqs, 8, length)).reshape(-1, length)
-    in_all, wq, wo, small, seg_all = start_gather(
-        inputs, w_qkv.transpose(1, 0, 2), w_out, small, seg8, nz, ne, hw, 0
+    in_all, wq, wo, small, seg_all, cot = start_gather(
+        inputs, w_qkv.transpose(1, 0, 2), w_out, small, seg8, cotangent, nz, ne, hw, 0
     )
     small = small.transpose(1, 0, 2).reshape(-1, width)
     router_t = small[:expert_count]
@@ -770,7 +845,6 @@
     my_gains = lax.dynamic_slice_in_dim(gain_mat, e * hw, hw, axis=1)
     seg_all = seg_all.reshape(ne * num_seqs, 8, length)[:, 0]
 
-    cot, _ = lax.optimization_barrier((cotangent, small))
     g_all = lax.all_gather(cot, both, axis=0, tiled=True)
     in_all = in_all.reshape(ne * count, width).astype(F32)
     h1_all = (in_all * rms_scale(in_all) * gain_mat[0]).astype(BF)
@@ -801,10 +875,13 @@
     )
     gates = picks * probs
 
-    h2_all, gates_all = gather_tokens(h2, nz, ne, True, 2, small=gates.T)
-    h2_all = h2_all.reshape(-1, width)
-    gates2 = lax.dynamic_slice_in_dim(gates_all, e * per_dev, per_dev, axis=1)
-    gates2 = gates2.transpose(0, 2, 1).reshape(-1, per_dev)
+    split = 64
+    high = gates.astype(BF)
+    low = (gates - high.astype(F32)).astype(BF)
+    blank = jnp.zeros((count, split - expert_count), BF)
+    h2_all = gather_tokens(
+        jnp.concatenate([h2, high, blank, low, blank], axis=1), nz, ne, True, 2
+    ).reshape(-1, width + 2 * split)
     wg = lax.dynamic_slice_in_dim(w_gate, z * fl, fl, axis=2)
     wu = lax.dynamic_slice_in_dim(w_up, z * fl, fl, axis=2)
     wd = lax.dynamic_slice_in_dim(w_down, z * fl, fl, axis=1)
@@ -813,21 +890,26 @@
     ).reshape(2 * per_dev * fl, width)
     w_in = jnp.concatenate([wg[0], wg[1], wu[0], wu[1]], axis=1)
     wd = wd.reshape(per_dev * fl, width)
-    mix, gh, gg, dwin, dwd = moe(
-        h2_all, g_all, gates2, w_in, wd.T, wd, w_in_t, nz, ne, count, min(4, ne)
-    )
-    grad_from_experts, gg = scatter_tokens(
-        gh.reshape(nz * ne, count, width), nz, ne, True, 3, small=gg
-    )
-    grad_gates = jnp.sum(gg.reshape(nz, ne, 8, count), axis=0)[:, :per_dev]
-    grad_gates = grad_gates.reshape(expert_count, count).T
-
-    mix = lax.psum_scatter(mix.reshape(-1, width), "expert", scatter_dimension=0, tiled=True)
+    mix, gh, dwin, dwd = moe(
+        h2_all, g_all, w_in, wd.T, wd, w_in_t, per_dev, nz, ne, count, min(4, ne)
+    )
+    gh_sum, mix = scatter_tokens(
+        gh.reshape(nz * ne, count, width + 2 * split), nz, ne, True, 3,
+        after=mix.reshape(-1, width),
+    )
+    grad_from_experts = gh_sum[:, :width]
+    grad_gates = (
+        gh_sum[:, width : width + expert_count]
+        + gh_sum[:, width + split : width + split + expert_count]
+    )
+
+    mix = lax.psum_scatter(mix, "expert", scatter_dimension=0, tiled=True)
     mix = lax.psum_scatter(mix, "dp", scatter_dimension=0, tiled=True)
     output = (x1 + mix.astype(F32)).astype(BF)
 
     dwin = lax.all_to_all(
-        dwin.reshape(nz, width // nz, 2 * per_dev * fl), "dp", split_axis=0, concat_axis=0, tiled=True
+        dwin.reshape(nz, width // nz, 2 * per_dev * fl),
+        "dp", split_axis=0, concat_axis=0, tiled=True,
     )
     grad_w_gate, grad_w_up = lay_experts(dwin, per_dev, fl)
     grad_w_down = dwd.reshape(per_dev, fl, width)
@@ -835,13 +917,13 @@
     grad_top = cotangent.astype(F32)
     grad_probs = picks * grad_gates
     glog = (probs * (grad_probs - jnp.sum(probs * grad_probs, axis=-1, keepdims=True))).astype(BF)
-    local_router = dot(h2, glog, TN)
+    local_router = dot(glog, h2, TN)
     gh2 = grad_from_experts + dot(glog, router_t, NN)
     grad_ffn, gain_ffn = rms_backward(x1, a2, gain_mat[3], gh2)
     gx1 = grad_top + grad_ffn
     gab = gx1.astype(BF)
 
-    gab_all = gather_tokens(gab, nz, ne, False, 4)[0].reshape(-1, width)
+    gab_all = gather_tokens(gab, nz, ne, False, 4).reshape(-1, width)
     go = dot(gab_all, wo, NT).astype(BF).reshape(shape_heads)
     grad_q, grad_k, gv = jax.vmap(attend_backward)(rq, rk, vb, seg_all, lse, go)
     gqn = rotate(grad_q, cos_tab, -sin_tab).reshape(plane, hw)
@@ -861,31 +943,28 @@
     grad_inputs = (gx1 + grad_front).astype(BF)
 
     part_out = dot(o, gab_all, TN).astype(BF)
-    part_out = lax.all_to_all(
-        part_out.reshape(hw, ne, hw).transpose(1, 0, 2),
-        "expert", split_axis=0, concat_axis=0, tiled=True,
-    ).reshape(width, hw)
+    part_out = swap_in_plane(part_out, ne, 8)
     parts = [dot(h1_all, part, TN).astype(BF) for part in gproj] + [part_out]
     mine = lax.psum_scatter(
         jnp.concatenate(parts, axis=1), "dp", scatter_dimension=0, tiled=True
     )
-    wide = gather_tokens(mine, nz, ne, False, 6)[0]
+    wide = gather_tokens(mine, nz, ne, False, 6)
     grad_w_qkv, grad_w_out = lay_mixer(wide, 4, hw)
     grad_w_qkv = grad_w_qkv.transpose(1, 0, 2)
 
     place = lambda part: lax.dynamic_update_slice_in_dim(
-        jnp.zeros((width,), F32), part, e * hw, axis=0
+        jnp.zeros((1, width), F32), part[None], e * hw, axis=1
     )
     tiny = jnp.concatenate(
         [
-            local_router,
-            jnp.stack([gain_attn, place(gain_q), place(gain_k), gain_ffn], axis=1),
+            local_router, gain_attn[None], place(gain_q), place(gain_k), gain_ffn[None],
+            jnp.zeros((-(expert_count + 4) % 8, width), F32),
         ],
-        axis=1,
-    )
-    tiny = lax.psum(tiny, both)
-    tiny = lax.dynamic_slice_in_dim(tiny, z * (width // nz), width // nz, axis=0)
-    grad_w_router, grad_gains = tiny[:, :expert_count], tiny[:, expert_count:]
+        axis=0,
+    )
+    tiny = reduce_columns(tiny, nz, ne, 7)
+    grad_w_router = tiny[:expert_count].T
+    grad_gains = tiny[expert_count : expert_count + 4].T
     return (
         output,
         grad_inputs,

time: 1090 us -> 886 us (0.81)
  waiting for transfers between devices: 249 us -> 0.57 us
  Pallas kernels: 638 us -> 692 us
    psum x1 -> x0, waiting for transfers between devices: 176 us -> none  [body(): tiny = lax.psum(tiny, both)]
    pallas_call x6 -> x8, Pallas kernels: 365 us -> 495 us  [the longest x3 199 us: gather_tokens(): pl.pallas_call(functools.partial(gather_kernel, nz, ne, spread), out_shap...]
    pallas_call x1, Pallas kernels: 159 us -> 84.6 us  [start_gather(): pl.pallas_call(functools.partial(start_kernel, nz, ne), out_shape=[jax.Sh...]
    reduce_scatter x1, waiting for transfers between devices: 71.9 us -> 0.01 us  [body(): lax.psum_scatter(jnp.concatenate(parts, axis=1), 'dp', scatter_dimension=...]
  transfers between devices with their start and end apart: 7 -> 5, of which waited for: 3 -> 0; matrix products, arithmetic and copies ran while one was open for 13% -> 14% of each run, Pallas kernels for 50% -> 48%
where the time goes in v3:
time: 886 us; the launch traced here: 880 us
  Pallas kernels  692 us (78%)
  matrix products  47.8 us (5%)
  local copies, waits for them, and re-layouts  45.5 us (5%)
  other arithmetic  44.9 us (5%)
  blocking collectives  29.1 us (3%)
  between operations  14.8 us (2%)
    pallas_call x3, Pallas kernels, gather_tokens(): pl.pallas_call(functools.partial(gather_kernel, nz, ne, spread), out_shap...  199 us
    pallas_call x3, Pallas kernels, scatter_tokens(): pl.pallas_call(functools.partial(scatter_kernel, nz, ne, spread), out_sha...  143 us
    pallas_call x1, Pallas kernels, reduce_columns(): pl.pallas_call(functools.partial(reduce_kernel, nz, ne), out_shape=jax.Sh...  126 us
    pallas_call x1, Pallas kernels, moe(): pl.pallas_call(functools.partial(moe_kernel, fl), grid=(count // tile,),...  96.2 us
    pallas_call x1, Pallas kernels, start_gather(): pl.pallas_call(functools.partial(start_kernel, nz, ne), out_shape=[jax.Sh...  84.6 us
    dot_general x15, matrix products, dot(): return lax.dot_general(a, b, (dims, ((), ())), preferred_element_type=F32)  35.4 us
    pallas_call x1, Pallas kernels, swap_in_plane(): pl.pallas_call(functools.partial(swap_kernel, ne), out_shape=jax.ShapeDty...  26.1 us
  transfers between devices with their start and end apart: 5, of which 0 were waited for; matrix products, arithmetic and copies ran while one was open for 14% of the time, Pallas kernels for 48%

profile of v3, /device:TPU:0, one launch (start us, length us, event | category | flops | bytes accessed | tf_op | source)
XLA Modules:
  0.0 879.8 jit_solution(1389774053055130202)
XLA Ops:
  11.9 84.6 %start_gather.1 = (bf16[8,128,2048]{2,1,0:T(8,128)(2,1)}, bf16[3,2048,256]{2,1,0:T(8,128)(2,1)}, bf16[256,2048]{1,0:T(8,128)(2,1)}, bf16[4,32,512]{2,1,0:T(8,128...) custom-call(bf16[128,2048]{1,0:T(8,128)(2,1)} %x_ref.1, ...), custom_call_target="tpu_custom_call", output_to_operand_aliasing={{5}: (5, {})} | custom-call | tf_op jit(solution)/shard_map/start_gather/pallas_call | solution.py:616
  105.2 12.9 %psum.14 = f32[2,1024]{1,0:T(2,128)S(1)} all-reduce(f32[2,1024]{1,0:T(2,128)S(1)} %pad_maximum_fusion.11), channel_id=1, replica_groups=mesh['dp'=4,'expert'=8] {'expert'}, use_global_device_ids=true, to_apply=%region_3.0 | all-reduce | flops 2048 | bytes 16384 | tf_op jit(solution)/shard_map/psum | solution.py:858
  124.4 5.1 convolution_convert_fusion.8
  140.0 30.4 %scatter_tokens.3 = f32[128,2048]{1,0:T(8,128)} custom-call(bf16[8,128,2048]{2,1,0:T(8,128)(2,1)} %bitcast.185), custom_call_target="tpu_custom_call" | custom-call | tf_op jit(solution)/shard_map/scatter_tokens/pallas_call | solution.py:350
  175.4 134.3 %gather_tokens.3 = bf16[32,128,2176]{2,1,0:T(8,128)(2,1)} custom-call(bf16[128,2176]{1,0:T(8,128)(2,1)} %concatenate.46.x_ref), custom_call_target="tpu_custom_call" | custom-call | tf_op jit(solution)/shard_map/gather_tokens/pallas_call | solution.py:236
  314.6 6.2 copy.119
  330.1 96.2 %moe.1 = (bf16[8,4,128,2048]{3,2,1,0:T(8,128)(2,1)}, bf16[4096,2176]{1,0:T(8,128)(2,1)}, bf16[2048,1024]{1,0:T(8,128)(2,1)}, f32[512,2048]{1,0:T(8,128)}) custom-call(bf16[4096,2176]{1,0:T(8,128)(2,1)} %bitcast.186, bf16[4096,2048]{1,0:T(8,128)(2,1)} %all-gather.2.cloned.1.call-done.g_ref, bf16[2048,1024]{1,0:T(8,128)(2,1)} %pad_maximum_fusion.win_ref, ...), custom_call_target="tpu_custom_call" | custom-call | flops 77309411328 | bytes 117440512 | tf_op jit(solution)/shard_map/moe/pallas_call | solution.py:790
  426.3 86.3 %scatter_tokens.4 = (bf16[4096,2048]{1,0:T(8,128)(2,1)}, f32[128,2176]{1,0:T(8,128)}) custom-call(bf16[32,128,2176]{2,1,0:T(8,128)(2,1)} %bitcast.187, bf16[4096,2048]{1,0:T(8,128)(2,1)} %bitcast.184), custom_call_target="tpu_custom_call", output_to_operand_aliasing={{0}: (1, {})} | custom-call | tf_op jit(solution)/shard_map/scatter_tokens/pallas_call | solution.py:350
  513.1 5.4 fusion.2
  521.5 22.9 %gather_tokens.4 = bf16[8,128,2048]{2,1,0:T(8,128)(2,1)} custom-call(bf16[128,2048]{1,0:T(8,128)(2,1)} %fusion.75.x_ref), custom_call_target="tpu_custom_call" | custom-call | tf_op jit(solution)/shard_map/gather_tokens/pallas_call | solution.py:236
  544.4 4.7 convolution_convert_fusion.7
  558.0 3.7 convolution_bitcast_fusion.1
  561.7 3.7 convolution_bitcast_fusion
  565.4 4.5 multiply_subtract_fusion
  574.8 4.5 convolution_convert_fusion.1.x_ref
  579.3 26.1 %swap_in_plane.1 = bf16[2048,256]{1,0:T(8,128)(2,1)} custom-call(bf16[256,2048]{1,0:T(8,128)(2,1)} %convolution_convert_fusion.1.x_ref), custom_call_target="tpu_custom_call" | custom-call | tf_op jit(solution)/shard_map/swap_in_plane/pallas_call | solution.py:666
  609.1 16.1 %psum.15 = f32[2,1024]{1,0:T(2,128)S(1)} all-reduce(f32[2,1024]{1,0:T(2,128)S(1)} %pad_maximum_fusion.12), channel_id=1, replica_groups=mesh['dp'=4,'expert'=8] {'expert'}, use_global_device_ids=true, to_apply=%region_18.19 | all-reduce | flops 2048 | bytes 16384 | tf_op jit(solution)/shard_map/psum | solution.py:934
  637.3 4.9 all-to-all-start
  647.9 5.0 add_convert_fusion
  652.9 26.1 %scatter_tokens.5 = f32[128,2048]{1,0:T(8,128)} custom-call(bf16[8,128,2048]{2,1,0:T(8,128)(2,1)} %bitcast.188), custom_call_target="tpu_custom_call" | custom-call | tf_op jit(solution)/shard_map/scatter_tokens/pallas_call | solution.py:350
  682.4 126.4 %reduce_columns.1 = f32[2,24,256]{2,1,0:T(8,128)} custom-call(f32[8,24,256]{2,1,0:T(8,128)} %bitcast.210), custom_call_target="tpu_custom_call" | custom-call | tf_op jit(solution)/shard_map/reduce_columns/pallas_call | solution.py:437
  811.5 5.9 lay_experts.1
  817.4 42.4 %gather_tokens.5.x_ref = bf16[8,512,1024]{2,1,0:T(8,128)(2,1)} custom-call(bf16[512,1024]{1,0:T(8,128)(2,1)} %reduce-scatter.8.cloned.1.call-done.x_ref), custom_call_target="tpu_custom_call" | custom-call | tf_op jit(solution)/shard_map/gather_tokens/pallas_call | solution.py:236
  859.8 10.3 %lay_mixer.1 = (f32[3,512,2048]{2,1,0:T(8,128)}, f32[512,2048]{1,0:T(8,128)}) custom-call(bf16[8,512,1024]{2,1,0:T(8,128)(2,1)} %gather_tokens.5.x_ref), custom_call_target="tpu_custom_call" | custom-call | tf_op jit(solution)/shard_map/lay_mixer/pallas_call | solution.py:688
  (193 shorter events, 96.7 us)
Async XLA Ops:
  7.2 323.0 %all-gather.2.cloned.1.call-start = ((), (), s32[]{:S(2)}) async-start(), calls=%async_computation.4 | async-start | bytes 17301504 | tf_op jit(solution)/shard_map/all_gather | solution.py:848
  96.5 545.8 %reduce-scatter.4.cloned.1.call-start = ((), (), s32[]{:S(2)}) async-start(), calls=%async_computation.5 | async-start | bytes 18874368 | tf_op jit(solution)/shard_map/reduce_scatter | solution.py:906
  103.8 14.4 %copy-start.7 = (f32[1024,256]{0,1:T(8,128)}, f32[1024,256]{0,1:T(8,128)S(1)}, u32[]{:S(2)}) copy-start(f32[1024,256]{0,1:T(8,128)S(1)} %get-tuple-element.90) | copy-start | bytes 3145732
  105.1 15.3 %copy-start.5 = (f32[1024,256]{0,1:T(8,128)}, f32[1024,256]{0,1:T(8,128)S(1)}, u32[]{:S(2)}) copy-start(f32[1024,256]{0,1:T(8,128)S(1)} %get-tuple-element.92) | copy-start | bytes 3145732
  124.4 6.8 copy-start.16
  140.0 30.4 %copy-start.35 = (bf16[4,32,512]{2,1,0:T(8,128)(2,1)S(1)}, bf16[4,32,512]{2,1,0:T(8,128)(2,1)}, u32[]{:S(2)}) copy-start(bf16[4,32,512]{2,1,0:T(8,128)(2,1)} %get-tuple-element.26) | copy-start | bytes 393220
  140.0 30.4 %copy-start.13 = (bf16[128,2048]{1,0:T(8,128)(2,1)S(1)}, bf16[128,2048]{1,0:T(8,128)(2,1)}, u32[]{:S(2)}) copy-start(bf16[128,2048]{1,0:T(8,128)(2,1)} %x_ref.1) | copy-start | bytes 1572868
  140.0 34.0 %copy-start.38 = (s32[128,8]{0,1:T(8,128)S(1)}, s32[128,8]{0,1:T(8,128)}, u32[]{:S(2)}) copy-start(s32[128,8]{0,1:T(8,128)} %param.13) | copy-start | bytes 12292
  173.6 136.1 %copy-start.10 = (bf16[128,2048]{1,0:T(8,128)(2,1)}, bf16[128,2048]{1,0:T(8,128)(2,1)S(1)}, u32[]{:S(2)}) copy-start(bf16[128,2048]{1,0:T(8,128)(2,1)S(1)} %multiply_convert_fusion.3) | copy-start | bytes 1572868
  322.5 5.3 copy-start.12
  512.6 304.8 %reduce-scatter.8.cloned.1.call-start = ((), (), s32[]{:S(2)}) async-start(), calls=%async_computation.7 | async-start | bytes 5242880 | tf_op jit(solution)/shard_map/reduce_scatter | solution.py:948
  513.1 5.4 copy-start.31
  513.1 5.8 copy-start.2
  513.1 7.3 copy-start.15
  544.4 8.6 copy-start.4
  574.8 30.6 %copy-start.6 = (f32[1024,256]{0,1:T(8,128)S(1)}, f32[1024,256]{0,1:T(8,128)}, u32[]{:S(2)}) copy-start(f32[1024,256]{0,1:T(8,128)} %copy-done.5) | copy-start | bytes 3145732
  574.8 32.3 %copy-start.34 = (f32[1,1024]{1,0:T(1,128)S(1)}, f32[1,1024]{1,0:T(1,128)}, u32[]{:S(2)}) copy-start(f32[1,1024]{1,0:T(1,128)} %copy-done.33) | copy-start | bytes 12292
  574.8 32.3 %copy-start.37 = (f32[1,256]{1,0:T(1,128)S(1)}, f32[1,256]{1,0:T(1,128)}, u32[]{:S(2)}) copy-start(f32[1,256]{1,0:T(1,128)} %copy-done.36) | copy-start | bytes 3076
  637.3 5.5 copy-start.39
  637.3 174.2 %all-to-all-start = ((bf16[4,512,1024]{2,1,0:T(8,128)(2,1)}), bf16[4,512,1024]{2,1,0:T(8,128)(2,1)}, u32[]{:S(2)}, u32[]{:S(2)}) async-start(bf16[4,512,1024]{2,1,0:T(8,128)(2,1)} %bitcast.202), calls=%async_computation.3 | async-start | bytes 8388608 | tf_op jit(solution)/shard_map/all_to_all | solution.py:910
  642.2 227.9 %reduce-scatter.6.cloned.1.call-start = ((), (), s32[]{:S(2)}) async-start(), calls=%async_computation.6 | async-start | bytes 2621440 | tf_op jit(solution)/shard_map/reduce_scatter | solution.py:907
  652.9 26.1 %copy-start.11 = (bf16[128,2048]{1,0:T(8,128)(2,1)S(1)}, bf16[128,2048]{1,0:T(8,128)(2,1)}, u32[]{:S(2)}) copy-start(bf16[128,2048]{1,0:T(8,128)(2,1)} %copy-done.10) | copy-start | bytes 1572868
  652.9 26.4 %copy-start.14 = (bf16[128,2048]{1,0:T(8,128)(2,1)S(1)}, bf16[128,2048]{1,0:T(8,128)(2,1)}, u32[]{:S(2)}) copy-start(bf16[128,2048]{1,0:T(8,128)(2,1)} %x_ref.1) | copy-start | bytes 1572868
  859.8 10.3 %copy-start.8 = (f32[128,2048]{1,0:T(8,128)S(1)}, f32[128,2048]{1,0:T(8,128)}, u32[]{:S(2)}) copy-start(f32[128,2048]{1,0:T(8,128)} %scatter_tokens.5) | copy-start | bytes 3145732
  (21 other events, 46.6 us)
Sparse Core Ops, SparseCore 0:
  96.6 156.1 all-gather.1
  512.7 127.0 reduce-scatter.3
  642.7 138.1 reduce-scatter.7
  783.0 64.2 reduce-scatter.5

commit v4 on v3

--- a/solution.py
+++ b/solution.py
@@ -722,7 +722,7 @@
 
 
 def moe_kernel(
-    fl, h_ref, g_ref, win_ref, wdt_ref, wd_ref, wint_ref,
+    fl, h_ref, g_ref, win_ref, wd_ref,
     mix_ref, gh_ref, dwin_ref, dwd_ref, acc_in, acc_d,
 ):
     step = pl.program_id(0)
@@ -733,7 +733,7 @@
     g = g_ref[...]
     extra = h_ref[:, width:].astype(F32)
     pre = dot(h, win_ref[...], NN)
-    graw = dot(g, wdt_ref[...], NN)
+    graw = dot(g, wd_ref[...], NT)
     scaled_act, grad_gate, grad_up = [], [], []
     lanes = lax.broadcasted_iota(jnp.int32, (tile, 128), 1)
     gg = jnp.zeros((tile, 128), F32)
@@ -760,7 +760,7 @@
     gin = jnp.concatenate(grad_gate + grad_up, axis=1)
     blocks, rows = mix_ref.shape[0], mix_ref.shape[2]
     mix_ref[...] = dot(a, wd_ref[...], NN).astype(BF).reshape(blocks, 1, rows, width)
-    gh_ref[:, :width] = dot(gin, wint_ref[...], NN).astype(BF)
+    gh_ref[:, :width] = dot(gin, win_ref[...], NT).astype(BF)
     gh_ref[:, width:] = gg.astype(BF)
 
     @pl.when(step == 0)
@@ -777,7 +777,7 @@
         dwd_ref[...] = acc_d[...]
 
 
-def moe(h_all, g_all, w_in, wd_t, wd, w_in_t, per_dev, nz, ne, rows_dev, blocks):
+def moe(h_all, g_all, w_in, wd, per_dev, nz, ne, rows_dev, blocks):
     count, width = g_all.shape
     wide = h_all.shape[1]
     hid4 = w_in.shape[1]
@@ -792,7 +792,7 @@
         grid=(count // tile,),
         in_specs=[
             rows(wide), rows(width),
-            whole(w_in.shape), whole(wd_t.shape), whole(wd.shape), whole(w_in_t.shape),
+            whole(w_in.shape), whole(wd.shape),
         ],
         out_specs=[
             pl.BlockSpec((blocks, 1, rows_dev, width), lambda i: (i % turns, i // turns, 0, 0)),
@@ -813,7 +813,409 @@
             transcendentals=count * hid2,
         ),
         name="moe",
-    )(h_all, g_all, w_in, wd_t, wd, w_in_t)
+    )(h_all, g_all, w_in, wd)
+
+
+def moe_net_kernel(
+    nz, ne, per_dev, slots, h_ref, g_ref, wg_ref, wu_ref, wd_ref,
+    hall_ref, mix_ref, gh_ref, dwin_ref, dwd_ref,
+    win, wd, acc_in, acc_d, htile, gtile, mixbuf, qbuf, cgot, acc, got, zgot, dbuf,
+    wload, tload, mixsem, keep, flush, zsend, zrecv, send, recv,
+    csend, crecv, credit, rsend, rrecv, ysend, yrecv,
+):
+    z, e = lax.axis_index("dp"), lax.axis_index("expert")
+    rows, width = g_ref.shape[1], g_ref.shape[2]
+    half = rows // 2
+    fl = wd.shape[0] // per_dev
+    upper = [2 << b for b in range(ne.bit_length() - 2)]
+    stages = len(upper)
+    pairs = ne // 2
+    steps = nz * pairs
+    gather_orders = [upper + [1], upper[::-1] + [1]]
+    sum_orders = [[1] + upper, [1] + upper[::-1]]
+    at = [e]
+    for bit in [1] + upper:
+        at = at + [flip(i, bit) for i in at]
+    partner = (z, at[1])
+
+    def plane(r):
+        low = jnp.minimum(z, nz - 1 - z)
+        near = jnp.where(lax.rem(r, 2) == 1, z - (r + 1) // 2, z + r // 2)
+        far = jnp.where(2 * z < nz, z + (r - low), z - (r - low))
+        return jnp.where(r <= 2 * low, near, far)
+
+    planes = [z] + [nearest(z, r, nz) for r in range(1, nz)]
+
+    def part(s):
+        return pl.ds(s * half, half)
+
+    def subset_mask(order, subset):
+        return sum(bit for b, bit in enumerate(order) if subset >> b & 1)
+
+    def pass_on(r, s, stage, subset, own=False):
+        order = gather_orders[s]
+        dst = hall_ref.at[plane(r) * ne + at[subset_mask(order, subset)], part(s)]
+        n = (1 << stage) - 1 + subset
+        src = h_ref.at[part(s)] if own else dst
+        return remote(src, dst, send.at[r, s, n], recv.at[r, s, n], (z, at[order[stage]]))
+
+    def take(r, s, stage, subset):
+        order = gather_orders[s]
+        mask = subset_mask(order, subset) | order[stage]
+        n = (1 << stage) - 1 + subset
+        here = hall_ref.at[plane(r) * ne + at[mask], part(s)]
+        remote(here, here, send.at[r, s, n], recv.at[r, s, n], partner).wait_recv()
+        for later in range(stage + 1, stages + 1):
+            pass_on(r, s, later, subset + (1 << stage)).start()
+
+    def start_round(r):
+        if r > 0:
+            here = hall_ref.at[planes[r] * ne + e]
+            remote(here, here, zsend.at[r], zrecv.at[planes[r]], partner).wait_recv()
+        for stage in range(stages + 1):
+            for s in range(2):
+                pass_on(r, s, stage, 0, own=r == 0).start()
+
+    def take_pair(r, i):
+        if i == 1:
+            for stage in range(stages):
+                for s in range(2):
+                    take(r, s, stage, 0)
+        mask = 2 * i
+        for s in range(2):
+            order = gather_orders[s]
+            places = [b for b in range(stages) if order[b] & mask]
+            if len(places) > 1:
+                take(r, s, places[-1], sum(1 << b for b in places[:-1]))
+        for s in range(2):
+            order = gather_orders[s]
+            take(r, s, stages, sum(1 << b for b in range(stages) if order[b] & mask))
+
+    def blocks_of(k):
+        r, i = k // pairs, lax.rem(k, pairs)
+        home = plane(r)
+        lane = e
+        for b, bit in enumerate(upper):
+            lane = lane + lax.rem(i // (1 << b), 2) * (at[bit] - e)
+        return home, lane, lane + (at[1] - e)
+
+    def loads(k):
+        home, one, two = blocks_of(k)
+        p = lax.rem(k, 2)
+        out = []
+        for j, lane in enumerate((one, two)):
+            to = pl.ds(j * rows, rows)
+            block = home * ne + lane
+            out.append(pltpu.make_async_copy(hall_ref.at[block], htile.at[p, to], tload.at[p, 2 * j]))
+            out.append(
+                pltpu.make_async_copy(g_ref.at[block], gtile.at[p, to], tload.at[p, 2 * j + 1])
+            )
+        return out
+
+    def mix_out(k):
+        home, one, two = blocks_of(k)
+        p = lax.rem(k, 2)
+        return [
+            pltpu.make_async_copy(
+                mixbuf.at[p, pl.ds(j * rows, rows)], mix_ref.at[lane, home], mixsem.at[p, j]
+            )
+            for j, lane in enumerate((one, two))
+        ]
+
+    def to_partner(k):
+        return remote(
+            qbuf.at[lax.rem(k, 2)], cgot.at[lax.rem(k, slots)],
+            csend.at[lax.rem(k, 2)], crecv.at[lax.rem(k, slots)], partner,
+        )
+
+    def place_of(t, keep_index):
+        return (1 << stages) - (1 << (stages - t + 1)) + keep_index
+
+    def push(r, s, t, keep_index):
+        order = sum_orders[s]
+        mask = order[t] | subset_mask(order[t + 1 :], keep_index)
+        n = place_of(t, keep_index)
+        return remote(
+            acc.at[r, mask // 2, part(s)], got.at[r, s, n],
+            rsend.at[r, s, n], rrecv.at[r, s, n], (z, at[order[t]]),
+        )
+
+    def merge(k):
+        slot = lax.rem(k, slots)
+        remote(cgot.at[slot], cgot.at[slot], csend.at[0], crecv.at[slot], partner).wait_recv()
+        r, i = k // pairs, lax.rem(k, pairs)
+        add_rows(acc.at[r, i], cgot.at[slot])
+
+        @pl.when(k + slots < steps)
+        def _():
+            pl.semaphore_signal(credit, inc=1, device_id=partner, device_id_type=MESH)
+
+        for j in range(1, pairs):
+
+            @pl.when(i == j)
+            def _():
+                for s in range(2):
+                    order = sum_orders[s]
+                    if order[1] & (2 * j):
+                        rest = [b for b, bit in enumerate(order[2:]) if bit & (2 * j)]
+                        push(r, s, 1, sum(1 << b for b in rest)).start()
+
+    def home_copy(r, s):
+        return remote(
+            acc.at[r, 0, part(s)], zgot.at[z, part(s)], ysend.at[r, s], yrecv.at[z, s],
+            (plane(r), e),
+        )
+
+    def settle(r, t):
+        for s in range(2):
+            order = sum_orders[s]
+            for index in range(1 << (stages - t)):
+                copy = push(r, s, t, index)
+                copy.wait_recv()
+                mask = subset_mask(order[t + 1 :], index)
+                add_rows(acc.at[r, mask // 2, part(s)], got.at[r, s, place_of(t, index)])
+            if t < stages:
+                for index in range(1 << (stages - t - 1)):
+                    push(r, s, t + 1, index).start()
+            else:
+
+                @pl.when(r > 0)
+                def _():
+                    home_copy(r, s).start()
+
+    weights = []
+    for i in range(per_dev):
+        cols = pl.ds(z * fl, fl)
+        weights += [
+            (wg_ref.at[i, :, cols], win.at[:, pl.ds(i * fl, fl)]),
+            (wu_ref.at[i, :, cols], win.at[:, pl.ds((per_dev + i) * fl, fl)]),
+            (wd_ref.at[i, cols, :], wd.at[pl.ds(i * fl, fl), :]),
+        ]
+    weights = [
+        pltpu.make_async_copy(src, dst, wload.at[j]) for j, (src, dst) in enumerate(weights)
+    ]
+    for copy in weights:
+        copy.start()
+    meet_column_and_plane(nz, ne, z, e, True)
+    own = pltpu.make_async_copy(h_ref, hall_ref.at[z * ne + e], keep)
+    own.start()
+    for r in range(1, nz):
+        remote(
+            h_ref, hall_ref.at[z * ne + e], zsend.at[r], zrecv.at[z], (planes[r], e)
+        ).start()
+    start_round(0)
+    acc_in[...] = jnp.zeros_like(acc_in)
+    acc_d[...] = jnp.zeros_like(acc_d)
+    take_pair(0, 0)
+    own.wait()
+    for copy in loads(0):
+        copy.start()
+    for copy in weights:
+        copy.wait()
+
+    tile = 2 * rows
+    lanes = lax.broadcasted_iota(jnp.int32, (tile, 128), 1)
+    split = 64
+
+    def step(k, carry):
+        p = lax.rem(k, 2)
+        r, i = k // pairs, lax.rem(k, pairs)
+        for copy in loads(k):
+            copy.wait()
+        pre = dot(htile[p, :, :width], win[...], NN)
+        graw = dot(gtile[p], wd[...], NT)
+        extra = htile[p, :, width:].astype(F32)
+        scaled_act, grad_gate, grad_up = [], [], []
+        gg = jnp.zeros((tile, 128), F32)
+        for j in range(per_dev):
+            u = pre[:, j * fl : (j + 1) * fl]
+            w = pre[:, (per_dev + j) * fl : (per_dev + 1 + j) * fl]
+            gr = graw[:, j * fl : (j + 1) * fl]
+            mine = e * per_dev + j
+            picked = (lanes == mine) | (lanes == mine + split)
+            gate = jnp.sum(jnp.where(picked, extra, 0.0), axis=-1, keepdims=True)
+            sig = 1.0 / (1.0 + jnp.exp(-u))
+            silu = u * sig
+            act = silu * w
+            total = jnp.sum(act.astype(BF).astype(F32) * gr, axis=-1, keepdims=True)
+            rounded = total.astype(BF).astype(F32)
+            gg = jnp.where(lanes == mine, rounded, gg)
+            gg = jnp.where(lanes == mine + split, total - rounded, gg)
+            scaled_act.append((gate * act).astype(BF))
+            gact = gate * gr
+            grad_gate.append((gact * w * (sig * (1.0 + u * (1.0 - sig)))).astype(BF))
+            grad_up.append((gact * silu).astype(BF))
+        a = jnp.concatenate(scaled_act, axis=1)
+        gin = jnp.concatenate(grad_gate + grad_up, axis=1)
+
+        for r1 in range(1, nz):
+
+            @pl.when(k == (r1 - 1) * (pairs - 1) + 1)
+            def _():
+                start_round(r1)
+
+        @pl.when(k + 1 < steps)
+        def _():
+            ahead = k + 1
+            for j in range(pairs):
+
+                @pl.when(lax.rem(ahead, pairs) == j)
+                def _():
+                    take_pair(ahead // pairs, j)
+
+            for copy in loads(ahead):
+                copy.start()
+
+        @pl.when(k >= 2)
+        def _():
+            for copy in mix_out(k - 2):
+                copy.wait()
+            to_partner(k - 2).wait_send()
+
+        mixbuf[p] = dot(a, wd[...], NN).astype(BF)
+        for copy in mix_out(k):
+            copy.start()
+        back = dot(gin, win[...], NT).astype(BF)
+        gg = gg.astype(BF)
+        acc[r, i, :, :width] = back[:rows]
+        acc[r, i, :, width:] = gg[:rows]
+        qbuf[p, :, :width] = back[rows:]
+        qbuf[p, :, width:] = gg[rows:]
+        acc_in[...] += dot(htile[p, :, :width], gin, TN)
+        acc_d[...] += dot(a, gtile[p], TN)
+
+        @pl.when(k >= slots)
+        def _():
+            pl.semaphore_wait(credit, 1)
+
+        to_partner(k).start()
+
+        @pl.when(k >= 1)
+        def _():
+            merge(k - 1)
+
+        for t in range(1, stages + 1):
+            late = k - pairs - 2 * t
+
+            @pl.when((late >= 0) & (lax.rem(late + pairs, pairs) == 0))
+            def _():
+                settle(late // pairs, t)
+
+        return carry
+
+    lax.fori_loop(0, steps, step, 0)
+    merge(steps - 1)
+    final = pltpu.make_async_copy(acc_d, dwd_ref, flush.at[0])
+    final.start()
+    left = sorted(
+        (r * pairs + pairs + 2 * t, r, t)
+        for r in range(nz)
+        for t in range(1, stages + 1)
+        if r * pairs + pairs + 2 * t >= steps
+    )
+    chunk = dbuf.shape[1]
+
+    def flush_chunk(c):
+        return pltpu.make_async_copy(
+            dbuf.at[c % 2], dwin_ref.at[pl.ds(c * chunk, chunk)], flush.at[1 + c % 2]
+        )
+
+    chunks = acc_in.shape[0] // chunk
+    for c in range(chunks):
+        if c >= 2:
+            flush_chunk(c - 2).wait()
+        dbuf[c % 2] = acc_in[pl.ds(c * chunk, chunk), :].astype(BF)
+        flush_chunk(c).start()
+    for _, r, t in left:
+        settle(jnp.int32(r), t)
+    for s in range(2):
+        for r in range(1, nz):
+            here = zgot.at[planes[r], part(s)]
+            remote(here, here, ysend.at[r, s], yrecv.at[planes[r], s], partner).wait_recv()
+
+        def total_rows(n, carry):
+            span = pl.ds(pl.multiple_of(s * half + n * 16, 16), 16)
+            total = acc[0, 0, span, :].astype(F32)
+            for r in range(1, nz):
+                total = total + zgot[planes[r], span, :].astype(F32)
+            gh_ref[span, :] = total
+            return carry
+
+        lax.fori_loop(0, half // 16, total_rows, 0)
+    final.wait()
+    for c in range(max(chunks - 2, 0), chunks):
+        flush_chunk(c).wait()
+    for k in range(max(steps - 2, 0), steps):
+        for copy in mix_out(jnp.int32(k)):
+            copy.wait()
+        to_partner(jnp.int32(k)).wait_send()
+    for r in range(nz):
+        if r > 0:
+            remote(
+                h_ref, hall_ref.at[z * ne + e], zsend.at[r], zrecv.at[z], (planes[r], e)
+            ).wait_send()
+        for s in range(2):
+            for stage in range(stages + 1):
+                for subset in range(1 << stage):
+                    pass_on(r, s, stage, subset, own=r == 0 and subset == 0).wait_send()
+            for t in range(1, stages + 1):
+                for index in range(1 << (stages - t)):
+                    push(r, s, t, index).wait_send()
+            if r > 0:
+                home_copy(jnp.int32(r), s).wait_send()
+
+
+def moe_net_scratch(nz, ne, per_dev, rows, width, wide, fl):
+    pairs = ne // 2
+    slots = 4
+    stages = ne.bit_length() - 2
+    vmem = [
+        ((width, 2 * per_dev * fl), BF),
+        ((per_dev * fl, width), BF),
+        ((width, 2 * per_dev * fl), F32),
+        ((per_dev * fl, width), F32),
+        ((2, 2 * rows, wide), BF),
+        ((2, 2 * rows, width), BF),
+        ((2, 2 * rows, width), BF),
+        ((2, rows, wide), BF),
+        ((slots, rows, wide), BF),
+        ((nz, pairs, rows, wide), BF),
+        ((nz, 2, max(pairs - 1, 1), rows // 2, wide), BF),
+        ((nz, rows, wide), BF),
+        ((2, width // 8, 2 * per_dev * fl), BF),
+    ]
+    size = sum(functools.reduce(lambda a, b: a * b, s) * (2 if d == BF else 4) for s, d in vmem)
+    sems = [
+        DMA((3 * per_dev,)), DMA((2, 4)), DMA((2, 2)), DMA, DMA((3,)),
+        DMA((nz,)), DMA((nz,)), DMA((nz, 2, ne - 1)), DMA((nz, 2, ne - 1)),
+        DMA((2,)), DMA((slots,)), pltpu.SemaphoreType.REGULAR,
+        DMA((nz, 2, max(pairs - 1, 1))), DMA((nz, 2, max(pairs - 1, 1))),
+        DMA((nz, 2)), DMA((nz, 2)),
+    ]
+    fits = size <= 54_000_000 and stages >= 1 and nz > 1 and nz * pairs > slots
+    return fits, slots, [pltpu.VMEM(*v) for v in vmem] + sems
+
+
+def moe_net(h, g_all, w_gate, w_up, w_down, nz, ne, fl, slots, scratch, cid):
+    rows, wide = h.shape
+    per_dev, width, _ = w_gate.shape
+    return pl.pallas_call(
+        functools.partial(moe_net_kernel, nz, ne, per_dev, slots),
+        out_shape=[
+            jax.ShapeDtypeStruct((nz * ne, rows, wide), BF),
+            jax.ShapeDtypeStruct((ne, nz, rows, width), BF),
+            jax.ShapeDtypeStruct((rows, wide), F32),
+            jax.ShapeDtypeStruct((width, 2 * per_dev * fl), BF),
+            jax.ShapeDtypeStruct((per_dev * fl, width), F32),
+        ],
+        in_specs=[VMEM, ANY, ANY, ANY, ANY],
+        out_specs=[ANY, ANY, VMEM, ANY, ANY],
+        scratch_shapes=scratch,
+        compiler_params=pltpu.CompilerParams(
+            collective_id=cid, has_side_effects=True, vmem_limit_bytes=66_500_000
+        ),
+        name="moe_net",
+    )(h, g_all.reshape(nz * ne, rows, width), w_gate, w_up, w_down)
 
 
 def body(inputs, segments, routes, w_qkv, w_out, w_router, gains, w_gate, w_up, w_down, cotangent):
@@ -879,24 +1281,26 @@
     high = gates.astype(BF)
     low = (gates - high.astype(F32)).astype(BF)
     blank = jnp.zeros((count, split - expert_count), BF)
-    h2_all = gather_tokens(
-        jnp.concatenate([h2, high, blank, low, blank], axis=1), nz, ne, True, 2
-    ).reshape(-1, width + 2 * split)
-    wg = lax.dynamic_slice_in_dim(w_gate, z * fl, fl, axis=2)
-    wu = lax.dynamic_slice_in_dim(w_up, z * fl, fl, axis=2)
-    wd = lax.dynamic_slice_in_dim(w_down, z * fl, fl, axis=1)
-    w_in_t = jnp.concatenate(
-        [wg.transpose(0, 2, 1), wu.transpose(0, 2, 1)], axis=0
-    ).reshape(2 * per_dev * fl, width)
-    w_in = jnp.concatenate([wg[0], wg[1], wu[0], wu[1]], axis=1)
-    wd = wd.reshape(per_dev * fl, width)
-    mix, gh, dwin, dwd = moe(
-        h2_all, g_all, w_in, wd.T, wd, w_in_t, per_dev, nz, ne, count, min(4, ne)
-    )
-    gh_sum, mix = scatter_tokens(
-        gh.reshape(nz * ne, count, width + 2 * split), nz, ne, True, 3,
-        after=mix.reshape(-1, width),
-    )
+    h2_wide = jnp.concatenate([h2, high, blank, low, blank], axis=1)
+    wide = width + 2 * split
+    fits, slots, scratch = moe_net_scratch(nz, ne, per_dev, count, width, wide, fl)
+    if fits:
+        _, mix, gh_sum, dwin, dwd = moe_net(
+            h2_wide, g_all, w_gate, w_up, w_down, nz, ne, fl, slots, scratch, 2
+        )
+        mix = mix.reshape(-1, width)
+    else:
+        h2_all = gather_tokens(h2_wide, nz, ne, True, 2).reshape(-1, wide)
+        wg = lax.dynamic_slice_in_dim(w_gate, z * fl, fl, axis=2)
+        wu = lax.dynamic_slice_in_dim(w_up, z * fl, fl, axis=2)
+        wd = lax.dynamic_slice_in_dim(w_down, z * fl, fl, axis=1).reshape(per_dev * fl, width)
+        w_in = jnp.concatenate([*wg, *wu], axis=1)
+        mix, gh, dwin, dwd = moe(
+            h2_all, g_all, w_in, wd, per_dev, nz, ne, count, min(4, ne)
+        )
+        gh_sum, mix = scatter_tokens(
+            gh.reshape(nz * ne, count, wide), nz, ne, True, 3, after=mix.reshape(-1, width)
+        )
     grad_from_experts = gh_sum[:, :width]
     grad_gates = (
         gh_sum[:, width : width + expert_count]

time: 886 us -> 798 us (0.901)
  Pallas kernels: 692 us -> 582 us
  waiting for transfers between devices: 0.57 us -> 37.3 us
  local copies, waits for them, and re-layouts: 45.5 us -> 33.8 us
    pallas_call x3 -> x2, Pallas kernels: 199 us -> 67.3 us  [gather_tokens(): pl.pallas_call(functools.partial(gather_kernel, nz, ne, spread), out_shap...]
    pallas_call x1, Pallas kernels: 96.2 us -> 203 us  [moe_net(): pl.pallas_call(functools.partial(moe_net_kernel, nz, ne, per_dev, slots),...]
    pallas_call x3 -> x2, Pallas kernels: 143 us -> 57.7 us  [scatter_tokens(): pl.pallas_call(functools.partial(scatter_kernel, nz, ne, spread), out_sha...]
    all_gather x1, waiting for transfers between devices: 0.01 us -> 36.7 us  [body(): g_all = lax.all_gather(cot, both, axis=0, tiled=True)]
  transfers between devices with their start and end apart: 5 -> 5, of which waited for: 0 -> 1; matrix products, arithmetic and copies ran while one was open for 14% -> 13% of each run, Pallas kernels for 48% -> 37%
where the time goes in v4:
time: 798 us; the launch traced here: 792 us
  Pallas kernels  582 us (73%)
  matrix products  47.2 us (6%)
  other arithmetic  38.8 us (5%)
  waiting for transfers between devices  37.3 us (5%)
  local copies, waits for them, and re-layouts  33.8 us (4%)
  blocking collectives  29 us (4%)
  between operations  15.2 us (2%)
  starting transfers between devices  8.22 us (1%)
    pallas_call x1, Pallas kernels, moe_net(): pl.pallas_call(functools.partial(moe_net_kernel, nz, ne, per_dev, slots),...  203 us
    pallas_call x1, Pallas kernels, reduce_columns(): pl.pallas_call(functools.partial(reduce_kernel, nz, ne), out_shape=jax.Sh...  125 us
    pallas_call x1, Pallas kernels, start_gather(): pl.pallas_call(functools.partial(start_kernel, nz, ne), out_shape=[jax.Sh...  84.6 us
    pallas_call x2, Pallas kernels, gather_tokens(): pl.pallas_call(functools.partial(gather_kernel, nz, ne, spread), out_shap...  67.3 us
    pallas_call x2, Pallas kernels, scatter_tokens(): pl.pallas_call(functools.partial(scatter_kernel, nz, ne, spread), out_sha...  57.7 us
    all_gather x1, waiting for transfers between devices, body(): g_all = lax.all_gather(cot, both, axis=0, tiled=True)  36.7 us
    dot_general x15, matrix products, dot(): return lax.dot_general(a, b, (dims, ((), ())), preferred_element_type=F32)  34.4 us
    pallas_call x1, Pallas kernels, swap_in_plane(): pl.pallas_call(functools.partial(swap_kernel, ne), out_shape=jax.ShapeDty...  28.4 us
  transfers between devices with their start and end apart: 5, of which 1 were waited for; matrix products, arithmetic and copies ran while one was open for 13% of the time, Pallas kernels for 37%

profile of v4, /device:TPU:0, one launch (start us, length us, event | category | flops | bytes accessed | tf_op | source)
XLA Modules:
  0.0 792.0 jit_solution(4109396715596942915)
XLA Ops:
  11.9 84.6 %start_gather.1 = (bf16[8,128,2048]{2,1,0:T(8,128)(2,1)}, bf16[3,2048,256]{2,1,0:T(8,128)(2,1)}, bf16[256,2048]{1,0:T(8,128)(2,1)}, bf16[4,32,512]{2,1,0:T(8,128...) custom-call(bf16[128,2048]{1,0:T(8,128)(2,1)} %x_ref.1, ...), custom_call_target="tpu_custom_call", output_to_operand_aliasing={{5}: (5, {})} | custom-call | tf_op jit(solution)/shard_map/start_gather/pallas_call | solution.py:616
  96.5 3.2 multiply_reduce_fusion
  105.0 13.2 %psum.14 = f32[2,1024]{1,0:T(2,128)S(1)} all-reduce(f32[2,1024]{1,0:T(2,128)S(1)} %pad_maximum_fusion.9), channel_id=1, replica_groups=mesh['dp'=4,'expert'=8] {'expert'}, use_global_device_ids=true, to_apply=%region_3.0 | all-reduce | flops 2048 | bytes 16384 | tf_op jit(solution)/shard_map/psum | solution.py:1260
  125.4 3.7 convolution_convert_fusion.8
  135.9 3.3 convolution_convert_fusion
  139.2 31.4 %scatter_tokens.2 = f32[128,2048]{1,0:T(8,128)} custom-call(bf16[8,128,2048]{2,1,0:T(8,128)(2,1)} %bitcast.167), custom_call_target="tpu_custom_call" | custom-call | tf_op jit(solution)/shard_map/scatter_tokens/pallas_call | solution.py:350
  176.0 36.7 %all-gather.2.cloned.1.call-done = bf16[4096,2048]{1,0:T(8,128)(2,1)} async-done(((bf16[128,2048]{1,0:T(8,128)(2,1)}), bf16[4096,2048]{1,0:T(8,128)(2,1)}) %all-gather.2.cloned.1.call-update) | async-done | bytes 16777232 | tf_op jit(solution)/shard_map/all_gather | solution.py:1250
  212.7 203.2 %moe_net.1 = (bf16[32,128,2176]{2,1,0:T(8,128)(2,1)}, bf16[8,4,128,2048]{3,2,1,0:T(8,128)(2,1)}, f32[128,2176]{1,0:T(8,128)}, bf16[2048,1024]{1,0:T(8,128)(2,1)}, f32[512,2048]{1,0:T(8,128)}) custom-call(bf16[128,2176]{1,0:T(8,128)(2,1)} %concatenate.40.h_ref, bf16[32,128,2048]{2,1,0:T(8,128)(2,1)} %bitcast.168, bf16[2,2048,1024]{2,1,0:T(8,128)(2,1)} %wg_ref.1, ...), custom_call_target="tpu_custom_call" | custom-call | tf_op jit(solution)/shard_map/moe_net/pallas_call | solution.py:1202
  416.6 5.4 fusion.2
  425.1 24.7 %gather_tokens.2 = bf16[8,128,2048]{2,1,0:T(8,128)(2,1)} custom-call(bf16[128,2048]{1,0:T(8,128)(2,1)} %fusion.75.x_ref), custom_call_target="tpu_custom_call" | custom-call | tf_op jit(solution)/shard_map/gather_tokens/pallas_call | solution.py:236
  449.8 4.8 convolution_convert_fusion.7
  463.8 3.8 convolution_bitcast_fusion.1
  467.6 3.8 convolution_bitcast_fusion
  479.9 4.7 convolution_convert_fusion.1.x_ref
  484.6 28.4 %swap_in_plane.1 = bf16[2048,256]{1,0:T(8,128)(2,1)} custom-call(bf16[256,2048]{1,0:T(8,128)(2,1)} %convolution_convert_fusion.1.x_ref), custom_call_target="tpu_custom_call" | custom-call | tf_op jit(solution)/shard_map/swap_in_plane/pallas_call | solution.py:666
  516.7 15.8 %psum.15 = f32[2,1024]{1,0:T(2,128)S(1)} all-reduce(f32[2,1024]{1,0:T(2,128)S(1)} %pad_maximum_fusion.10), channel_id=1, replica_groups=mesh['dp'=4,'expert'=8] {'expert'}, use_global_device_ids=true, to_apply=%region_18.19 | all-reduce | flops 2048 | bytes 16384 | tf_op jit(solution)/shard_map/psum | solution.py:1338
  544.9 7.9 %all-to-all-start = ((bf16[4,512,1024]{2,1,0:T(8,128)(2,1)}), bf16[4,512,1024]{2,1,0:T(8,128)(2,1)}, u32[]{:S(2)}, u32[]{:S(2)}) async-start(bf16[4,512,1024]{2,1,0:T(8,128)(2,1)} %bitcast.183), calls=%async_computation.3 | async-start | bytes 8388608 | tf_op jit(solution)/shard_map/all_to_all | solution.py:1314
  558.7 5.0 add_convert_fusion
  563.6 26.3 %scatter_tokens.3 = f32[128,2048]{1,0:T(8,128)} custom-call(bf16[8,128,2048]{2,1,0:T(8,128)(2,1)} %bitcast.170), custom_call_target="tpu_custom_call" | custom-call | tf_op jit(solution)/shard_map/scatter_tokens/pallas_call | solution.py:350
  593.2 125.1 %reduce_columns.1 = f32[2,24,256]{2,1,0:T(8,128)} custom-call(f32[8,24,256]{2,1,0:T(8,128)} %bitcast.190), custom_call_target="tpu_custom_call" | custom-call | tf_op jit(solution)/shard_map/reduce_columns/pallas_call | solution.py:437
  721.1 5.9 lay_experts.1
  727.0 42.7 %gather_tokens.3.x_ref = bf16[8,512,1024]{2,1,0:T(8,128)(2,1)} custom-call(bf16[512,1024]{1,0:T(8,128)(2,1)} %reduce-scatter.8.cloned.1.call-done.x_ref), custom_call_target="tpu_custom_call" | custom-call | tf_op jit(solution)/shard_map/gather_tokens/pallas_call | solution.py:236
  769.7 10.3 %lay_mixer.1 = (f32[3,512,2048]{2,1,0:T(8,128)}, f32[512,2048]{1,0:T(8,128)}) custom-call(bf16[8,512,1024]{2,1,0:T(8,128)(2,1)} %gather_tokens.3.x_ref), custom_call_target="tpu_custom_call" | custom-call | tf_op jit(solution)/shard_map/lay_mixer/pallas_call | solution.py:688
  780.0 3.2 fusion.17
  (240 shorter events, 79.9 us)
Async XLA Ops:
  7.2 205.5 %all-gather.2.cloned.1.call-start = ((), (), s32[]{:S(2)}) async-start(), calls=%async_computation.4 | async-start | bytes 17301504 | tf_op jit(solution)/shard_map/all_gather | solution.py:1250
  96.5 456.4 %reduce-scatter.4.cloned.1.call-start = ((), (), s32[]{:S(2)}) async-start(), calls=%async_computation.5 | async-start | bytes 18874368 | tf_op jit(solution)/shard_map/reduce_scatter | solution.py:1310
  103.6 14.7 %copy-start.7 = (f32[1024,256]{0,1:T(8,128)}, f32[1024,256]{0,1:T(8,128)S(1)}, u32[]{:S(2)}) copy-start(f32[1024,256]{0,1:T(8,128)S(1)} %get-tuple-element.82) | copy-start | bytes 3145732
  105.0 16.4 %copy-start.5 = (f32[1024,256]{0,1:T(8,128)}, f32[1024,256]{0,1:T(8,128)S(1)}, u32[]{:S(2)}) copy-start(f32[1024,256]{0,1:T(8,128)S(1)} %get-tuple-element.84) | copy-start | bytes 3145732
  139.2 31.4 %copy-start.10 = (bf16[128,2048]{1,0:T(8,128)(2,1)S(1)}, bf16[128,2048]{1,0:T(8,128)(2,1)}, u32[]{:S(2)}) copy-start(bf16[128,2048]{1,0:T(8,128)(2,1)} %x_ref.1) | copy-start | bytes 1572868
  139.2 35.0 %copy-start.62 = (s32[128,8]{0,1:T(8,128)S(1)}, s32[128,8]{0,1:T(8,128)}, u32[]{:S(2)}) copy-start(s32[128,8]{0,1:T(8,128)} %param.13) | copy-start | bytes 12292
  174.9 37.8 %copy-start.57 = (f32[128]{0:T(128)}, f32[128]{0:T(128)S(1)}, u32[]{:S(2)}) copy-start(f32[128]{0:T(128)S(1)} %fusion.65) | copy-start | bytes 1540
  415.9 311.1 %reduce-scatter.8.cloned.1.call-start = ((), (), s32[]{:S(2)}) async-start(), calls=%async_computation.7 | async-start | bytes 5242880 | tf_op jit(solution)/shard_map/reduce_scatter | solution.py:1352
  422.9 31.6 %copy-start.63 = (f32[128]{0:T(128)}, f32[128]{0:T(128)S(1)}, u32[]{:S(2)}) copy-start(f32[128]{0:T(128)S(1)} %broadcast_multiply_fusion.2) | copy-start | bytes 1540
  460.1 11.2 %copy-start.39 = (f32[128,64]{1,0:T(8,128)S(1)}, f32[128,64]{1,0:T(8,128)}, u32[]{:S(2)}) copy-start(f32[128,64]{1,0:T(8,128)} %copy-done.38) | copy-start | bytes 98308
  460.1 11.2 %copy-start.42 = (f32[128,64]{1,0:T(8,128)S(1)}, f32[128,64]{1,0:T(8,128)}, u32[]{:S(2)}) copy-start(f32[128,64]{1,0:T(8,128)} %get-tuple-element.78) | copy-start | bytes 98308
  479.9 33.1 %copy-start.6 = (f32[1024,256]{0,1:T(8,128)S(1)}, f32[1024,256]{0,1:T(8,128)}, u32[]{:S(2)}) copy-start(f32[1024,256]{0,1:T(8,128)} %copy-done.5) | copy-start | bytes 3145732
  479.9 33.1 %copy-start.46 = (f32[1,1024]{1,0:T(1,128)S(1)}, f32[1,1024]{1,0:T(1,128)}, u32[]{:S(2)}) copy-start(f32[1,1024]{1,0:T(1,128)} %copy-done.45) | copy-start | bytes 12292
  479.9 33.2 %copy-start.51 = (f32[1,256]{1,0:T(1,128)S(1)}, f32[1,256]{1,0:T(1,128)}, u32[]{:S(2)}) copy-start(f32[1,256]{1,0:T(1,128)} %copy-done.50) | copy-start | bytes 3076
  479.9 34.8 %copy-start.48 = (f32[1,1024]{1,0:T(1,128)S(1)}, f32[1,1024]{1,0:T(1,128)}, u32[]{:S(2)}) copy-start(f32[1,1024]{1,0:T(1,128)} %copy-done.47) | copy-start | bytes 12292
  479.9 34.8 %copy-start.53 = (f32[1,256]{1,0:T(1,128)S(1)}, f32[1,256]{1,0:T(1,128)}, u32[]{:S(2)}) copy-start(f32[1,256]{1,0:T(1,128)} %copy-done.52) | copy-start | bytes 3076
  544.9 176.2 %all-to-all-start = ((bf16[4,512,1024]{2,1,0:T(8,128)(2,1)}), bf16[4,512,1024]{2,1,0:T(8,128)(2,1)}, u32[]{:S(2)}, u32[]{:S(2)}) async-start(bf16[4,512,1024]{2,1,0:T(8,128)(2,1)} %bitcast.183), calls=%async_computation.3 | async-start | bytes 8388608 | tf_op jit(solution)/shard_map/all_to_all | solution.py:1314
  552.8 227.2 %reduce-scatter.6.cloned.1.call-start = ((), (), s32[]{:S(2)}) async-start(), calls=%async_computation.6 | async-start | bytes 2621440 | tf_op jit(solution)/shard_map/reduce_scatter | solution.py:1311
  553.4 36.8 %copy-start.65 = (f32[128]{0:T(128)}, f32[128]{0:T(128)S(1)}, u32[]{:S(2)}) copy-start(f32[128]{0:T(128)S(1)} %add_rsqrt_fusion.2) | copy-start | bytes 1540
  563.6 26.6 %copy-start.11 = (bf16[128,2048]{1,0:T(8,128)(2,1)S(1)}, bf16[128,2048]{1,0:T(8,128)(2,1)}, u32[]{:S(2)}) copy-start(bf16[128,2048]{1,0:T(8,128)(2,1)} %x_ref.1) | copy-start | bytes 1572868
  769.6 10.3 %copy-start.8 = (f32[128,2048]{1,0:T(8,128)S(1)}, f32[128,2048]{1,0:T(8,128)}, u32[]{:S(2)}) copy-start(f32[128,2048]{1,0:T(8,128)} %scatter_tokens.3) | copy-start | bytes 3145732
  769.7 10.3 %copy-start.12 = (bf16[128,2048]{1,0:T(8,128)(2,1)S(1)}, bf16[128,2048]{1,0:T(8,128)(2,1)}, u32[]{:S(2)}) copy-start(bf16[128,2048]{1,0:T(8,128)(2,1)} %x_ref.1) | copy-start | bytes 1572868
  769.7 10.3 %copy-start.61 = (f32[128]{0:T(128)S(1)}, f32[128]{0:T(128)}, u32[]{:S(2)}) copy-start(f32[128]{0:T(128)} %copy-done.59) | copy-start | bytes 1540
  769.7 10.3 %copy-start.64 = (f32[128]{0:T(128)S(1)}, f32[128]{0:T(128)}, u32[]{:S(2)}) copy-start(f32[128]{0:T(128)} %copy-done.63) | copy-start | bytes 1540
  (49 other events, 180.4 us)
Sparse Core Ops, SparseCore 0:
  96.6 116.0 all-gather.1
  416.0 133.8 reduce-scatter.3
  552.8 137.9 reduce-scatter.7
  693.0 64.6 reduce-scatter.5

commit v5 on v4

--- a/solution.py
+++ b/solution.py
@@ -35,51 +35,6 @@
     scaled = grad_out * gain_col
     grad_values = inv_rms * (scaled - normed * jnp.mean(scaled * normed, axis=-1, keepdims=True))
     return (grad_values, grad_gain)
-
-
-def rope_tables(length):
-    half = HD // 2
-    freqs = jnp.exp(-jnp.log(ROPE_BASE) * (2.0 * jnp.arange(half, dtype=F32) / HD))
-    angles = jnp.arange(length, dtype=F32)[:, None] * freqs[None, :]
-    return (jnp.cos(angles)[:, None, :], jnp.sin(angles)[:, None, :])
-
-
-def rotate(values, cos_tab, sin_tab):
-    first, second = jnp.split(values, 2, axis=-1)
-    return jnp.concatenate(
-        [first * cos_tab - second * sin_tab, second * cos_tab + first * sin_tab], axis=-1
-    )
-
-
-def attend_scores(query_rot, key_rot, seg_ids):
-    places = jnp.arange(seg_ids.shape[0], dtype=jnp.int32)
-    allowed = (places[:, None] >= places[None, :]) & (seg_ids[:, None] == seg_ids[None, :])
-    scores = jnp.einsum("qhd,khd->hqk", query_rot, key_rot, preferred_element_type=F32)
-    scores = scores * query_rot.shape[-1] ** (-0.5)
-    return jnp.where(allowed[None], scores, MASKED)
-
-
-def attend_forward(query_rot, key_rot, value_bf, seg_ids):
-    scores = attend_scores(query_rot, key_rot, seg_ids)
-    row_max = jnp.max(scores, axis=-1, keepdims=True)
-    log_total = row_max + jnp.log(jnp.sum(jnp.exp(scores - row_max), axis=-1, keepdims=True))
-    weights_bf = jnp.exp(scores - log_total).astype(BF)
-    mixed = jnp.einsum("hqk,khd->qhd", weights_bf, value_bf, preferred_element_type=F32)
-    return (mixed.astype(BF), log_total)
-
-
-def attend_backward(query_rot, key_rot, value_bf, seg_ids, log_total, grad_heads):
-    scores = attend_scores(query_rot, key_rot, seg_ids)
-    probs = jnp.exp(scores - log_total)
-    grad_value = jnp.einsum(
-        "hqk,qhd->khd", probs.astype(BF), grad_heads, preferred_element_type=F32
-    ).astype(BF)
-    grad_probs = jnp.einsum("qhd,khd->hqk", grad_heads, value_bf, preferred_element_type=F32)
-    delta = jnp.sum(probs * grad_probs, axis=-1, keepdims=True)
-    grad_scores = (probs * (grad_probs - delta) * query_rot.shape[-1] ** (-0.5)).astype(BF)
-    grad_query = jnp.einsum("hqk,khd->qhd", grad_scores, key_rot, preferred_element_type=F32)
-    grad_key = jnp.einsum("hqk,qhd->khd", grad_scores, query_rot, preferred_element_type=F32)
-    return (grad_query, grad_key, grad_value)
 
 
 MESH = pl.DeviceIdType.MESH
@@ -639,39 +594,281 @@
     )(x, w_qkv, w_out, small, seg, after)
 
 
-def swap_kernel(ne, x_ref, out_ref, send, recv):
-    z, e = lax.axis_index("dp"), lax.axis_index("expert")
-    hw = x_ref.shape[0]
+def rope_lanes(length):
+    half = HD // 2
+    freqs = jnp.exp(-jnp.log(ROPE_BASE) * (2.0 * jnp.arange(half, dtype=F32) / HD))
+    angles = jnp.arange(length, dtype=F32)[:, None] * freqs[None, :]
+    cos, sin = jnp.cos(angles), jnp.sin(angles)
+    return jnp.concatenate([cos, cos], axis=1), jnp.concatenate([-sin, sin], axis=1)
+
+
+def turn(x, cos, sin):
+    return x * cos + pltpu.roll(x, HD // 2, 1) * sin
+
+
+def meet_plane(ne, z, e):
     sem = pltpu.get_barrier_semaphore()
     for r in range(1, ne):
-        to = (z, lax.rem(e + r, ne))
-        pl.semaphore_signal(sem, inc=1, device_id=to, device_id_type=MESH)
+        pl.semaphore_signal(
+            sem, inc=1, device_id=(z, lax.rem(e + r, ne)), device_id_type=MESH
+        )
     pl.semaphore_wait(sem, ne - 1)
-    mine = pl.ds(pl.multiple_of(e * hw, hw), hw)
+
+
+def plane_totals(ne, z, e, mine, theirs, send, recv):
     copies = []
     for r in range(1, ne):
-        to = lax.rem(e + r, ne)
-        src = x_ref.at[:, pl.ds(pl.multiple_of(to * hw, hw), hw)]
-        copy = remote(src, out_ref.at[mine, :], send.at[r], recv.at[r], (z, to))
+        to = (z, lax.rem(e + r, ne))
+        copy = remote(mine, theirs.at[r], send.at[r], recv.at[r], to)
         copy.start()
         copies.append(copy)
-    out_ref[mine, :] = x_ref[:, mine]
+    total = mine[...]
+    for r, copy in enumerate(copies):
+        copy.wait_recv()
+        total = total + theirs[r + 1]
     for copy in copies:
         copy.wait_send()
-        copy.wait_recv()
-
-
-def swap_in_plane(x, ne, cid):
-    hw, width = x.shape
+    return total
+
+
+def store_columns(sums, first, columns):
+    rows = columns[0].shape[0]
+    lanes = lax.broadcasted_iota(jnp.int32, (rows, 128), 1)
+    wide = jnp.zeros((rows, 128), F32)
+    for j, column in enumerate(columns):
+        wide = jnp.where(lanes == j, column, wide)
+    sums[:, pl.ds(first, rows)] = wide.T[:8]
+
+
+def as_columns(total, out):
+    rows = total.shape[1]
+    for first in range(0, rows, 128):
+        chunk = total[:, first : first + 128]
+        out[first : first + 128, :] = jnp.concatenate([chunk] * 16, axis=0).T
+
+
+def allowed_pairs(seg_ref, n):
+    length = seg_ref.shape[2]
+    keys = jnp.broadcast_to(seg_ref[n, :1].astype(F32), (length, length))
+    i = lax.broadcasted_iota(jnp.int32, (length, length), 0)
+    j = lax.broadcasted_iota(jnp.int32, (length, length), 1)
+    return (i >= j) & (keys == keys.T)
+
+
+def attend(rq, rk, allowed):
+    scores = jnp.where(allowed, dot(rq, rk, NT) * HD ** (-0.5), MASKED)
+    top = jnp.max(scores, axis=-1, keepdims=True)
+    lse = top + jnp.log(jnp.sum(jnp.exp(scores - top), axis=-1, keepdims=True))
+    return jnp.exp(scores - lse)
+
+
+def attn_fwd_kernel(
+    ne, x_ref, wq_ref, wo_ref, gain_ref, mine_ref, seg_ref, cos_ref, sin_ref,
+    h1_ref, q_ref, k_ref, rq_ref, rk_ref, v_ref, o_ref, scale_ref, x1_ref,
+    sums, theirs, send, recv,
+):
+    z, e = lax.axis_index("dp"), lax.axis_index("expert")
+    width = x_ref.shape[2]
+    count, hw = q_ref.shape
+    length = seg_ref.shape[2]
+    rows_dev = x_ref.shape[1]
+    tile = min(512, count)
+    meet_plane(ne, z, e)
+
+    def normed(b, carry):
+        x = x_ref[b].astype(F32)
+        h1 = x * rms_scale(x) * gain_ref[:1]
+        h1_ref[pl.ds(pl.multiple_of(b * rows_dev, rows_dev), rows_dev), :] = h1.astype(BF)
+        return carry
+
+    lax.fori_loop(0, ne, normed, 0)
+    for first in range(0, count, tile):
+        rows = slice(first, first + tile)
+        h1 = h1_ref[rows, :]
+        q, k = dot(h1, wq_ref[0], NN), dot(h1, wq_ref[1], NN)
+        q_ref[rows, :] = q
+        k_ref[rows, :] = k
+        v_ref[rows, :] = dot(h1, wq_ref[2], NN).astype(BF)
+        store_columns(
+            sums, first, [jnp.sum(t * t, axis=-1, keepdims=True) for t in (q, k)]
+        )
+    total = plane_totals(ne, z, e, sums, theirs, send, recv)
+    as_columns(lax.rsqrt(total / width + EPS), scale_ref)
+    cos, sin = cos_ref[...], sin_ref[...]
+
+    def sequence(n, carry):
+        rows = pl.ds(pl.multiple_of(n * length, length), length)
+        allowed = allowed_pairs(seg_ref, n)
+        aq, ak = scale_ref[rows, 0:1], scale_ref[rows, 1:2]
+        for c in range(0, hw, HD):
+            cols = slice(c, c + HD)
+            rq = turn(q_ref[rows, cols] * aq * mine_ref[1:2, cols], cos, sin).astype(BF)
+            rk = turn(k_ref[rows, cols] * ak * mine_ref[2:3, cols], cos, sin).astype(BF)
+            rq_ref[rows, cols] = rq
+            rk_ref[rows, cols] = rk
+            probs = attend(rq, rk, allowed).astype(BF)
+            o_ref[rows, cols] = dot(probs, v_ref[rows, cols], NN).astype(BF)
+        return carry
+
+    lax.fori_loop(0, count // length, sequence, 0)
+    for first in range(0, count, tile):
+        x1 = dot(o_ref[first : first + tile, :], wo_ref[...], NN).astype(BF)
+        blocks = tile // rows_dev
+        x1_ref[first // rows_dev : first // rows_dev + blocks] = x1.reshape(
+            blocks, rows_dev, width
+        )
+
+
+def attn_fwd(in_all, wq, wo, gain_mat, my_gains, seg, tables, cid):
+    ne, rows_dev, width = in_all.shape
+    count, hw = ne * rows_dev, wo.shape[0]
     return pl.pallas_call(
-        functools.partial(swap_kernel, ne),
-        out_shape=jax.ShapeDtypeStruct((width, hw), x.dtype),
-        in_specs=[VMEM],
-        out_specs=VMEM,
-        scratch_shapes=[DMA((ne,)), DMA((ne,))],
-        compiler_params=pltpu.CompilerParams(collective_id=cid, has_side_effects=True),
-        name="swap_in_plane",
-    )(x)
+        functools.partial(attn_fwd_kernel, ne),
+        out_shape=[
+            jax.ShapeDtypeStruct((count, width), BF),
+            jax.ShapeDtypeStruct((count, hw), F32),
+            jax.ShapeDtypeStruct((count, hw), F32),
+            jax.ShapeDtypeStruct((count, hw), BF),
+            jax.ShapeDtypeStruct((count, hw), BF),
+            jax.ShapeDtypeStruct((count, hw), BF),
+            jax.ShapeDtypeStruct((count, hw), BF),
+            jax.ShapeDtypeStruct((count, 128), F32),
+            jax.ShapeDtypeStruct((ne, rows_dev, width), BF),
+        ],
+        in_specs=[VMEM] * 8,
+        out_specs=[VMEM] * 9,
+        scratch_shapes=[
+            pltpu.VMEM((8, count), F32), pltpu.VMEM((ne, 8, count), F32), DMA((ne,)), DMA((ne,)),
+        ],
+        compiler_params=pltpu.CompilerParams(
+            collective_id=cid, has_side_effects=True, vmem_limit_bytes=60_000_000
+        ),
+        name="attn_fwd",
+    )(in_all, wq, wo, gain_mat, my_gains, seg, *tables)
+
+
+def attn_bwd_kernel(
+    ne, gab_ref, wq_ref, wo_ref, mine_ref, seg_ref, cos_ref, sin_ref,
+    h1_ref, q_ref, k_ref, rq_ref, rk_ref, v_ref, o_ref, scale_ref,
+    gh1_ref, parts_ref, gain_ref,
+    pout, go_ref, gqn_ref, gkn_ref, gp_ref, sums, theirs, means, send, recv, psend, precv,
+):
+    z, e = lax.axis_index("dp"), lax.axis_index("expert")
+    count, hw = q_ref.shape
+    width = gab_ref.shape[2]
+    rows_dev = gab_ref.shape[1]
+    length = seg_ref.shape[2]
+    tile = min(512, count)
+    blocks = tile // rows_dev
+    meet_plane(ne, z, e)
+
+    gab = lambda first: gab_ref[first // rows_dev : first // rows_dev + blocks].reshape(tile, width)
+    part = dot(o_ref[:tile, :], gab(0), TN)
+    for first in range(tile, count, tile):
+        part = part + dot(o_ref[first : first + tile, :], gab(first), TN)
+    pout[...] = part.astype(BF)
+    for first in range(0, count, tile):
+        go_ref[first : first + tile, :] = dot(gab(first), wo_ref[...], NT).astype(BF)
+    my_rows = pl.ds(pl.multiple_of(e * hw, hw), hw)
+    last = pl.ds(3 * hw, hw)
+    gives = []
+    for r in range(1, ne):
+        to = lax.rem(e + r, ne)
+        give = remote(
+            pout.at[:, pl.ds(pl.multiple_of(to * hw, hw), hw)], parts_ref.at[my_rows, last],
+            psend.at[r], precv.at[r], (z, to),
+        )
+        give.start()
+        gives.append(give)
+    parts_ref[my_rows, last] = pout[:, my_rows]
+
+    cos, sin = cos_ref[...], -sin_ref[...]
+    gain_ref[...] = jnp.zeros_like(gain_ref)
+
+    def sequence(n, carry):
+        start = pl.multiple_of(n * length, length)
+        rows = pl.ds(start, length)
+        allowed = allowed_pairs(seg_ref, n)
+        aq, ak = scale_ref[rows, 0:1], scale_ref[rows, 1:2]
+        sum_q = jnp.zeros((length, 1), F32)
+        sum_k = jnp.zeros((length, 1), F32)
+        for c in range(0, hw, HD):
+            cols = slice(c, c + HD)
+            rq, rk, go = rq_ref[rows, cols], rk_ref[rows, cols], go_ref[rows, cols]
+            probs = attend(rq, rk, allowed)
+            gv = dot(probs.astype(BF), go, TN).astype(BF)
+            gp_ref[rows, slice(2 * hw + c, 2 * hw + c + HD)] = gv
+            grad = dot(go, v_ref[rows, cols], NT)
+            delta = jnp.sum(probs * grad, axis=-1, keepdims=True)
+            gs = (probs * (grad - delta) * HD ** (-0.5)).astype(BF)
+            gqn = turn(dot(gs, rk, NN), cos, sin)
+            gkn = turn(dot(gs, rq, TN), cos, sin)
+            gqn_ref[rows, cols] = gqn
+            gkn_ref[rows, cols] = gkn
+            tq = gqn * (q_ref[rows, cols] * aq)
+            tk = gkn * (k_ref[rows, cols] * ak)
+            gain_ref[0:1, cols] += jnp.sum(tq, axis=0, keepdims=True)
+            gain_ref[1:2, cols] += jnp.sum(tk, axis=0, keepdims=True)
+            sum_q = sum_q + jnp.sum(tq * mine_ref[1:2, cols], axis=-1, keepdims=True)
+            sum_k = sum_k + jnp.sum(tk * mine_ref[2:3, cols], axis=-1, keepdims=True)
+        store_columns(sums, start, [sum_q, sum_k])
+        return carry
+
+    lax.fori_loop(0, count // length, sequence, 0)
+    total = plane_totals(ne, z, e, sums, theirs, send, recv)
+    as_columns(total / width, means)
+    for first in range(0, count, tile):
+        rows = slice(first, first + tile)
+        aq, ak = scale_ref[rows, 0:1], scale_ref[rows, 1:2]
+        mq, mk = means[rows, 0:1], means[rows, 1:2]
+        gq = aq * (gqn_ref[rows, :] * mine_ref[1:2] - q_ref[rows, :] * aq * mq)
+        gk = ak * (gkn_ref[rows, :] * mine_ref[2:3] - k_ref[rows, :] * ak * mk)
+        gp_ref[rows, :hw] = gq.astype(BF)
+        gp_ref[rows, hw : 2 * hw] = gk.astype(BF)
+    for first in range(0, width, tile):
+        rows = slice(first, first + tile)
+        parts_ref[rows, : 3 * hw] = dot(h1_ref[:, rows], gp_ref[...], TN).astype(BF)
+    for first in range(0, count, tile):
+        rows = slice(first, first + tile)
+        gh1 = dot(gp_ref[rows, :hw], wq_ref[0], NT)
+        for j in range(1, 3):
+            gh1 = gh1 + dot(gp_ref[rows, j * hw : (j + 1) * hw], wq_ref[j], NT)
+        gh1_ref[first // rows_dev : first // rows_dev + blocks] = gh1.astype(BF).reshape(
+            blocks, rows_dev, width
+        )
+    for give in gives:
+        give.wait_send()
+        give.wait_recv()
+
+
+def attn_bwd(gab, wq, wo, my_gains, seg, tables, saved, cid):
+    ne, rows_dev, width = gab.shape
+    count, hw = ne * rows_dev, wo.shape[0]
+    return pl.pallas_call(
+        functools.partial(attn_bwd_kernel, ne),
+        out_shape=[
+            jax.ShapeDtypeStruct((ne, rows_dev, width), BF),
+            jax.ShapeDtypeStruct((width, 4 * hw), BF),
+            jax.ShapeDtypeStruct((8, hw), F32),
+        ],
+        in_specs=[VMEM] * 15,
+        out_specs=[VMEM] * 3,
+        scratch_shapes=[
+            pltpu.VMEM((hw, width), BF),
+            pltpu.VMEM((count, hw), BF),
+            pltpu.VMEM((count, hw), F32),
+            pltpu.VMEM((count, hw), F32),
+            pltpu.VMEM((count, 3 * hw), BF),
+            pltpu.VMEM((8, count), F32),
+            pltpu.VMEM((ne, 8, count), F32),
+            pltpu.VMEM((count, 128), F32),
+            DMA((ne,)), DMA((ne,)), DMA((ne,)), DMA((ne,)),
+        ],
+        compiler_params=pltpu.CompilerParams(
+            collective_id=cid, has_side_effects=True, vmem_limit_bytes=64_000_000
+        ),
+        name="attn_bwd",
+    )(gab, wq, wo, my_gains, seg, *tables, *saved)
 
 
 def lay_kernel(kinds, hw, x_ref, *outs):
@@ -1245,28 +1442,14 @@
     router_t = small[:expert_count]
     gain_mat = small[expert_count : expert_count + 4].astype(F32)
     my_gains = lax.dynamic_slice_in_dim(gain_mat, e * hw, hw, axis=1)
-    seg_all = seg_all.reshape(ne * num_seqs, 8, length)[:, 0]
+    seg_all = seg_all.reshape(ne * num_seqs, 8, length)
 
     g_all = lax.all_gather(cot, both, axis=0, tiled=True)
-    in_all = in_all.reshape(ne * count, width).astype(F32)
-    h1_all = (in_all * rms_scale(in_all) * gain_mat[0]).astype(BF)
     inputs_f = inputs.astype(F32)
     scale_one = rms_scale(inputs_f)
-    plane = h1_all.shape[0]
-    shape_heads = (ne * num_seqs, length, heads, HD)
-
-    q, k, v = [dot(h1_all, wq[j], NN) for j in range(3)]
-    sums = jnp.stack([jnp.sum(q * q, axis=-1), jnp.sum(k * k, axis=-1)])
-    scales = lax.rsqrt(lax.psum(sums, "expert") / width + EPS)
-    aq, ak = scales[0][:, None], scales[1][:, None]
-    cos_tab, sin_tab = rope_tables(length)
-    rq = rotate((q * aq * my_gains[1]).reshape(shape_heads), cos_tab, sin_tab).astype(BF)
-    rk = rotate((k * ak * my_gains[2]).reshape(shape_heads), cos_tab, sin_tab).astype(BF)
-    vb = v.astype(BF).reshape(shape_heads)
-    o, lse = jax.vmap(attend_forward)(rq, rk, vb, seg_all)
-    o = o.reshape(plane, hw)
-    x1_part = dot(o, wo, NN).astype(BF)
-    (x1_sum,) = scatter_tokens(x1_part.reshape(ne, count, width), nz, ne, False, 1)
+    tables = rope_lanes(length)
+    *saved, x1_part = attn_fwd(in_all, wq, wo, gain_mat, my_gains, seg_all, tables, 9)
+    (x1_sum,) = scatter_tokens(x1_part, nz, ne, False, 1)
     x1 = inputs_f + x1_sum
 
     a2 = rms_scale(x1)
@@ -1327,31 +1510,13 @@
     gx1 = grad_top + grad_ffn
     gab = gx1.astype(BF)
 
-    gab_all = gather_tokens(gab, nz, ne, False, 4).reshape(-1, width)
-    go = dot(gab_all, wo, NT).astype(BF).reshape(shape_heads)
-    grad_q, grad_k, gv = jax.vmap(attend_backward)(rq, rk, vb, seg_all, lse, go)
-    gqn = rotate(grad_q, cos_tab, -sin_tab).reshape(plane, hw)
-    gkn = rotate(grad_k, cos_tab, -sin_tab).reshape(plane, hw)
-    nq, nk = q * aq, k * ak
-    sq, sk = gqn * my_gains[1], gkn * my_gains[2]
-    sums = jnp.stack([jnp.sum(sq * nq, axis=-1), jnp.sum(sk * nk, axis=-1)])
-    means = lax.psum(sums, "expert") / width
-    gq = (aq * (sq - nq * means[0][:, None])).astype(BF)
-    gk = (ak * (sk - nk * means[1][:, None])).astype(BF)
-    gproj = [gq, gk, gv.reshape(plane, hw)]
-    gain_q, gain_k = jnp.sum(gqn * nq, axis=0), jnp.sum(gkn * nk, axis=0)
-
-    gh1_part = sum(dot(part, wq[j], NT) for j, part in enumerate(gproj)).astype(BF)
-    (gh1,) = scatter_tokens(gh1_part.reshape(ne, count, width), nz, ne, False, 5)
+    gab_all = gather_tokens(gab, nz, ne, False, 4)
+    gh1_part, parts, gain_qk = attn_bwd(gab_all, wq, wo, my_gains, seg_all, tables, saved, 10)
+    mine = lax.psum_scatter(parts, "dp", scatter_dimension=0, tiled=True)
+    (gh1,) = scatter_tokens(gh1_part, nz, ne, False, 5)
     grad_front, gain_attn = rms_backward(inputs_f, scale_one, gain_mat[0], gh1)
     grad_inputs = (gx1 + grad_front).astype(BF)
 
-    part_out = dot(o, gab_all, TN).astype(BF)
-    part_out = swap_in_plane(part_out, ne, 8)
-    parts = [dot(h1_all, part, TN).astype(BF) for part in gproj] + [part_out]
-    mine = lax.psum_scatter(
-        jnp.concatenate(parts, axis=1), "dp", scatter_dimension=0, tiled=True
-    )
     wide = gather_tokens(mine, nz, ne, False, 6)
     grad_w_qkv, grad_w_out = lay_mixer(wide, 4, hw)
     grad_w_qkv = grad_w_qkv.transpose(1, 0, 2)
@@ -1361,7 +1526,7 @@
     )
     tiny = jnp.concatenate(
         [
-            local_router, gain_attn[None], place(gain_q), place(gain_k), gain_ffn[None],
+            local_router, gain_attn[None], place(gain_qk[0]), place(gain_qk[1]), gain_ffn[None],
             jnp.zeros((-(expert_count + 4) % 8, width), F32),
         ],
         axis=0,

time: 798 us -> 750 us (0.940)
  waiting for transfers between devices: 37.3 us -> 98 us
  matrix products: 47.2 us -> 2.22 us
  blocking collectives: 29 us -> 0 us
  other arithmetic: 38.8 us -> 14.9 us
  local copies, waits for them, and re-layouts: 33.8 us -> 15.6 us
  Pallas kernels: 582 us -> 594 us
    pallas_call x1 -> x2, Pallas kernels: 28.4 us -> 76.9 us  [the longest x1 50.6 us: attn_bwd(): pl.pallas_call(functools.partial(attn_bwd_kernel, ne), out_shape=[jax.Sha...]
    reduce_scatter x1, waiting for transfers between devices: 0.01 us -> 44.1 us  [body(): mix = lax.psum_scatter(mix, 'expert', scatter_dimension=0, tiled=True)]
    pallas_call x1, Pallas kernels: 125 us -> 86.5 us  [reduce_columns(): pl.pallas_call(functools.partial(reduce_kernel, nz, ne), out_shape=jax.Sh...]
    dot_general x15 -> x3, matrix products: 34.4 us -> 2.22 us  [dot(): return lax.dot_general(a, b, (dims, ((), ())), preferred_element_type=F32)]
    psum x2 -> x0, blocking collectives: 29 us -> none  [the longest x1 15.8 us: body(): means = lax.psum(sums, 'expert') / width]
    all_gather x1, waiting for transfers between devices: 36.7 us -> 53.9 us  [body(): g_all = lax.all_gather(cot, both, axis=0, tiled=True)]
    dot_general x6 -> x0, matrix products: 12.8 us -> none  [the longest x1 3.81 us: attend_backward(): jnp.einsum('hqk,khd->qhd', grad_scores, key_rot, preferred_element_type=F32)]
    convert_element_type x4 -> x0, other arithmetic: 10.4 us -> none  [the longest x2 6.39 us: body(): h1_all = (in_all * rms_scale(in_all) * gain_mat[0]).astype(BF)]
  transfers between devices with their start and end apart: 5 -> 5, of which waited for: 1 -> 2; matrix products, arithmetic and copies ran while one was open for 13% -> 3% of each run, Pallas kernels for 37% -> 41%
where the time goes in v5:
time: 750 us; the launch traced here: 749 us
  Pallas kernels  594 us (79%)
  waiting for transfers between devices  98 us (13%)
  local copies, waits for them, and re-layouts  15.6 us (2%)
  other arithmetic  14.9 us (2%)
  between operations  14.3 us (2%)
  starting transfers between devices  9.44 us (1%)
    pallas_call x1, Pallas kernels, moe_net(): pl.pallas_call(functools.partial(moe_net_kernel, nz, ne, per_dev, slots),...  199 us
    pallas_call x1, Pallas kernels, reduce_columns(): pl.pallas_call(functools.partial(reduce_kernel, nz, ne), out_shape=jax.Sh...  86.5 us
    pallas_call x1, Pallas kernels, start_gather(): pl.pallas_call(functools.partial(start_kernel, nz, ne), out_shape=[jax.Sh...  84.5 us
    pallas_call x2, Pallas kernels, scatter_tokens(): pl.pallas_call(functools.partial(scatter_kernel, nz, ne, spread), out_sha...  66.4 us
    pallas_call x2, Pallas kernels, gather_tokens(): pl.pallas_call(functools.partial(gather_kernel, nz, ne, spread), out_shap...  64.1 us
    all_gather x1, waiting for transfers between devices, body(): g_all = lax.all_gather(cot, both, axis=0, tiled=True)  53.9 us
    pallas_call x1, Pallas kernels, attn_bwd(): pl.pallas_call(functools.partial(attn_bwd_kernel, ne), out_shape=[jax.Sha...  50.6 us
    reduce_scatter x1, waiting for transfers between devices, body(): mix = lax.psum_scatter(mix, 'expert', scatter_dimension=0, tiled=True)  44.1 us
  transfers between devices with their start and end apart: 5, of which 2 were waited for; matrix products, arithmetic and copies ran while one was open for 3% of the time, Pallas kernels for 41%

profile of v5, /device:TPU:0, one launch (start us, length us, event | category | flops | bytes accessed | tf_op | source)
XLA Modules:
  0.0 748.6 jit_solution(15804470938382129056)
XLA Ops:
  7.2 1.9 copy.46._
  9.2 1.4 maximum_maximum_fusion.small_ref
  11.9 84.5 %start_gather.1 = (bf16[8,128,2048]{2,1,0:T(8,128)(2,1)}, bf16[3,2048,256]{2,1,0:T(8,128)(2,1)}, bf16[256,2048]{1,0:T(8,128)(2,1)}, bf16[4,32,512]{2,1,0:T(8,128...) custom-call(bf16[128,2048]{1,0:T(8,128)(2,1)} %x_ref.1, ...), custom_call_target="tpu_custom_call", output_to_operand_aliasing={{5}: (5, {})} | custom-call | tf_op jit(solution)/shard_map/start_gather/pallas_call | solution.py:571
  98.9 26.3 %attn_fwd.1 = (bf16[1024,2048]{1,0:T(8,128)(2,1)}, f32[1024,256]{1,0:T(8,128)}, f32[1024,256]{1,0:T(8,128)}, bf16[1024,256]{1,0:T(8,128)(2,1)}, bf16[1024,256]{1...) custom-call(bf16[8,128,2048]{2,1,0:T(8,128)(2,1)} %get-tuple-element, ...), custom_call_target="tpu_custom_call" | custom-call | tf_op jit(solution)/shard_map/attn_fwd/pallas_call | solution.py:725
  125.3 38.4 %scatter_tokens.2 = f32[128,2048]{1,0:T(8,128)} custom-call(bf16[8,128,2048]{2,1,0:T(8,128)(2,1)} %get-tuple-element.40.x_ref), custom_call_target="tpu_custom_call" | custom-call | tf_op jit(solution)/shard_map/scatter_tokens/pallas_call | solution.py:305
  163.7 2.0 multiply_reduce_fusion.2
  169.0 53.9 %all-gather.2.cloned.1.call-done = bf16[4096,2048]{1,0:T(8,128)(2,1)} async-done(((bf16[128,2048]{1,0:T(8,128)(2,1)}), bf16[4096,2048]{1,0:T(8,128)(2,1)}) %all-gather.2.cloned.1.call-update) | async-done | bytes 16777232 | tf_op jit(solution)/shard_map/all_gather | solution.py:1447
  222.9 199.5 %moe_net.1 = (bf16[32,128,2176]{2,1,0:T(8,128)(2,1)}, bf16[8,4,128,2048]{3,2,1,0:T(8,128)(2,1)}, f32[128,2176]{1,0:T(8,128)}, bf16[2048,1024]{1,0:T(8,128)(2,1)}, f32[512,2048]{1,0:T(8,128)}) custom-call(bf16[128,2176]{1,0:T(8,128)(2,1)} %concatenate.29.h_ref, bf16[32,128,2048]{2,1,0:T(8,128)(2,1)} %bitcast.40, bf16[2,2048,1024]{2,1,0:T(8,128)(2,1)} %wg_ref.1, ...), custom_call_target="tpu_custom_call" | custom-call | tf_op jit(solution)/shard_map/moe_net/pallas_call | solution.py:1399
  425.5 1.7 multiply_reduce_fusion
  428.2 2.2 fusion.15.x_ref
  430.4 23.4 %gather_tokens.2.gab_ref = bf16[8,128,2048]{2,1,0:T(8,128)(2,1)} custom-call(bf16[128,2048]{1,0:T(8,128)(2,1)} %fusion.15.x_ref), custom_call_target="tpu_custom_call" | custom-call | tf_op jit(solution)/shard_map/gather_tokens/pallas_call | solution.py:191
  453.8 50.6 %attn_bwd.1 = (bf16[8,128,2048]{2,1,0:T(8,128)(2,1)}, bf16[2048,1024]{1,0:T(8,128)(2,1)}, f32[8,256]{1,0:T(8,128)}) custom-call(bf16[8,128,2048]{2,1,0:T(8,128)(2,1)} %gather_tokens.2.gab_ref, bf16[3,2048,256]{2,1,0:T(8,128)(2,1)} %get-tuple-element.36.wq_ref, bf16[256,2048]{1,0:T(8,128)(2,1)} %get-tuple-element.37.wo_ref, ...), custom_call_target="tpu_custom_call" | custom-call | tf_op jit(solution)/shard_map/attn_bwd/pallas_call | solution.py:847
  504.5 9.3 %all-to-all-start = ((bf16[4,512,1024]{2,1,0:T(8,128)(2,1)}), bf16[4,512,1024]{2,1,0:T(8,128)(2,1)}, u32[]{:S(2)}, u32[]{:S(2)}) async-start(bf16[4,512,1024]{2,1,0:T(8,128)(2,1)} %bitcast.44), calls=%async_computation.3 | async-start | bytes 8388608 | tf_op jit(solution)/shard_map/all_to_all | solution.py:1497
  513.8 44.1 %reduce-scatter.4.cloned.1.call-done = bf16[512,2048]{1,0:T(8,128)(2,1)} async-done(((bf16[4096,2048]{1,0:T(8,128)(2,1)}), bf16[512,2048]{1,0:T(8,128)(2,1)}) %reduce-scatter.4.cloned.1.call-update) | async-done | bytes 2097168 | tf_op jit(solution)/shard_map/reduce_scatter | solution.py:1493
  558.2 28.0 %scatter_tokens.3 = f32[128,2048]{1,0:T(8,128)} custom-call(bf16[8,128,2048]{2,1,0:T(8,128)(2,1)} %get-tuple-element.52.x_ref), custom_call_target="tpu_custom_call" | custom-call | tf_op jit(solution)/shard_map/scatter_tokens/pallas_call | solution.py:305
  586.3 1.6 fusion.8
  589.3 1.4 concatenate.35
  590.7 86.5 %reduce_columns.1 = f32[2,24,256]{2,1,0:T(8,128)} custom-call(f32[8,24,256]{2,1,0:T(8,128)} %bitcast.45), custom_call_target="tpu_custom_call" | custom-call | tf_op jit(solution)/shard_map/reduce_columns/pallas_call | solution.py:392
  677.3 1.3 slice.65
  680.0 5.9 lay_experts.1
  685.9 40.6 %gather_tokens.3.x_ref = bf16[8,512,1024]{2,1,0:T(8,128)(2,1)} custom-call(bf16[512,1024]{1,0:T(8,128)(2,1)} %reduce-scatter.8.cloned.1.call-done.x_ref), custom_call_target="tpu_custom_call" | custom-call | tf_op jit(solution)/shard_map/gather_tokens/pallas_call | solution.py:191
  726.5 10.3 %lay_mixer.1 = (f32[3,512,2048]{2,1,0:T(8,128)}, f32[512,2048]{1,0:T(8,128)}) custom-call(bf16[8,512,1024]{2,1,0:T(8,128)(2,1)} %gather_tokens.3.x_ref), custom_call_target="tpu_custom_call" | custom-call | tf_op jit(solution)/shard_map/lay_mixer/pallas_call | solution.py:885
  736.9 3.2 fusion.7
  740.1 2.0 copy.50
  (106 shorter events, 14.1 us)
Async XLA Ops:
  7.2 215.7 %all-gather.2.cloned.1.call-start = ((), (), s32[]{:S(2)}) async-start(), calls=%async_computation.4 | async-start | bytes 17301504 | tf_op jit(solution)/shard_map/all_gather | solution.py:1447
  96.5 461.5 %reduce-scatter.4.cloned.1.call-start = ((), (), s32[]{:S(2)}) async-start(), calls=%async_computation.5 | async-start | bytes 18874368 | tf_op jit(solution)/shard_map/reduce_scatter | solution.py:1493
  125.2 38.4 %copy-start.16 = (bf16[4,32,512]{2,1,0:T(8,128)(2,1)S(1)}, bf16[4,32,512]{2,1,0:T(8,128)(2,1)}, u32[]{:S(2)}) copy-start(bf16[4,32,512]{2,1,0:T(8,128)(2,1)} %get-tuple-element.38) | copy-start | bytes 393220
  125.3 38.4 %copy-start.4 = (bf16[128,2048]{1,0:T(8,128)(2,1)S(1)}, bf16[128,2048]{1,0:T(8,128)(2,1)}, u32[]{:S(2)}) copy-start(bf16[128,2048]{1,0:T(8,128)(2,1)} %x_ref.1) | copy-start | bytes 1572868
  125.3 40.5 %copy-start.15 = (f32[4,4,512]{2,0,1:T(4,128)S(1)}, f32[4,4,512]{2,0,1:T(4,128)}, u32[]{:S(2)}) copy-start(f32[4,4,512]{2,0,1:T(4,128)} %copy-done.14) | copy-start | bytes 98308
  125.3 42.0 %copy-start.24 = (s32[128,8]{0,1:T(8,128)S(1)}, s32[128,8]{0,1:T(8,128)}, u32[]{:S(2)}) copy-start(s32[128,8]{0,1:T(8,128)} %param.13) | copy-start | bytes 12292
  163.7 4.3 copy-start.12
  167.9 55.0 %copy-start.19 = (f32[128]{0:T(128)}, f32[128]{0:T(128)S(1)}, u32[]{:S(2)}) copy-start(f32[128]{0:T(128)S(1)} %fusion.13) | copy-start | bytes 1540
  422.5 3.0 copy-start.1
  422.5 3.0 copy-start.13
  422.5 3.0 copy-start.22
  422.5 263.4 %reduce-scatter.8.cloned.1.call-start = ((), (), s32[]{:S(2)}) async-start(), calls=%async_computation.7 | async-start | bytes 5242880 | tf_op jit(solution)/shard_map/reduce_scatter | solution.py:1515
  427.2 3.1 copy-start.25
  504.5 53.5 %copy-start.29 = (f32[128]{0:T(128)S(1)}, f32[128]{0:T(128)}, u32[]{:S(2)}) copy-start(f32[128]{0:T(128)} %get-tuple-element.69) | copy-start | bytes 1540
  504.5 175.5 %all-to-all-start = ((bf16[4,512,1024]{2,1,0:T(8,128)(2,1)}), bf16[4,512,1024]{2,1,0:T(8,128)(2,1)}, u32[]{:S(2)}, u32[]{:S(2)}) async-start(bf16[4,512,1024]{2,1,0:T(8,128)(2,1)} %bitcast.44), calls=%async_computation.3 | async-start | bytes 8388608 | tf_op jit(solution)/shard_map/all_to_all | solution.py:1497
  513.8 72.5 %copy-start.5 = (bf16[128,2048]{1,0:T(8,128)(2,1)S(1)}, bf16[128,2048]{1,0:T(8,128)(2,1)}, u32[]{:S(2)}) copy-start(bf16[128,2048]{1,0:T(8,128)(2,1)} %x_ref.1) | copy-start | bytes 1572868
  513.8 223.0 %reduce-scatter.6.cloned.1.call-start = ((), (), s32[]{:S(2)}) async-start(), calls=%async_computation.6 | async-start | bytes 2621440 | tf_op jit(solution)/shard_map/reduce_scatter | solution.py:1494
  558.0 119.3 %copy-start.27 = (f32[128]{0:T(128)}, f32[128]{0:T(128)S(1)}, u32[]{:S(2)}) copy-start(f32[128]{0:T(128)S(1)} %add_rsqrt_fusion) | copy-start | bytes 1540
  726.5 10.3 %copy-start.2 = (f32[128,2048]{1,0:T(8,128)S(1)}, f32[128,2048]{1,0:T(8,128)}, u32[]{:S(2)}) copy-start(f32[128,2048]{1,0:T(8,128)} %scatter_tokens.3) | copy-start | bytes 3145732
  726.5 10.3 %copy-start.6 = (bf16[128,2048]{1,0:T(8,128)(2,1)S(1)}, bf16[128,2048]{1,0:T(8,128)(2,1)}, u32[]{:S(2)}) copy-start(bf16[128,2048]{1,0:T(8,128)(2,1)} %x_ref.1) | copy-start | bytes 1572868
  726.5 10.3 %copy-start.23 = (f32[128]{0:T(128)S(1)}, f32[128]{0:T(128)}, u32[]{:S(2)}) copy-start(f32[128]{0:T(128)} %copy-done.21) | copy-start | bytes 1540
  726.5 10.3 %copy-start.26 = (f32[128]{0:T(128)S(1)}, f32[128]{0:T(128)}, u32[]{:S(2)}) copy-start(f32[128]{0:T(128)} %copy-done.25) | copy-start | bytes 1540
  726.5 10.3 %copy-start.28 = (f32[128]{0:T(128)S(1)}, f32[128]{0:T(128)}, u32[]{:S(2)}) copy-start(f32[128]{0:T(128)} %copy-done.27) | copy-start | bytes 1540
  736.9 3.2 copy-start.7
  (11 other events, 11.5 us)
Sparse Core Ops, SparseCore 0:
  96.6 126.2 all-gather.1
  422.6 135.2 reduce-scatter.3
  560.2 119.9 reduce-scatter.7
  682.3 46.2 reduce-scatter.5

commit v6 on v5

--- a/solution.py
+++ b/solution.py
@@ -326,86 +326,6 @@
     )(parts, *more)[::-1]
 
 
-def reduce_kernel(nz, ne, x_ref, out_ref, got, total, far, send1, recv1, send2, recv2):
-    z, e = lax.axis_index("dp"), lax.axis_index("expert")
-    per = ne // nz
-    meet_all(nz, ne, z, e)
-    first = []
-    for r in range(1, ne):
-        to = lax.rem(e + r, ne)
-        copy = remote(x_ref.at[to], got.at[r], send1.at[r], recv1.at[r], (z, to))
-        copy.start()
-        first.append(copy)
-    acc = x_ref[e]
-    for r, copy in enumerate(first):
-        copy.wait_recv()
-        acc = acc + got[r + 1]
-    total[...] = acc
-    home, place = e // per, lax.rem(e, per)
-    for r in range(ne):
-        to = lax.rem(e + r, ne)
-        copy = remote(total, far.at[z, place], send2.at[r], recv2, (home, to))
-        if r > 0:
-            copy.start()
-        else:
-
-            @pl.when(home != z)
-            def _():
-                copy.start()
-
-            @pl.when(home == z)
-            def _():
-                far[z, place] = total[...]
-
-    for copy in first:
-        copy.wait_send()
-    for r in range(ne):
-        copy = remote(total, far.at[z, place], send2.at[r], recv2, (home, e))
-        if r > 0:
-            copy.wait_send()
-        else:
-
-            @pl.when(home != z)
-            def _():
-                copy.wait_send()
-
-    def arrive(count):
-        flat = got.at[pl.ds(0, count)]
-        remote(flat, flat, send2.at[0], recv2, (z, e)).wait_recv()
-
-    @pl.when(home == z)
-    def _():
-        arrive(nz * per - 1)
-
-    @pl.when(home != z)
-    def _():
-        arrive(nz * per)
-
-    for i in range(per):
-        out_ref[i] = sum(far[k, i] for k in range(nz))
-
-
-def reduce_columns(x, nz, ne, cid):
-    rows, width = x.shape
-    per = ne // nz
-    x = x.reshape(rows, ne, width // ne).transpose(1, 0, 2)
-    out = pl.pallas_call(
-        functools.partial(reduce_kernel, nz, ne),
-        out_shape=jax.ShapeDtypeStruct((per, rows, width // ne), F32),
-        in_specs=[VMEM],
-        out_specs=VMEM,
-        scratch_shapes=[
-            pltpu.VMEM((ne, rows, width // ne), F32),
-            pltpu.VMEM((rows, width // ne), F32),
-            pltpu.VMEM((nz, per, rows, width // ne), F32),
-            DMA((ne,)), DMA((ne,)), DMA((ne,)), DMA,
-        ],
-        compiler_params=pltpu.CompilerParams(collective_id=cid, has_side_effects=True),
-        name="reduce_columns",
-    )(x)
-    return out.transpose(1, 0, 2).reshape(rows, per * (width // ne))
-
-
 def start_kernel(
     nz, ne, x_ref, wqkv_ref, wout_ref, small_ref, seg_ref, _,
     out_ref, wq_ref, wo_ref, small_out, seg_out, _2,
@@ -871,31 +791,332 @@
     )(gab, wq, wo, my_gains, seg, *tables, *saved)
 
 
-def lay_kernel(kinds, hw, x_ref, *outs):
-    for k in range(kinds):
-        piece = x_ref[0, :, k * hw : (k + 1) * hw].astype(F32)
-        if k < kinds - 1:
-            outs[0][k] = piece
+class PlaneScatter:
+    def __init__(self, ne, z, e, x_ref, acc, got, loads, send, recv):
+        self.ne, self.z, self.e = ne, z, e
+        self.x, self.acc, self.got = x_ref, acc, got
+        self.loads, self.send, self.recv = loads, send, recv
+        self.half = acc.shape[2]
+        self.stages = ne.bit_length() - 1
+        self.orders = bit_orders(ne)
+        self.first = [0]
+        for j in range(self.stages):
+            self.first.append(self.first[j] + (ne >> (j + 1)))
+        self.pending, self.arrivals = [], {}
+
+    def push(self, s, j):
+        order = self.orders[s]
+        peer_e = flip(self.e, order[j])
+        rest = self.ne >> (j + 1)
+        for i in range(rest):
+            n = self.first[j] + i
+            if j == 0:
+                block = flips(peer_e, order[:0:-1])[i]
+                src = self.x.at[block, pl.ds(s * self.half, self.half)]
+            else:
+                src = self.acc.at[s, rest + i]
+            copy = remote(
+                src, self.got.at[s, n], self.send.at[s, n], self.recv.at[s, n], (self.z, peer_e)
+            )
+            copy.start()
+            self.pending.append(copy.wait_send)
+            self.arrivals.setdefault((s, j), []).append((copy.wait_recv, i, n))
+
+    def start(self):
+        for s in range(2):
+            self.push(s, 0)
+            for i, block in enumerate(flips(self.e, self.orders[s][:0:-1])):
+                copy = pltpu.make_async_copy(
+                    self.x.at[block, pl.ds(s * self.half, self.half)],
+                    self.acc.at[s, i],
+                    self.loads.at[s, i],
+                )
+                copy.start()
+                self.arrivals.setdefault((s, -1), []).append(copy.wait)
+
+    def stage(self, j):
+        for s in range(2):
+            if j == 0:
+                for wait in self.arrivals.pop((s, -1)):
+                    wait()
+            for wait, i, n in self.arrivals.pop((s, j)):
+                wait()
+                add_rows(self.acc.at[s, i], self.got.at[s, n])
+            if j + 1 < self.stages:
+                self.push(s, j + 1)
+
+    def finish(self):
+        for wait in self.pending:
+            wait()
+
+
+def tail_kernel(
+    nz, ne, kinds, gain_row, parts_ref, gh1_ref, x_ref, gx1_ref, gain_ref, tiny_ref,
+    grad_ref, qkv_ref, out_ref, small_ref,
+    work, below, above, wide, stage, acc, got, gsum, tbuf, tgot, total, far,
+    wload, usend, urecv, dsend, drecv, zsend, zrecv, gsend, grecv, glocal,
+    hload, hsend, hrecv, flush, send1, recv1, send2, recv2,
+):
+    z, e = lax.axis_index("dp"), lax.axis_index("expert")
+    per = ne // nz
+    chunks, rows = work.shape[1], work.shape[2]
+    hw = work.shape[3] // kinds
+    width = x_ref.shape[1]
+    loads = [
+        pltpu.make_async_copy(
+            parts_ref.at[pl.ds((t * chunks + c) * rows, rows)], work.at[t, c], wload.at[t, c]
+        )
+        for c in range(chunks)
+        for t in range(nz)
+    ]
+    for copy in loads:
+        copy.start()
+    meet_all(nz, ne, z, e)
+    mine = PlaneScatter(ne, z, e, gh1_ref, acc, got, hload, hsend, hrecv)
+    mine.start()
+    for copy in loads:
+        copy.wait()
+
+    def rise(t, c):
+        return remote(
+            work.at[t, c], below.at[t, c], usend.at[t, c], urecv.at[t, c], (z + 1, e)
+        )
+
+    def sink(t, c):
+        return remote(
+            work.at[t, c], above.at[t, c], dsend.at[t, c], drecv.at[t, c], (z - 1, e)
+        )
+
+    for c in range(chunks):
+        for t in range(nz - 1, 0, -1):
+
+            @pl.when(z == 0)
+            def _():
+                rise(t, c).start()
+
+        for t in range(nz - 1):
+
+            @pl.when(z == nz - 1)
+            def _():
+                sink(t, c).start()
+
+    def arrive(t, c, buffer, recv):
+        remote(buffer.at[t, c], buffer.at[t, c], usend.at[0, 0], recv.at[t, c], (z, e)).wait_recv()
+        add_rows(work.at[t, c], buffer.at[t, c])
+
+    def line(c):
+        for far_off in range(nz - 1):
+            up, down = nz - 1 - far_off, far_off
+
+            @pl.when((z < up) & (z > 0))
+            def _():
+                arrive(up, c, below, urecv)
+                rise(up, c).start()
+
+            @pl.when((z > down) & (z < nz - 1))
+            def _():
+                arrive(down, c, above, drecv)
+                sink(down, c).start()
+
+        @pl.when(z > 0)
+        def _():
+            arrive(z, c, below, urecv)
+
+        @pl.when(z < nz - 1)
+        def _():
+            arrive(z, c, above, drecv)
+
+    def spread(c):
+        net = PlaneGather(
+            nz, ne, z, e, False, work.at[z, c], wide.at[c], zsend, zrecv,
+            gsend.at[c], grecv.at[c], glocal.at[c],
+        )
+        net.start_round(0)
+        return net
+
+    def outs(c):
+        p = c % 2
+        span = pl.ds(c * rows, rows)
+        return [
+            pltpu.make_async_copy(
+                stage.at[p, j], qkv_ref.at[j, span] if j < kinds - 1 else out_ref.at[span],
+                flush.at[p, j],
+            )
+            for j in range(kinds)
+        ]
+
+    def lay(c, net):
+        net.finish_round(0)
+        net.finish()
+        p = c % 2
+        if c >= 2:
+            for copy in outs(c - 2):
+                copy.wait()
+
+        def column(n, carry):
+            cols = pl.ds(pl.multiple_of(n * hw, hw), hw)
+            for j in range(kinds):
+                stage[p, j, :, cols] = wide[c, n, :, j * hw : (j + 1) * hw].astype(F32)
+            return carry
+
+        lax.fori_loop(0, ne, column, 0)
+        for copy in outs(c):
+            copy.start()
+
+    for j in range(mine.stages):
+        mine.stage(j)
+    line(0)
+    nets = {0: spread(0)}
+
+    half = acc.shape[2]
+    gsum[...] = jnp.zeros_like(gsum)
+    for s in range(2):
+
+        def front(n, carry):
+            here = pl.ds(pl.multiple_of(n * 16, 16), 16)
+            span = pl.ds(pl.multiple_of(s * half + n * 16, 16), 16)
+            grad = acc[s, 0, here, :].astype(F32)
+            x = x_ref[span, :].astype(F32)
+            scale = rms_scale(x)
+            normed = x * scale
+            gsum[...] += grad * normed
+            scaled = grad * gain_ref[:1]
+            inner = jnp.mean(scaled * normed, axis=-1, keepdims=True)
+            grad_ref[span, :] = (gx1_ref[span, :] + scale * (scaled - normed * inner)).astype(BF)
+            return carry
+
+        lax.fori_loop(0, half // 16, front, 0)
+    tbuf[...] = tiny_ref[...]
+    tbuf[gain_row : gain_row + 1, :] = jnp.sum(gsum[...], axis=0, keepdims=True)
+
+    cw = width // ne
+    block = lambda ee: pl.ds(pl.multiple_of(ee * cw, cw), cw)
+    first = []
+    for r in range(1, ne):
+        to = lax.rem(e + r, ne)
+        copy = remote(tbuf.at[:, block(to)], tgot.at[r], send1.at[r], recv1.at[r], (z, to))
+        copy.start()
+        first.append(copy)
+    if chunks > 1:
+        line(1)
+        nets[1] = spread(1)
+    sums = tbuf[:, block(e)]
+    for r, copy in enumerate(first):
+        copy.wait_recv()
+        sums = sums + tgot[r + 1]
+    total[...] = sums
+    home, place = e // per, lax.rem(e, per)
+
+    def give(r):
+        to = lax.rem(e + r, ne)
+        return remote(total, far.at[z, place], send2.at[r], recv2, (home, to))
+
+    for r in range(ne):
+        if r > 0:
+            give(r).start()
         else:
-            outs[1][...] = piece
-
-
-def lay_mixer(wide, kinds, hw):
-    ne, rows, _ = wide.shape
-    return pl.pallas_call(
-        functools.partial(lay_kernel, kinds, hw),
-        grid=(ne,),
-        in_specs=[pl.BlockSpec((1, rows, kinds * hw), lambda i: (i, 0, 0))],
-        out_specs=[
-            pl.BlockSpec((kinds - 1, rows, hw), lambda i: (0, 0, i)),
-            pl.BlockSpec((rows, hw), lambda i: (0, i)),
+
+            @pl.when(home != z)
+            def _():
+                give(0).start()
+
+            @pl.when(home == z)
+            def _():
+                far[z, place] = total[...]
+
+    lay(0, nets.pop(0))
+    for c in range(2, chunks):
+        line(c)
+        nets[c] = spread(c)
+        lay(c - 1, nets.pop(c - 1))
+    if chunks > 1:
+        lay(chunks - 1, nets.pop(chunks - 1))
+    for copy in first:
+        copy.wait_send()
+
+    def arrived(count):
+        flat = tgot.at[pl.ds(0, count)]
+        remote(flat, flat, send2.at[0], recv2, (z, e)).wait_recv()
+
+    for r in range(ne):
+        if r > 0:
+            give(r).wait_send()
+        else:
+
+            @pl.when(home != z)
+            def _():
+                give(0).wait_send()
+                arrived(nz * per)
+
+            @pl.when(home == z)
+            def _():
+                arrived(nz * per - 1)
+
+    for i in range(per):
+        small_ref[i] = sum(far[k, i] for k in range(nz))
+    mine.finish()
+    for c in range(chunks):
+        for t in range(nz):
+
+            @pl.when(z < t)
+            def _():
+                rise(t, c).wait_send()
+
+            @pl.when(z > t)
+            def _():
+                sink(t, c).wait_send()
+
+    for c in range(max(chunks - 2, 0), chunks):
+        for copy in outs(c):
+            copy.wait()
+
+
+def tail(parts, gh1_part, x, gx1, gain_mat, tiny, gain_row, nz, ne, hw, cid):
+    width, total_cols = parts.shape
+    kinds = total_cols // hw
+    count = x.shape[0]
+    depth = width // nz
+    rows = min(128, depth)
+    chunks = depth // rows
+    small_rows, cw = tiny.shape[0], width // ne
+    per = ne // nz
+    block = (nz, chunks, rows, total_cols)
+    out = pl.pallas_call(
+        functools.partial(tail_kernel, nz, ne, kinds, gain_row),
+        out_shape=[
+            jax.ShapeDtypeStruct((count, width), BF),
+            jax.ShapeDtypeStruct((kinds - 1, depth, width), F32),
+            jax.ShapeDtypeStruct((depth, width), F32),
+            jax.ShapeDtypeStruct((per, small_rows, cw), F32),
         ],
-        out_shape=[
-            jax.ShapeDtypeStruct((kinds - 1, rows, ne * hw), F32),
-            jax.ShapeDtypeStruct((rows, ne * hw), F32),
+        in_specs=[ANY, ANY, VMEM, VMEM, VMEM, VMEM],
+        out_specs=[VMEM, ANY, ANY, VMEM],
+        scratch_shapes=[
+            pltpu.VMEM(block, BF), pltpu.VMEM(block, BF), pltpu.VMEM(block, BF),
+            pltpu.VMEM((chunks, ne, rows, total_cols), BF),
+            pltpu.VMEM((2, kinds, rows, width), F32),
+            pltpu.VMEM((2, ne // 2, count // 2, width), BF),
+            pltpu.VMEM((2, ne - 1, count // 2, width), BF),
+            pltpu.VMEM((16, width), F32),
+            pltpu.VMEM((small_rows, width), F32),
+            pltpu.VMEM((max(ne, nz * per), small_rows, cw), F32),
+            pltpu.VMEM((small_rows, cw), F32),
+            pltpu.VMEM((nz, per, small_rows, cw), F32),
+            DMA((nz, chunks)),
+            DMA((nz, chunks)), DMA((nz, chunks)), DMA((nz, chunks)), DMA((nz, chunks)),
+            DMA((nz,)), DMA((nz,)),
+            DMA((chunks, 1, 2, ne - 1)), DMA((chunks, 1, 2, ne - 1)), DMA((chunks,)),
+            DMA((2, ne // 2)), DMA((2, ne - 1)), DMA((2, ne - 1)),
+            DMA((2, kinds)),
+            DMA((ne,)), DMA((ne,)), DMA((ne,)), DMA,
         ],
-        name="lay_mixer",
-    )(wide)
+        compiler_params=pltpu.CompilerParams(
+            collective_id=cid, has_side_effects=True, vmem_limit_bytes=64_000_000
+        ),
+        name="tail",
+    )(parts, gh1_part, x, gx1, gain_mat, tiny)
+    *out, small = out
+    return *out, small.transpose(1, 0, 2).reshape(small_rows, per * cw)
 
 
 def lay_experts_kernel(per_dev, fl, x_ref, gate_ref, up_ref):
@@ -1446,7 +1667,6 @@
 
     g_all = lax.all_gather(cot, both, axis=0, tiled=True)
     inputs_f = inputs.astype(F32)
-    scale_one = rms_scale(inputs_f)
     tables = rope_lanes(length)
     *saved, x1_part = attn_fwd(in_all, wq, wo, gain_mat, my_gains, seg_all, tables, 9)
     (x1_sum,) = scatter_tokens(x1_part, nz, ne, False, 1)
@@ -1512,26 +1732,20 @@
 
     gab_all = gather_tokens(gab, nz, ne, False, 4)
     gh1_part, parts, gain_qk = attn_bwd(gab_all, wq, wo, my_gains, seg_all, tables, saved, 10)
-    mine = lax.psum_scatter(parts, "dp", scatter_dimension=0, tiled=True)
-    (gh1,) = scatter_tokens(gh1_part, nz, ne, False, 5)
-    grad_front, gain_attn = rms_backward(inputs_f, scale_one, gain_mat[0], gh1)
-    grad_inputs = (gx1 + grad_front).astype(BF)
-
-    wide = gather_tokens(mine, nz, ne, False, 6)
-    grad_w_qkv, grad_w_out = lay_mixer(wide, 4, hw)
-    grad_w_qkv = grad_w_qkv.transpose(1, 0, 2)
-
     place = lambda part: lax.dynamic_update_slice_in_dim(
         jnp.zeros((1, width), F32), part[None], e * hw, axis=1
     )
     tiny = jnp.concatenate(
         [
-            local_router, gain_attn[None], place(gain_qk[0]), place(gain_qk[1]), gain_ffn[None],
-            jnp.zeros((-(expert_count + 4) % 8, width), F32),
+            local_router, jnp.zeros((1, width), F32), place(gain_qk[0]), place(gain_qk[1]),
+            gain_ffn[None], jnp.zeros((-(expert_count + 4) % 8, width), F32),
         ],
         axis=0,
     )
-    tiny = reduce_columns(tiny, nz, ne, 7)
+    grad_inputs, grad_w_qkv, grad_w_out, tiny = tail(
+        parts, gh1_part, inputs, gx1, gain_mat, tiny, expert_count, nz, ne, hw, 5
+    )
+    grad_w_qkv = grad_w_qkv.transpose(1, 0, 2)
     grad_w_router = tiny[:expert_count].T
     grad_gains = tiny[expert_count : expert_count + 4].T
     return (

time: 750 us -> 846 us (1.13)
  waiting for transfers between devices: 98 us -> 202 us
  Pallas kernels: 594 us -> 575 us
  local copies, waits for them, and re-layouts: 15.6 us -> 31.2 us
    reduce_scatter x1, waiting for transfers between devices: 44.1 us -> 112 us  [body(): mix = lax.psum_scatter(mix, 'expert', scatter_dimension=0, tiled=True)]
    pallas_call x2 -> x1, Pallas kernels: 96.8 us -> 159 us  [tail(): pl.pallas_call(functools.partial(tail_kernel, nz, ne, kinds, gain_row), o...]
    pallas_call x2 -> x1, Pallas kernels: 64.1 us -> 23.2 us  [gather_tokens(): pl.pallas_call(functools.partial(gather_kernel, nz, ne, spread), out_shap...]
    reduce_scatter x1, waiting for transfers between devices: 0.01 us -> 35.5 us  [body(): mix = lax.psum_scatter(mix, 'dp', scatter_dimension=0, tiled=True)]
    pallas_call x2 -> x1, Pallas kernels: 66.4 us -> 38.3 us  [scatter_tokens(): pl.pallas_call(functools.partial(scatter_kernel, nz, ne, spread), out_sha...]
    unnamed x64 -> x41, local copies, waits for them, and re-layouts: 7.74 us -> 23.3 us
    pallas_call x1, Pallas kernels: 50.6 us -> 38 us  [attn_bwd(): pl.pallas_call(functools.partial(attn_bwd_kernel, ne), out_shape=[jax.Sha...]
  transfers between devices with their start and end apart: 5 -> 4, of which waited for: 2 -> 3; matrix products, arithmetic and copies ran while one was open for 3% -> 1% of each run, Pallas kernels for 41% -> 8%
where the time goes in v6:
time: 846 us; the launch traced here: 844 us
  Pallas kernels  575 us (68%)
  waiting for transfers between devices  202 us (24%)
  local copies, waits for them, and re-layouts  31.2 us (4%)
  between operations  14.1 us (2%)
  other arithmetic  10.1 us (1%)
  starting transfers between devices  9.52 us (1%)
    pallas_call x1, Pallas kernels, moe_net(): pl.pallas_call(functools.partial(moe_net_kernel, nz, ne, per_dev, slots),...  199 us
    pallas_call x1, Pallas kernels, tail(): pl.pallas_call(functools.partial(tail_kernel, nz, ne, kinds, gain_row), o...  159 us
    reduce_scatter x1, waiting for transfers between devices, body(): mix = lax.psum_scatter(mix, 'expert', scatter_dimension=0, tiled=True)  112 us
    pallas_call x1, Pallas kernels, start_gather(): pl.pallas_call(functools.partial(start_kernel, nz, ne), out_shape=[jax.Sh...  84.5 us
    all_gather x1, waiting for transfers between devices, body(): g_all = lax.all_gather(cot, both, axis=0, tiled=True)  54.5 us
    pallas_call x1, Pallas kernels, scatter_tokens(): pl.pallas_call(functools.partial(scatter_kernel, nz, ne, spread), out_sha...  38.3 us
    pallas_call x1, Pallas kernels, attn_bwd(): pl.pallas_call(functools.partial(attn_bwd_kernel, ne), out_shape=[jax.Sha...  38 us
    reduce_scatter x1, waiting for transfers between devices, body(): mix = lax.psum_scatter(mix, 'dp', scatter_dimension=0, tiled=True)  35.5 us
  transfers between devices with their start and end apart: 4, of which 3 were waited for; matrix products, arithmetic and copies ran while one was open for 1% of the time, Pallas kernels for 8%

profile of v6, /device:TPU:0, one launch (start us, length us, event | category | flops | bytes accessed | tf_op | source)
XLA Modules:
  0.0 843.7 jit_solution(1111131640123127451)
XLA Ops:
  7.2 1.9 copy.40._
  9.2 1.4 maximum_maximum_fusion.small_ref
  11.9 84.5 %start_gather.1 = (bf16[8,128,2048]{2,1,0:T(8,128)(2,1)}, bf16[3,2048,256]{2,1,0:T(8,128)(2,1)}, bf16[256,2048]{1,0:T(8,128)(2,1)}, bf16[4,32,512]{2,1,0:T(8,128...) custom-call(bf16[128,2048]{1,0:T(8,128)(2,1)} %x_ref.3, ...), custom_call_target="tpu_custom_call", output_to_operand_aliasing={{5}: (5, {})} | custom-call | tf_op jit(solution)/shard_map/start_gather/pallas_call | solution.py:491
  98.9 26.3 %attn_fwd.1 = (bf16[1024,2048]{1,0:T(8,128)(2,1)}, f32[1024,256]{1,0:T(8,128)}, f32[1024,256]{1,0:T(8,128)}, bf16[1024,256]{1,0:T(8,128)(2,1)}, bf16[1024,256]{1...) custom-call(bf16[8,128,2048]{2,1,0:T(8,128)(2,1)} %get-tuple-element, ...), custom_call_target="tpu_custom_call" | custom-call | tf_op jit(solution)/shard_map/attn_fwd/pallas_call | solution.py:645
  125.3 38.3 %scatter_tokens.1 = f32[128,2048]{1,0:T(8,128)} custom-call(bf16[8,128,2048]{2,1,0:T(8,128)(2,1)} %get-tuple-element.42.x_ref), custom_call_target="tpu_custom_call" | custom-call | tf_op jit(solution)/shard_map/scatter_tokens/pallas_call | solution.py:305
  163.7 1.5 multiply_reduce_fusion.2
  168.4 54.5 %all-gather.2.cloned.1.call-done = bf16[4096,2048]{1,0:T(8,128)(2,1)} async-done(((bf16[128,2048]{1,0:T(8,128)(2,1)}), bf16[4096,2048]{1,0:T(8,128)(2,1)}) %all-gather.2.cloned.1.call-update) | async-done | bytes 16777232 | tf_op jit(solution)/shard_map/all_gather | solution.py:1668
  222.9 199.5 %moe_net.1 = (bf16[32,128,2176]{2,1,0:T(8,128)(2,1)}, bf16[8,4,128,2048]{3,2,1,0:T(8,128)(2,1)}, f32[128,2176]{1,0:T(8,128)}, bf16[2048,1024]{1,0:T(8,128)(2,1)}, f32[512,2048]{1,0:T(8,128)}) custom-call(bf16[128,2176]{1,0:T(8,128)(2,1)} %concatenate.18.h_ref, bf16[32,128,2048]{2,1,0:T(8,128)(2,1)} %bitcast.31, bf16[2,2048,1024]{2,1,0:T(8,128)(2,1)} %wg_ref.1, ...), custom_call_target="tpu_custom_call" | custom-call | tf_op jit(solution)/shard_map/moe_net/pallas_call | solution.py:1620
  422.5 9.4 %all-to-all-start = ((bf16[4,512,1024]{2,1,0:T(8,128)(2,1)}), bf16[4,512,1024]{2,1,0:T(8,128)(2,1)}, u32[]{:S(2)}, u32[]{:S(2)}) async-start(bf16[4,512,1024]{2,1,0:T(8,128)(2,1)} %bitcast.36), calls=%async_computation.2 | async-start | bytes 8388608 | tf_op jit(solution)/shard_map/all_to_all | solution.py:1717
  431.9 111.8 %reduce-scatter.3.cloned.1.call-done = bf16[512,2048]{1,0:T(8,128)(2,1)} async-done(((bf16[4096,2048]{1,0:T(8,128)(2,1)}), bf16[512,2048]{1,0:T(8,128)(2,1)}) %reduce-scatter.3.cloned.1.call-update) | async-done | bytes 2097168 | tf_op jit(solution)/shard_map/reduce_scatter | solution.py:1713
  546.0 1.7 multiply_reduce_fusion
  548.0 6.3 lay_experts.1
  554.2 35.5 %reduce-scatter.5.cloned.1.call-done = bf16[128,2048]{1,0:T(8,128)(2,1)} async-done(((bf16[512,2048]{1,0:T(8,128)(2,1)}), bf16[128,2048]{1,0:T(8,128)(2,1)}) %reduce-scatter.5.cloned.1.call-update) | async-done | bytes 524304 | tf_op jit(solution)/shard_map/reduce_scatter | solution.py:1714
  589.7 2.7 fusion.5
  592.5 23.2 %gather_tokens.1.gab_ref = bf16[8,128,2048]{2,1,0:T(8,128)(2,1)} custom-call(bf16[128,2048]{1,0:T(8,128)(2,1)} %get-tuple-element.67.x_ref), custom_call_target="tpu_custom_call" | custom-call | tf_op jit(solution)/shard_map/gather_tokens/pallas_call | solution.py:191
  615.6 38.0 %attn_bwd.1 = (bf16[8,128,2048]{2,1,0:T(8,128)(2,1)}, bf16[2048,1024]{1,0:T(8,128)(2,1)}, f32[8,256]{1,0:T(8,128)}) custom-call(bf16[8,128,2048]{2,1,0:T(8,128)(2,1)} %gather_tokens.1.gab_ref, bf16[3,2048,256]{2,1,0:T(8,128)(2,1)} %get-tuple-element.38.wq_ref, bf16[256,2048]{1,0:T(8,128)(2,1)} %get-tuple-element.39.wo_ref, ...), custom_call_target="tpu_custom_call" | custom-call | tf_op jit(solution)/shard_map/attn_bwd/pallas_call | solution.py:767
  655.1 1.4 concatenate.19.tiny_ref
  656.4 158.8 %tail.1 = (bf16[128,2048]{1,0:T(8,128)(2,1)}, f32[3,512,2048]{2,1,0:T(8,128)}, f32[512,2048]{1,0:T(8,128)}, f32[2,24,256]{2,1,0:T(8,128)}) custom-call(bf16[2048,1024]{1,0:T(8,128)(2,1)} %get-tuple-element.54.parts_ref, bf16[8,128,2048]{2,1,0:T(8,128)(2,1)} %get-tuple-element.55.gh1_ref, bf16[128,2048]{1,0:T(8,128)(2,1)} %x_ref.3, ...), custom_call_target="tpu_custom_call" | custom-call | tf_op jit(solution)/shard_map/tail/pallas_call | solution.py:1084
  815.9 1.3 slice.59
  817.9 1.9 copy.47
  819.8 11.7 %copy.48 = f32[512,3,2048]{2,0,1:T(8,128)} copy(f32[512,3,2048]{2,0,1:T(8,128)} %bitcast.33) | data formatting | bytes 25165824
  831.5 2.1 copy.49
  833.6 1.6 copy-done.3
  835.2 2.0 copy.50
  (73 shorter events, 12.4 us)
Async XLA Ops:
  7.2 215.7 %all-gather.2.cloned.1.call-start = ((), (), s32[]{:S(2)}) async-start(), calls=%async_computation.3 | async-start | bytes 17301504 | tf_op jit(solution)/shard_map/all_gather | solution.py:1668
  96.5 447.3 %reduce-scatter.3.cloned.1.call-start = ((), (), s32[]{:S(2)}) async-start(), calls=%async_computation.4 | async-start | bytes 18874368 | tf_op jit(solution)/shard_map/reduce_scatter | solution.py:1713
  97.3 1.7 copy-start.12
  125.2 38.4 %copy-start.13 = (bf16[4,32,512]{2,1,0:T(8,128)(2,1)S(1)}, bf16[4,32,512]{2,1,0:T(8,128)(2,1)}, u32[]{:S(2)}) copy-start(bf16[4,32,512]{2,1,0:T(8,128)(2,1)} %get-tuple-element.40) | copy-start | bytes 393220
  125.2 38.4 %copy-start.2 = (bf16[128,2048]{1,0:T(8,128)(2,1)S(1)}, bf16[128,2048]{1,0:T(8,128)(2,1)}, u32[]{:S(2)}) copy-start(bf16[128,2048]{1,0:T(8,128)(2,1)} %x_ref.3) | copy-start | bytes 1572868
  125.2 41.4 %copy-start.16 = (s32[128,8]{0,1:T(8,128)S(1)}, s32[128,8]{0,1:T(8,128)}, u32[]{:S(2)}) copy-start(s32[128,8]{0,1:T(8,128)} %param.13) | copy-start | bytes 12292
  163.7 3.8 copy-start.10
  165.2 1.0 copy-start
  165.2 1.4 copy-start.14
  166.7 0.6 copy-start.6
  166.8 0.6 copy-start.8
  422.4 121.4 %copy-start.7 = (f32[128,16]{1,0:T(8,128)S(1)}, f32[128,16]{1,0:T(8,128)}, u32[]{:S(2)}) copy-start(f32[128,16]{1,0:T(8,128)} %copy-done.6) | copy-start | bytes 24580
  422.4 121.4 %copy-start.9 = (f32[128,16]{1,0:T(8,128)S(1)}, f32[128,16]{1,0:T(8,128)}, u32[]{:S(2)}) copy-start(f32[128,16]{1,0:T(8,128)} %copy-done.8) | copy-start | bytes 24580
  422.4 123.6 %copy-start.1 = (f32[128,2048]{1,0:T(8,128)S(1)}, f32[128,2048]{1,0:T(8,128)}, u32[]{:S(2)}) copy-start(f32[128,2048]{1,0:T(8,128)} %copy-done) | copy-start | bytes 3145732
  422.4 123.6 %copy-start.11 = (bf16[4,2,8,512]{3,2,0,1:T(8,128)(2,1)S(1)}, bf16[4,2,8,512]{3,2,0,1:T(8,128)(2,1)}, u32[]{:S(2)}) copy-start(bf16[4,2,8,512]{3,2,0,1:T(8,128)(2,1)} %copy-done.10) | copy-start | bytes 196612
  422.5 123.6 %copy-start.15 = (f32[128]{0:T(128)S(1)}, f32[128]{0:T(128)}, u32[]{:S(2)}) copy-start(f32[128]{0:T(128)} %copy-done.14) | copy-start | bytes 1540
  422.5 125.5 %all-to-all-start = ((bf16[4,512,1024]{2,1,0:T(8,128)(2,1)}), bf16[4,512,1024]{2,1,0:T(8,128)(2,1)}, u32[]{:S(2)}, u32[]{:S(2)}) async-start(bf16[4,512,1024]{2,1,0:T(8,128)(2,1)} %bitcast.36), calls=%async_computation.2 | async-start | bytes 8388608 | tf_op jit(solution)/shard_map/all_to_all | solution.py:1717
  431.9 157.8 %reduce-scatter.5.cloned.1.call-start = ((), (), s32[]{:S(2)}) async-start(), calls=%async_computation.5 | async-start | bytes 2621440 | tf_op jit(solution)/shard_map/reduce_scatter | solution.py:1714
  544.9 44.8 %copy-start.5 = (bf16[128,2048]{1,0:T(8,128)(2,1)S(1)}, bf16[128,2048]{1,0:T(8,128)(2,1)}, u32[]{:S(2)}) copy-start(bf16[128,2048]{1,0:T(8,128)(2,1)} %param.21) | copy-start | bytes 1572868
  819.8 11.7 %copy-start.4 = (f32[512,2048]{1,0:T(8,128)S(1)}, f32[512,2048]{1,0:T(8,128)}, u32[]{:S(2)}) copy-start(f32[512,2048]{1,0:T(8,128)} %get-tuple-element.94) | copy-start | bytes 12582916
  831.4 3.7 copy-start.3
Sparse Core Ops, SparseCore 0:
  96.6 126.2 all-gather.1
  422.5 121.1 reduce-scatter.2
  546.1 43.6 reduce-scatter.4

commit v7 on v6

--- a/solution.py
+++ b/solution.py
@@ -852,8 +852,8 @@
 
 def tail_kernel(
     nz, ne, kinds, gain_row, parts_ref, gh1_ref, x_ref, gx1_ref, gain_ref, tiny_ref,
-    grad_ref, qkv_ref, out_ref, small_ref,
-    work, below, above, wide, stage, acc, got, gsum, tbuf, tgot, total, far,
+    grad_ref, laid_ref, small_ref,
+    work, below, above, wide, acc, got, gsum, tbuf, tgot, total, far,
     wload, usend, urecv, dsend, drecv, zsend, zrecv, gsend, grecv, glocal,
     hload, hsend, hrecv, flush, send1, recv1, send2, recv2,
 ):
@@ -904,27 +904,23 @@
         remote(buffer.at[t, c], buffer.at[t, c], usend.at[0, 0], recv.at[t, c], (z, e)).wait_recv()
         add_rows(work.at[t, c], buffer.at[t, c])
 
-    def line(c):
-        for far_off in range(nz - 1):
-            up, down = nz - 1 - far_off, far_off
-
-            @pl.when((z < up) & (z > 0))
+    def line(t):
+        for p in range(nz):
+
+            @pl.when(z == p)
             def _():
-                arrive(up, c, below, urecv)
-                rise(up, c).start()
-
-            @pl.when((z > down) & (z < nz - 1))
-            def _():
-                arrive(down, c, above, drecv)
-                sink(down, c).start()
-
-        @pl.when(z > 0)
-        def _():
-            arrive(z, c, below, urecv)
-
-        @pl.when(z < nz - 1)
-        def _():
-            arrive(z, c, above, drecv)
+                c = t - (p - 1)
+                if p > 0 and 0 <= c < chunks:
+                    for target in range(nz - 1, p - 1, -1):
+                        arrive(target, c, below, urecv)
+                        if target > p:
+                            rise(target, c).start()
+                c = t - (nz - 2 - p)
+                if p < nz - 1 and 0 <= c < chunks:
+                    for target in range(p + 1):
+                        arrive(target, c, above, drecv)
+                        if target < p:
+                            sink(target, c).start()
 
     def spread(c):
         net = PlaneGather(
@@ -935,38 +931,41 @@
         return net
 
     def outs(c):
-        p = c % 2
         span = pl.ds(c * rows, rows)
-        return [
-            pltpu.make_async_copy(
-                stage.at[p, j], qkv_ref.at[j, span] if j < kinds - 1 else out_ref.at[span],
-                flush.at[p, j],
-            )
-            for j in range(kinds)
-        ]
+        copies = []
+        for n in range(ne):
+            for j in range(kinds):
+                copies.append(
+                    pltpu.make_async_copy(
+                        wide.at[c, n, :, pl.ds(j * hw, hw)],
+                        laid_ref.at[j, span, pl.ds(n * hw, hw)],
+                        flush.at[c, n, j],
+                    )
+                )
+        return copies
 
     def lay(c, net):
         net.finish_round(0)
         net.finish()
-        p = c % 2
-        if c >= 2:
-            for copy in outs(c - 2):
-                copy.wait()
-
-        def column(n, carry):
-            cols = pl.ds(pl.multiple_of(n * hw, hw), hw)
-            for j in range(kinds):
-                stage[p, j, :, cols] = wide[c, n, :, j * hw : (j + 1) * hw].astype(F32)
-            return carry
-
-        lax.fori_loop(0, ne, column, 0)
         for copy in outs(c):
             copy.start()
 
-    for j in range(mine.stages):
+    mine.stage(0)
+    line(0)
+    for j in range(1, mine.stages):
         mine.stage(j)
-    line(0)
-    nets = {0: spread(0)}
+    line(1)
+    nets = {}
+
+    def advance(t):
+        c = t - max(nz - 2, 0)
+        if 0 <= c < chunks:
+            nets[c] = spread(c)
+        if c - 1 in nets:
+            lay(c - 1, nets.pop(c - 1))
+
+    advance(0)
+    advance(1)
 
     half = acc.shape[2]
     gsum[...] = jnp.zeros_like(gsum)
@@ -997,9 +996,8 @@
         copy = remote(tbuf.at[:, block(to)], tgot.at[r], send1.at[r], recv1.at[r], (z, to))
         copy.start()
         first.append(copy)
-    if chunks > 1:
-        line(1)
-        nets[1] = spread(1)
+    line(2)
+    advance(2)
     sums = tbuf[:, block(e)]
     for r, copy in enumerate(first):
         copy.wait_recv()
@@ -1024,13 +1022,9 @@
             def _():
                 far[z, place] = total[...]
 
-    lay(0, nets.pop(0))
-    for c in range(2, chunks):
-        line(c)
-        nets[c] = spread(c)
-        lay(c - 1, nets.pop(c - 1))
-    if chunks > 1:
-        lay(chunks - 1, nets.pop(chunks - 1))
+    for t in range(3, chunks + nz):
+        line(t)
+        advance(t)
     for copy in first:
         copy.wait_send()
 
@@ -1066,7 +1060,7 @@
             def _():
                 sink(t, c).wait_send()
 
-    for c in range(max(chunks - 2, 0), chunks):
+    for c in range(chunks):
         for copy in outs(c):
             copy.wait()
 
@@ -1085,16 +1079,14 @@
         functools.partial(tail_kernel, nz, ne, kinds, gain_row),
         out_shape=[
             jax.ShapeDtypeStruct((count, width), BF),
-            jax.ShapeDtypeStruct((kinds - 1, depth, width), F32),
-            jax.ShapeDtypeStruct((depth, width), F32),
+            jax.ShapeDtypeStruct((kinds, depth, width), BF),
             jax.ShapeDtypeStruct((per, small_rows, cw), F32),
         ],
         in_specs=[ANY, ANY, VMEM, VMEM, VMEM, VMEM],
-        out_specs=[VMEM, ANY, ANY, VMEM],
+        out_specs=[VMEM, ANY, VMEM],
         scratch_shapes=[
             pltpu.VMEM(block, BF), pltpu.VMEM(block, BF), pltpu.VMEM(block, BF),
             pltpu.VMEM((chunks, ne, rows, total_cols), BF),
-            pltpu.VMEM((2, kinds, rows, width), F32),
             pltpu.VMEM((2, ne // 2, count // 2, width), BF),
             pltpu.VMEM((2, ne - 1, count // 2, width), BF),
             pltpu.VMEM((16, width), F32),
@@ -1107,7 +1099,7 @@
             DMA((nz,)), DMA((nz,)),
             DMA((chunks, 1, 2, ne - 1)), DMA((chunks, 1, 2, ne - 1)), DMA((chunks,)),
             DMA((2, ne // 2)), DMA((2, ne - 1)), DMA((2, ne - 1)),
-            DMA((2, kinds)),
+            DMA((chunks, ne, kinds)),
             DMA((ne,)), DMA((ne,)), DMA((ne,)), DMA,
         ],
         compiler_params=pltpu.CompilerParams(
@@ -1117,6 +1109,16 @@
     )(parts, gh1_part, x, gx1, gain_mat, tiny)
     *out, small = out
     return *out, small.transpose(1, 0, 2).reshape(small_rows, per * cw)
+
+
+def add_kernel(x_ref, y_ref, out_ref):
+    out_ref[...] = (x_ref[...] + y_ref[...].astype(F32)).astype(out_ref.dtype)
+
+
+def add_up(x, y):
+    return pl.pallas_call(
+        add_kernel, out_shape=jax.ShapeDtypeStruct(y.shape, y.dtype), name="add_up"
+    )(x, y)
 
 
 def lay_experts_kernel(per_dev, fl, x_ref, gate_ref, up_ref):
@@ -1176,8 +1178,7 @@
         grad_up.append((gact * silu).astype(BF))
     a = jnp.concatenate(scaled_act, axis=1)
     gin = jnp.concatenate(grad_gate + grad_up, axis=1)
-    blocks, rows = mix_ref.shape[0], mix_ref.shape[2]
-    mix_ref[...] = dot(a, wd_ref[...], NN).astype(BF).reshape(blocks, 1, rows, width)
+    mix_ref[...] = dot(a, wd_ref[...], NN).astype(BF)
     gh_ref[:, :width] = dot(gin, win_ref[...], NT).astype(BF)
     gh_ref[:, width:] = gg.astype(BF)
 
@@ -1195,14 +1196,13 @@
         dwd_ref[...] = acc_d[...]
 
 
-def moe(h_all, g_all, w_in, wd, per_dev, nz, ne, rows_dev, blocks):
+def moe(h_all, g_all, w_in, wd, per_dev, rows_dev, blocks):
     count, width = g_all.shape
     wide = h_all.shape[1]
     hid4 = w_in.shape[1]
     hid2 = wd.shape[0]
     fl = hid2 // per_dev
     tile = blocks * rows_dev
-    turns = ne // blocks
     rows = lambda n: pl.BlockSpec((tile, n), lambda i: (i, 0))
     whole = lambda s: pl.BlockSpec(s, lambda i: (0, 0), pipeline_mode=pl.Buffered(1))
     return pl.pallas_call(
@@ -1213,12 +1213,12 @@
             whole(w_in.shape), whole(wd.shape),
         ],
         out_specs=[
-            pl.BlockSpec((blocks, 1, rows_dev, width), lambda i: (i % turns, i // turns, 0, 0)),
+            rows(width),
             rows(wide),
             whole((width, hid4)), whole((hid2, width)),
         ],
         out_shape=[
-            jax.ShapeDtypeStruct((ne, nz, rows_dev, width), BF),
+            jax.ShapeDtypeStruct((count, width), BF),
             jax.ShapeDtypeStruct((count, wide), BF),
             jax.ShapeDtypeStruct((width, hid4), BF),
             jax.ShapeDtypeStruct((hid2, width), F32),
@@ -1335,7 +1335,7 @@
         p = lax.rem(k, 2)
         return [
             pltpu.make_async_copy(
-                mixbuf.at[p, pl.ds(j * rows, rows)], mix_ref.at[lane, home], mixsem.at[p, j]
+                mixbuf.at[p, pl.ds(j * rows, rows)], mix_ref.at[home * ne + lane], mixsem.at[p, j]
             )
             for j, lane in enumerate((one, two))
         ]
@@ -1621,7 +1621,7 @@
         functools.partial(moe_net_kernel, nz, ne, per_dev, slots),
         out_shape=[
             jax.ShapeDtypeStruct((nz * ne, rows, wide), BF),
-            jax.ShapeDtypeStruct((ne, nz, rows, width), BF),
+            jax.ShapeDtypeStruct((nz * ne, rows, width), BF),
             jax.ShapeDtypeStruct((rows, wide), F32),
             jax.ShapeDtypeStruct((width, 2 * per_dev * fl), BF),
             jax.ShapeDtypeStruct((per_dev * fl, width), F32),
@@ -1698,9 +1698,7 @@
         wu = lax.dynamic_slice_in_dim(w_up, z * fl, fl, axis=2)
         wd = lax.dynamic_slice_in_dim(w_down, z * fl, fl, axis=1).reshape(per_dev * fl, width)
         w_in = jnp.concatenate([*wg, *wu], axis=1)
-        mix, gh, dwin, dwd = moe(
-            h2_all, g_all, w_in, wd, per_dev, nz, ne, count, min(4, ne)
-        )
+        mix, gh, dwin, dwd = moe(h2_all, g_all, w_in, wd, per_dev, count, min(4, ne))
         gh_sum, mix = scatter_tokens(
             gh.reshape(nz * ne, count, wide), nz, ne, True, 3, after=mix.reshape(-1, width)
         )
@@ -1710,9 +1708,8 @@
         + gh_sum[:, width + split : width + split + expert_count]
     )
 
-    mix = lax.psum_scatter(mix, "expert", scatter_dimension=0, tiled=True)
-    mix = lax.psum_scatter(mix, "dp", scatter_dimension=0, tiled=True)
-    output = (x1 + mix.astype(F32)).astype(BF)
+    mix = lax.psum_scatter(mix, both, scatter_dimension=0, tiled=True)
+    output = add_up(x1, mix)
 
     dwin = lax.all_to_all(
         dwin.reshape(nz, width // nz, 2 * per_dev * fl),
@@ -1731,7 +1728,9 @@
     gab = gx1.astype(BF)
 
     gab_all = gather_tokens(gab, nz, ne, False, 4)
-    gh1_part, parts, gain_qk = attn_bwd(gab_all, wq, wo, my_gains, seg_all, tables, saved, 10)
+    gh1_part, parts, gain_qk = attn_bwd(
+        gab_all, wq, wo, my_gains, seg_all, tables, saved, 10
+    )
     place = lambda part: lax.dynamic_update_slice_in_dim(
         jnp.zeros((1, width), F32), part[None], e * hw, axis=1
     )
@@ -1742,10 +1741,11 @@
         ],
         axis=0,
     )
-    grad_inputs, grad_w_qkv, grad_w_out, tiny = tail(
+    grad_inputs, laid, tiny = tail(
         parts, gh1_part, inputs, gx1, gain_mat, tiny, expert_count, nz, ne, hw, 5
     )
-    grad_w_qkv = grad_w_qkv.transpose(1, 0, 2)
+    laid = laid.astype(F32)
+    grad_w_qkv, grad_w_out = laid[:-1].transpose(1, 0, 2), laid[-1]
     grad_w_router = tiny[:expert_count].T
     grad_gains = tiny[expert_count : expert_count + 4].T
     return (

time: 846 us -> 778 us (0.920)
  waiting for transfers between devices: 202 us -> 54.5 us
  Pallas kernels: 575 us -> 638 us
  other arithmetic: 10.1 us -> 20.1 us
    reduce_scatter x2 -> x1, waiting for transfers between devices: 147 us -> 0.01 us  [body(): mix = lax.psum_scatter(mix, both, scatter_dimension=0, tiled=True)]
    pallas_call x1, Pallas kernels: 159 us -> 187 us  [tail(): pl.pallas_call(functools.partial(tail_kernel, nz, ne, kinds, gain_row), o...]
    pallas_call x1, Pallas kernels: 23.2 us -> 40.4 us  [gather_tokens(): pl.pallas_call(functools.partial(gather_kernel, nz, ne, spread), out_shap...]
    pallas_call x1, Pallas kernels: 38 us -> 54.2 us  [attn_bwd(): pl.pallas_call(functools.partial(attn_bwd_kernel, ne), out_shape=[jax.Sha...]
    unnamed x41 -> x39, local copies, waits for them, and re-layouts: 23.3 us -> 8.74 us
    transpose x0 -> x1, local copies, waits for them, and re-layouts: none -> 11.5 us  [body(): grad_w_qkv, grad_w_out = (laid[:-1].transpose(1, 0, 2), laid[-1])]
    convert_element_type x0 -> x1, other arithmetic: none -> 11.3 us  [body(): laid = laid.astype(F32)]
  transfers between devices with their start and end apart: 4 -> 3, of which waited for: 3 -> 1; matrix products, arithmetic and copies ran while one was open for 1% -> 6% of each run, Pallas kernels for 8% -> 46%
where the time goes in v7:
time: 778 us; the launch traced here: 771 us
  Pallas kernels  638 us (82%)
  waiting for transfers between devices  54.5 us (7%)
  local copies, waits for them, and re-layouts  32.1 us (4%)
  other arithmetic  20.1 us (3%)
  between operations  14.4 us (2%)
  starting transfers between devices  9.51 us (1%)
    pallas_call x1, Pallas kernels, moe_net(): pl.pallas_call(functools.partial(moe_net_kernel, nz, ne, per_dev, slots),...  200 us
    pallas_call x1, Pallas kernels, tail(): pl.pallas_call(functools.partial(tail_kernel, nz, ne, kinds, gain_row), o...  187 us
    pallas_call x1, Pallas kernels, start_gather(): pl.pallas_call(functools.partial(start_kernel, nz, ne), out_shape=[jax.Sh...  84.5 us
    all_gather x1, waiting for transfers between devices, body(): g_all = lax.all_gather(cot, both, axis=0, tiled=True)  54.5 us
    pallas_call x1, Pallas kernels, attn_bwd(): pl.pallas_call(functools.partial(attn_bwd_kernel, ne), out_shape=[jax.Sha...  54.2 us
    pallas_call x1, Pallas kernels, gather_tokens(): pl.pallas_call(functools.partial(gather_kernel, nz, ne, spread), out_shap...  40.4 us
    pallas_call x1, Pallas kernels, scatter_tokens(): pl.pallas_call(functools.partial(scatter_kernel, nz, ne, spread), out_sha...  38.3 us
    pallas_call x1, Pallas kernels, attn_fwd(): pl.pallas_call(functools.partial(attn_fwd_kernel, ne), out_shape=[jax.Sha...  26.3 us
  transfers between devices with their start and end apart: 3, of which 1 were waited for; matrix products, arithmetic and copies ran while one was open for 6% of the time, Pallas kernels for 46%

profile of v7, /device:TPU:0, one launch (start us, length us, event | category | flops | bytes accessed | tf_op | source)
XLA Modules:
  0.0 770.9 jit_solution(15455710715873822186)
XLA Ops:
  7.2 1.9 copy.40._
  9.2 1.4 maximum_maximum_fusion.small_ref
  10.6 1.2 reshape.66.seg_ref
  11.9 84.5 %start_gather.1 = (bf16[8,128,2048]{2,1,0:T(8,128)(2,1)}, bf16[3,2048,256]{2,1,0:T(8,128)(2,1)}, bf16[256,2048]{1,0:T(8,128)(2,1)}, bf16[4,32,512]{2,1,0:T(8,128...) custom-call(bf16[128,2048]{1,0:T(8,128)(2,1)} %x_ref.3, ...), custom_call_target="tpu_custom_call", output_to_operand_aliasing={{5}: (5, {})} | custom-call | tf_op jit(solution)/shard_map/start_gather/pallas_call | solution.py:491
  98.9 26.3 %attn_fwd.1 = (bf16[1024,2048]{1,0:T(8,128)(2,1)}, f32[1024,256]{1,0:T(8,128)}, f32[1024,256]{1,0:T(8,128)}, bf16[1024,256]{1,0:T(8,128)(2,1)}, bf16[1024,256]{1...) custom-call(bf16[8,128,2048]{2,1,0:T(8,128)(2,1)} %get-tuple-element, ...), custom_call_target="tpu_custom_call" | custom-call | tf_op jit(solution)/shard_map/attn_fwd/pallas_call | solution.py:645
  125.2 38.3 %scatter_tokens.1 = f32[128,2048]{1,0:T(8,128)} custom-call(bf16[8,128,2048]{2,1,0:T(8,128)(2,1)} %get-tuple-element.41.x_ref), custom_call_target="tpu_custom_call" | custom-call | tf_op jit(solution)/shard_map/scatter_tokens/pallas_call | solution.py:305
  163.7 1.5 multiply_reduce_fusion.2
  168.4 54.5 %all-gather.2.cloned.1.call-done = bf16[4096,2048]{1,0:T(8,128)(2,1)} async-done(((bf16[128,2048]{1,0:T(8,128)(2,1)}), bf16[4096,2048]{1,0:T(8,128)(2,1)}) %all-gather.2.cloned.1.call-update) | async-done | bytes 16777232 | tf_op jit(solution)/shard_map/all_gather | solution.py:1668
  222.9 199.5 %moe_net.1 = (bf16[32,128,2176]{2,1,0:T(8,128)(2,1)}, bf16[32,128,2048]{2,1,0:T(8,128)(2,1)}, f32[128,2176]{1,0:T(8,128)}, bf16[2048,1024]{1,0:T(8,128)(2,1)}, f32[512,2048]{1,0:T(8,128)}) custom-call(bf16[128,2176]{1,0:T(8,128)(2,1)} %concatenate.18.h_ref, bf16[32,128,2048]{2,1,0:T(8,128)(2,1)} %bitcast.35, bf16[2,2048,1024]{2,1,0:T(8,128)(2,1)} %wg_ref.1, ...), custom_call_target="tpu_custom_call" | custom-call | tf_op jit(solution)/shard_map/moe_net/pallas_call | solution.py:1620
  422.5 9.4 %all-to-all-start = ((bf16[4,512,1024]{2,1,0:T(8,128)(2,1)}), bf16[4,512,1024]{2,1,0:T(8,128)(2,1)}, u32[]{:S(2)}, u32[]{:S(2)}) async-start(bf16[4,512,1024]{2,1,0:T(8,128)(2,1)} %bitcast.38), calls=%async_computation.1 | async-start | bytes 8388608 | tf_op jit(solution)/shard_map/all_to_all | solution.py:1714
  432.0 1.1 multiply_reduce_fusion.3
  433.1 1.1 multiply_convert_fusion.1
  434.2 1.7 multiply_reduce_fusion
  435.9 1.5 fusion.5
  437.4 40.4 %gather_tokens.1.gab_ref = bf16[8,128,2048]{2,1,0:T(8,128)(2,1)} custom-call(bf16[128,2048]{1,0:T(8,128)(2,1)} %get-tuple-element.65.x_ref), custom_call_target="tpu_custom_call" | custom-call | tf_op jit(solution)/shard_map/gather_tokens/pallas_call | solution.py:191
  477.8 54.2 %attn_bwd.1 = (bf16[8,128,2048]{2,1,0:T(8,128)(2,1)}, bf16[2048,1024]{1,0:T(8,128)(2,1)}, f32[8,256]{1,0:T(8,128)}) custom-call(bf16[8,128,2048]{2,1,0:T(8,128)(2,1)} %gather_tokens.1.gab_ref, bf16[3,2048,256]{2,1,0:T(8,128)(2,1)} %get-tuple-element.37.wq_ref, bf16[256,2048]{1,0:T(8,128)(2,1)} %get-tuple-element.38.wo_ref, ...), custom_call_target="tpu_custom_call" | custom-call | tf_op jit(solution)/shard_map/attn_bwd/pallas_call | solution.py:767
  533.7 1.4 concatenate.19.tiny_ref
  535.0 186.6 %tail.1 = (bf16[128,2048]{1,0:T(8,128)(2,1)}, bf16[4,512,2048]{2,1,0:T(8,128)(2,1)}, f32[2,24,256]{2,1,0:T(8,128)}) custom-call(bf16[2048,1024]{1,0:T(8,128)(2,1)} %get-tuple-element.53.parts_ref, bf16[8,128,2048]{2,1,0:T(8,128)(2,1)} %get-tuple-element.54.gh1_ref, bf16[128,2048]{1,0:T(8,128)(2,1)} %x_ref.3, f32[128,2048]{1,0:T(8,128)} %get-tuple-element.66.gx1_ref, ...), custom_call_target="tpu_custom_call" | custom-call | tf_op jit(solution)/shard_map/tail/pallas_call | solution.py:1078
  721.6 11.3 %convert_element_type.46 = f32[4,512,2048]{2,1,0:T(8,128)} convert(bf16[4,512,2048]{2,1,0:T(8,128)(2,1)} %get-tuple-element.57) | non-fusion elementwise | flops 4194304 | bytes 25165824 | tf_op jit(solution)/shard_map/convert_element_type | solution.py:1747
  734.1 4.7 slice_bitcast_fusion.1
  738.8 11.5 %slice_bitcast_fusion = f32[512,3,2048]{2,0,1:T(8,128)} fusion(f32[4,512,2048]{2,1,0:T(8,128)} %convert_element_type.46), kind=kLoop, calls=%fused_computation | loop fusion | bytes 25165824 | tf_op jit(solution)/shard_map/transpose | solution.py:1748
  750.3 5.9 lay_experts.1
  756.3 2.2 add_up.1
  759.3 4.7 copy.46
  (72 shorter events, 9.5 us)
Async XLA Ops:
  7.2 215.7 %all-gather.2.cloned.1.call-start = ((), (), s32[]{:S(2)}) async-start(), calls=%async_computation.2 | async-start | bytes 17301504 | tf_op jit(solution)/shard_map/all_gather | solution.py:1668
  96.4 659.9 %reduce-scatter.2.cloned.1.call-start = ((), (), s32[]{:S(2)}) async-start(), calls=%async_computation.3 | async-start | bytes 17301504 | tf_op jit(solution)/shard_map/reduce_scatter | solution.py:1711
  97.3 1.7 copy-start.11
  125.2 38.4 %copy-start.12 = (bf16[4,32,512]{2,1,0:T(8,128)(2,1)S(1)}, bf16[4,32,512]{2,1,0:T(8,128)(2,1)}, u32[]{:S(2)}) copy-start(bf16[4,32,512]{2,1,0:T(8,128)(2,1)} %get-tuple-element.39) | copy-start | bytes 393220
  125.2 38.4 %copy-start.2 = (bf16[128,2048]{1,0:T(8,128)(2,1)S(1)}, bf16[128,2048]{1,0:T(8,128)(2,1)}, u32[]{:S(2)}) copy-start(bf16[128,2048]{1,0:T(8,128)(2,1)} %x_ref.3) | copy-start | bytes 1572868
  125.2 41.4 %copy-start.16 = (s32[128,8]{0,1:T(8,128)S(1)}, s32[128,8]{0,1:T(8,128)}, u32[]{:S(2)}) copy-start(s32[128,8]{0,1:T(8,128)} %param.13) | copy-start | bytes 12292
  163.6 3.8 copy-start.8
  165.1 1.0 copy-start
  165.2 1.4 copy-start.14
  166.7 0.6 copy-start.4
  166.8 0.6 copy-start.6
  422.5 9.5 %copy-start.5 = (f32[128,16]{1,0:T(8,128)S(1)}, f32[128,16]{1,0:T(8,128)}, u32[]{:S(2)}) copy-start(f32[128,16]{1,0:T(8,128)} %copy-done.4) | copy-start | bytes 24580
  422.5 9.5 %copy-start.7 = (f32[128,16]{1,0:T(8,128)S(1)}, f32[128,16]{1,0:T(8,128)}, u32[]{:S(2)}) copy-start(f32[128,16]{1,0:T(8,128)} %copy-done.6) | copy-start | bytes 24580
  422.5 11.7 %copy-start.1 = (f32[128,2048]{1,0:T(8,128)S(1)}, f32[128,2048]{1,0:T(8,128)}, u32[]{:S(2)}) copy-start(f32[128,2048]{1,0:T(8,128)} %copy-done) | copy-start | bytes 3145732
  422.5 11.7 %copy-start.9 = (bf16[4,2,8,512]{3,2,0,1:T(8,128)(2,1)S(1)}, bf16[4,2,8,512]{3,2,0,1:T(8,128)(2,1)}, u32[]{:S(2)}) copy-start(bf16[4,2,8,512]{3,2,0,1:T(8,128)(2,1)} %copy-done.8) | copy-start | bytes 196612
  422.5 11.7 %copy-start.15 = (f32[128]{0:T(128)S(1)}, f32[128]{0:T(128)}, u32[]{:S(2)}) copy-start(f32[128]{0:T(128)} %copy-done.14) | copy-start | bytes 1540
  422.5 13.4 %copy-start.3 = (bf16[128,2048]{1,0:T(8,128)(2,1)S(1)}, bf16[128,2048]{1,0:T(8,128)(2,1)}, u32[]{:S(2)}) copy-start(bf16[128,2048]{1,0:T(8,128)(2,1)} %param.21) | copy-start | bytes 1572868
  422.5 327.8 %all-to-all-start = ((bf16[4,512,1024]{2,1,0:T(8,128)(2,1)}), bf16[4,512,1024]{2,1,0:T(8,128)(2,1)}, u32[]{:S(2)}, u32[]{:S(2)}) async-start(bf16[4,512,1024]{2,1,0:T(8,128)(2,1)} %bitcast.38), calls=%async_computation.1 | async-start | bytes 8388608 | tf_op jit(solution)/shard_map/all_to_all | solution.py:1714
  721.6 11.3 %copy-start.13 = (f32[2,24,256]{2,1,0:T(8,128)S(1)}, f32[2,24,256]{2,1,0:T(8,128)}, u32[]{:S(2)}) copy-start(f32[2,24,256]{2,1,0:T(8,128)} %get-tuple-element.58) | copy-start | bytes 147460
  750.3 8.2 %copy-start.10 = (bf16[128,2048]{1,0:T(8,128)(2,1)S(1)}, bf16[128,2048]{1,0:T(8,128)(2,1)}, u32[]{:S(2)}) copy-start(bf16[128,2048]{1,0:T(8,128)(2,1)} %get-tuple-element.89) | copy-start | bytes 1572868
Sparse Core Ops, SparseCore 0:
  96.6 126.2 all-gather.1
  422.6 284.0 reduce-scatter.1

commit v8 on v7

--- a/solution.py
+++ b/solution.py
@@ -208,87 +208,139 @@
     lax.fori_loop(0, dst.shape[0] // tile, step, 0)
 
 
-def scatter_kernel(nz, ne, spread, x_ref, *refs):
-    out_ref, acc, got, zgot, loads, send, recv, zsend, zrecv = refs[-9:]
-    z, e = lax.axis_index("dp"), lax.axis_index("expert")
-    meet_column_and_plane(nz, ne, z, e, spread)
-    rounds = nz if spread else 1
-    stages = ne.bit_length() - 1
-    half = out_ref.shape[0] // 2
-    orders = bit_orders(ne)
-    pending, arrivals, zwait = [], {}, {}
-    ranks = list(range(1, rounds)) + [0]
-    first = [0] * (stages + 1)
-    for j in range(stages):
-        first[j + 1] = first[j] + (ne >> (j + 1))
-
-    def plane_of(r):
-        return lax.rem(z + r, nz) * ne if spread else 0
-
-    def push(r, s, j):
-        order = orders[s]
-        peer = (z, flip(e, order[j]))
-        rest = ne >> (j + 1)
+class TokenScatter:
+    def __init__(self, nz, ne, z, e, spread, x_ref, acc, got, zgot, loads, send, recv, zsend, zrecv):
+        self.nz, self.ne, self.z, self.e, self.spread = nz, ne, z, e, spread
+        self.x, self.acc, self.got, self.zgot = x_ref, acc, got, zgot
+        self.loads, self.send, self.recv, self.zsend, self.zrecv = loads, send, recv, zsend, zrecv
+        self.rounds = nz if spread else 1
+        self.stages = ne.bit_length() - 1
+        self.steps = self.rounds + self.stages - 1
+        self.half = acc.shape[3]
+        self.orders = bit_orders(ne)
+        self.ranks = list(range(1, self.rounds)) + [0]
+        self.first = [0]
+        for j in range(self.stages):
+            self.first.append(self.first[j] + (ne >> (j + 1)))
+        self.pending, self.arrivals, self.zwait = [], {}, {}
+
+    def block(self, r, ee):
+        home = lax.rem(self.z + r, self.nz) * self.ne if self.spread else 0
+        return home + ee
+
+    def push(self, r, s, j):
+        order = self.orders[s]
+        peer_e = flip(self.e, order[j])
+        rest = self.ne >> (j + 1)
         for i in range(rest):
-            n = first[j] + i
+            n = self.first[j] + i
             if j == 0:
-                block = flips(peer[1], order[:0:-1])[i]
-                src = x_ref.at[plane_of(r) + block, pl.ds(s * half, half)]
+                ee = flips(peer_e, order[:0:-1])[i]
+                src = self.x.at[self.block(r, ee), pl.ds(s * self.half, self.half)]
             else:
-                src = acc.at[r, s, rest + i]
-            copy = remote(src, got.at[r, s, n], send.at[r, s, n], recv.at[r, s, n], peer)
+                src = self.acc.at[r, s, rest + i]
+            copy = remote(
+                src, self.got.at[r, s, n], self.send.at[r, s, n], self.recv.at[r, s, n],
+                (self.z, peer_e),
+            )
             copy.start()
-            pending.append(copy.wait_send)
-            arrivals.setdefault((r, s, j), []).append((copy.wait_recv, i, n))
-
-    for r in ranks:
-        for s in range(2):
-            push(r, s, 0)
-            for i, block in enumerate(flips(e, orders[s][:0:-1])):
-                copy = pltpu.make_async_copy(
-                    x_ref.at[plane_of(r) + block, pl.ds(s * half, half)],
-                    acc.at[r, s, i],
-                    loads.at[r, s, i],
-                )
-                copy.start()
-                arrivals.setdefault((r, s, -1), []).append(copy.wait)
-    for t in range(rounds + stages):
-        for place, r in enumerate(ranks):
+            self.pending.append(copy.wait_send)
+            self.arrivals.setdefault((r, s, j), []).append((copy.wait_recv, i, n))
+
+    def start(self):
+        for r in self.ranks:
+            for s in range(2):
+                self.push(r, s, 0)
+                for i, ee in enumerate(flips(self.e, self.orders[s][:0:-1])):
+                    copy = pltpu.make_async_copy(
+                        self.x.at[self.block(r, ee), pl.ds(s * self.half, self.half)],
+                        self.acc.at[r, s, i],
+                        self.loads.at[r, s, i],
+                    )
+                    copy.start()
+                    self.arrivals.setdefault((r, s, -1), []).append(copy.wait)
+
+    def step(self, t):
+        for place, r in enumerate(self.ranks):
             j = t - place
-            if not 0 <= j < stages:
+            if not 0 <= j < self.stages:
                 continue
             for s in range(2):
                 if j == 0:
-                    for wait in arrivals.pop((r, s, -1)):
+                    for wait in self.arrivals.pop((r, s, -1)):
                         wait()
-                for wait, i, n in arrivals.pop((r, s, j)):
+                for wait, i, n in self.arrivals.pop((r, s, j)):
                     wait()
-                    add_rows(acc.at[r, s, i], got.at[r, s, n])
-                if j + 1 < stages:
-                    push(r, s, j + 1)
+                    add_rows(self.acc.at[r, s, i], self.got.at[r, s, n])
+                if j + 1 < self.stages:
+                    self.push(r, s, j + 1)
                 elif r > 0:
                     copy = remote(
-                        acc.at[r, s, 0], zgot.at[r, s], zsend.at[r, s], zrecv.at[r, s],
-                        (lax.rem(z + r, nz), e),
+                        self.acc.at[r, s, 0], self.zgot.at[r, s],
+                        self.zsend.at[r, s], self.zrecv.at[r, s],
+                        (lax.rem(self.z + r, self.nz), self.e),
                     )
                     copy.start()
-                    pending.append(copy.wait_send)
-                    zwait[(r, s)] = copy.wait_recv
+                    self.pending.append(copy.wait_send)
+                    self.zwait[(r, s)] = copy.wait_recv
+
+    def arrive(self):
+        for wait in self.zwait.values():
+            wait()
+
+    def rows(self, s, here):
+        total = self.acc[0, s, 0, here, :].astype(F32)
+        for r in range(1, self.rounds):
+            total = total + self.zgot[r, s, here, :].astype(F32)
+        return total
+
+    def finish(self):
+        for wait in self.pending:
+            wait()
+
+    @staticmethod
+    def scratch(nz, ne, spread, count, width):
+        rounds = nz if spread else 1
+        half = count // 2
+        return [
+            pltpu.VMEM((rounds, 2, ne // 2, half, width), BF),
+            pltpu.VMEM((rounds, 2, ne - 1, half, width), BF),
+            pltpu.VMEM((nz if spread else 1, 2, half, width), BF),
+            DMA((rounds, 2, ne // 2)),
+            DMA((rounds, 2, ne - 1)),
+            DMA((rounds, 2, ne - 1)),
+            DMA((nz, 2)),
+            DMA((nz, 2)),
+        ]
+
+
+def over_rows(half, act, tile=16):
     for s in range(2):
-        for r in range(1, rounds):
-            zwait[(r, s)]()
-
-        def step(i, carry):
-            rows = pl.ds(pl.multiple_of(i * 16, 16), 16)
-            total = acc[0, s, 0, rows, :].astype(F32)
-            for r in range(1, rounds):
-                total = total + zgot[r, s, rows, :].astype(F32)
-            out_ref[pl.ds(pl.multiple_of(s * half + i * 16, 16), 16), :] = total.astype(out_ref.dtype)
+
+        def step(n, carry):
+            here = pl.ds(pl.multiple_of(n * tile, tile), tile)
+            span = pl.ds(pl.multiple_of(s * half + n * tile, tile), tile)
+            act(s, here, span)
             return carry
 
-        lax.fori_loop(0, half // 16, step, 0)
-    for wait in pending:
-        wait()
+        lax.fori_loop(0, half // tile, step, 0)
+
+
+def scatter_kernel(nz, ne, spread, x_ref, *refs):
+    out_ref, *rest = refs[-9:]
+    z, e = lax.axis_index("dp"), lax.axis_index("expert")
+    meet_column_and_plane(nz, ne, z, e, spread)
+    net = TokenScatter(nz, ne, z, e, spread, x_ref, *rest)
+    net.start()
+    for t in range(net.steps):
+        net.step(t)
+    net.arrive()
+
+    def write(s, here, span):
+        out_ref[span, :] = net.rows(s, here)
+
+    over_rows(net.half, write)
+    net.finish()
 
 
 def scatter_tokens(parts, nz, ne, spread, cid, after=None):
@@ -308,16 +360,7 @@
         + [jax.ShapeDtypeStruct((count, width), F32)],
         in_specs=[ANY] * (1 + len(more)),
         out_specs=[ANY] * len(more) + [VMEM],
-        scratch_shapes=[
-            pltpu.VMEM((rounds, 2, ne // 2, half, width), BF),
-            pltpu.VMEM((rounds, 2, ne - 1, half, width), BF),
-            pltpu.VMEM((nz, 2, half, width), BF),
-            DMA((rounds, 2, ne // 2)),
-            DMA((rounds, 2, ne - 1)),
-            DMA((rounds, 2, ne - 1)),
-            DMA((nz, 2)),
-            DMA((nz, 2)),
-        ],
+        scratch_shapes=TokenScatter.scratch(nz, ne, spread, count, width),
         input_output_aliases={1: 0} if more else {},
         compiler_params=pltpu.CompilerParams(
             collective_id=cid, has_side_effects=True, vmem_limit_bytes=64_000_000
@@ -327,9 +370,9 @@
 
 
 def start_kernel(
-    nz, ne, x_ref, wqkv_ref, wout_ref, small_ref, seg_ref, _,
-    out_ref, wq_ref, wo_ref, small_out, seg_out, _2,
-    wbuf, pbuf, zsend, zrecv, send, recv, local,
+    nz, ne, x_ref, wqkv_ref, wout_ref, small_ref, seg_ref, cot_ref,
+    out_ref, wq_ref, wo_ref, small_out, seg_out, cot_out,
+    wbuf, pbuf, zsend, zrecv, send, recv, local, czsend, czrecv, csend, crecv, clocal,
     up_send, up_recv, dn_send, dn_recv, wload, wkeep, pload, psend, precv, pkeep,
     small_send, small_recv, seg_send, seg_recv,
 ):
@@ -351,6 +394,10 @@
     for copy in pieces:
         copy.start()
     meet_all(nz, ne, z, e)
+    cot = PlaneGather(
+        nz, ne, z, e, True, cot_ref, cot_out, czsend, czrecv, csend, crecv, clocal
+    )
+    cot.spread_own()
 
     def rows_of(zz):
         return pl.ds(pl.multiple_of(zz * depth, depth), depth)
@@ -415,7 +462,10 @@
                 def _():
                     give.start()
     net.finish_round(0)
+    cot.start_round(0)
     for dist in range(1, nz):
+        cot.start_round(dist)
+        cot.finish_round(dist - 1)
         for j in range(kinds):
 
             @pl.when(z - dist >= 0)
@@ -438,6 +488,8 @@
                     if dist + 1 < nz:
                         hop(j, z + dist, dist + 1, False).start()
 
+    cot.finish_round(nz - 1)
+    cot.finish()
     net.finish()
     for keep in keeps:
         keep.wait()
@@ -485,7 +537,7 @@
     wait_all(seg_out, seg_send, seg_recv, ne - 1)
 
 
-def start_gather(x, w_qkv, w_out, small, seg, after, nz, ne, hw, cid):
+def start_gather(x, w_qkv, w_out, small, seg, cot, nz, ne, hw, cid):
     kinds, depth, width = w_qkv.shape
     per = ne // nz
     return pl.pallas_call(
@@ -496,22 +548,22 @@
             jax.ShapeDtypeStruct((hw, width), BF),
             jax.ShapeDtypeStruct((nz, *small.shape), small.dtype),
             jax.ShapeDtypeStruct((ne, *seg.shape), seg.dtype),
-            jax.ShapeDtypeStruct(after.shape, after.dtype),
+            jax.ShapeDtypeStruct((nz * ne, *cot.shape), cot.dtype),
         ],
-        in_specs=[VMEM, ANY, ANY, VMEM, VMEM, ANY],
+        in_specs=[VMEM, ANY, ANY, VMEM, VMEM, VMEM],
         out_specs=[ANY, ANY, ANY, VMEM, VMEM, ANY],
-        input_output_aliases={5: 5},
         scratch_shapes=[
             pltpu.VMEM((kinds, depth, hw), BF),
             pltpu.VMEM((per, hw, hw), BF),
             *PlaneGather.scratch(nz, ne, False),
+            *PlaneGather.scratch(nz, ne, True),
             DMA((nz, kinds)), DMA((nz, kinds)), DMA((nz, kinds)), DMA((nz, kinds)),
             DMA((kinds,)), DMA((kinds,)), DMA((per,)), DMA((nz, per)), DMA, DMA,
             DMA, DMA, DMA, DMA,
         ],
         compiler_params=pltpu.CompilerParams(collective_id=cid, has_side_effects=True),
         name="start_gather",
-    )(x, w_qkv, w_out, small, seg, after)
+    )(x, w_qkv, w_out, small, seg, cot)
 
 
 def rope_lanes(length):
@@ -791,71 +843,12 @@
     )(gab, wq, wo, my_gains, seg, *tables, *saved)
 
 
-class PlaneScatter:
-    def __init__(self, ne, z, e, x_ref, acc, got, loads, send, recv):
-        self.ne, self.z, self.e = ne, z, e
-        self.x, self.acc, self.got = x_ref, acc, got
-        self.loads, self.send, self.recv = loads, send, recv
-        self.half = acc.shape[2]
-        self.stages = ne.bit_length() - 1
-        self.orders = bit_orders(ne)
-        self.first = [0]
-        for j in range(self.stages):
-            self.first.append(self.first[j] + (ne >> (j + 1)))
-        self.pending, self.arrivals = [], {}
-
-    def push(self, s, j):
-        order = self.orders[s]
-        peer_e = flip(self.e, order[j])
-        rest = self.ne >> (j + 1)
-        for i in range(rest):
-            n = self.first[j] + i
-            if j == 0:
-                block = flips(peer_e, order[:0:-1])[i]
-                src = self.x.at[block, pl.ds(s * self.half, self.half)]
-            else:
-                src = self.acc.at[s, rest + i]
-            copy = remote(
-                src, self.got.at[s, n], self.send.at[s, n], self.recv.at[s, n], (self.z, peer_e)
-            )
-            copy.start()
-            self.pending.append(copy.wait_send)
-            self.arrivals.setdefault((s, j), []).append((copy.wait_recv, i, n))
-
-    def start(self):
-        for s in range(2):
-            self.push(s, 0)
-            for i, block in enumerate(flips(self.e, self.orders[s][:0:-1])):
-                copy = pltpu.make_async_copy(
-                    self.x.at[block, pl.ds(s * self.half, self.half)],
-                    self.acc.at[s, i],
-                    self.loads.at[s, i],
-                )
-                copy.start()
-                self.arrivals.setdefault((s, -1), []).append(copy.wait)
-
-    def stage(self, j):
-        for s in range(2):
-            if j == 0:
-                for wait in self.arrivals.pop((s, -1)):
-                    wait()
-            for wait, i, n in self.arrivals.pop((s, j)):
-                wait()
-                add_rows(self.acc.at[s, i], self.got.at[s, n])
-            if j + 1 < self.stages:
-                self.push(s, j + 1)
-
-    def finish(self):
-        for wait in self.pending:
-            wait()
-
-
 def tail_kernel(
-    nz, ne, kinds, gain_row, parts_ref, gh1_ref, x_ref, gx1_ref, gain_ref, tiny_ref,
-    grad_ref, laid_ref, small_ref,
-    work, below, above, wide, acc, got, gsum, tbuf, tgot, total, far,
+    nz, ne, kinds, gain_row, with_mix, parts_ref, gh1_ref, mix_ref, x_ref, x1_ref, gx1_ref,
+    gain_ref, tiny_ref, grad_ref, laid_ref, small_ref, out_ref,
+    work, below, above, wide, gsum, tbuf, tgot, total, far,
     wload, usend, urecv, dsend, drecv, zsend, zrecv, gsend, grecv, glocal,
-    hload, hsend, hrecv, flush, send1, recv1, send2, recv2,
+    flush, send1, recv1, send2, recv2, *nets_scratch,
 ):
     z, e = lax.axis_index("dp"), lax.axis_index("expert")
     per = ne // nz
@@ -872,8 +865,11 @@
     for copy in loads:
         copy.start()
     meet_all(nz, ne, z, e)
-    mine = PlaneScatter(ne, z, e, gh1_ref, acc, got, hload, hsend, hrecv)
+    mine = TokenScatter(nz, ne, z, e, False, gh1_ref, *nets_scratch[:8])
     mine.start()
+    if with_mix:
+        mix = TokenScatter(nz, ne, z, e, True, mix_ref, *nets_scratch[8:])
+        mix.start()
     for copy in loads:
         copy.wait()
 
@@ -950,10 +946,16 @@
         for copy in outs(c):
             copy.start()
 
-    mine.stage(0)
+    def mix_step(t):
+        if with_mix and t < mix.steps:
+            mix.step(t)
+
+    mine.step(0)
+    mix_step(0)
     line(0)
     for j in range(1, mine.stages):
-        mine.stage(j)
+        mine.step(j)
+    mix_step(1)
     line(1)
     nets = {}
 
@@ -967,24 +969,19 @@
     advance(0)
     advance(1)
 
-    half = acc.shape[2]
     gsum[...] = jnp.zeros_like(gsum)
-    for s in range(2):
-
-        def front(n, carry):
-            here = pl.ds(pl.multiple_of(n * 16, 16), 16)
-            span = pl.ds(pl.multiple_of(s * half + n * 16, 16), 16)
-            grad = acc[s, 0, here, :].astype(F32)
-            x = x_ref[span, :].astype(F32)
-            scale = rms_scale(x)
-            normed = x * scale
-            gsum[...] += grad * normed
-            scaled = grad * gain_ref[:1]
-            inner = jnp.mean(scaled * normed, axis=-1, keepdims=True)
-            grad_ref[span, :] = (gx1_ref[span, :] + scale * (scaled - normed * inner)).astype(BF)
-            return carry
-
-        lax.fori_loop(0, half // 16, front, 0)
+
+    def front(s, here, span):
+        grad = mine.rows(s, here)
+        x = x_ref[span, :].astype(F32)
+        scale = rms_scale(x)
+        normed = x * scale
+        gsum[...] += grad * normed
+        scaled = grad * gain_ref[:1]
+        inner = jnp.mean(scaled * normed, axis=-1, keepdims=True)
+        grad_ref[span, :] = (gx1_ref[span, :] + scale * (scaled - normed * inner)).astype(BF)
+
+    over_rows(mine.half, front)
     tbuf[...] = tiny_ref[...]
     tbuf[gain_row : gain_row + 1, :] = jnp.sum(gsum[...], axis=0, keepdims=True)
 
@@ -996,6 +993,7 @@
         copy = remote(tbuf.at[:, block(to)], tgot.at[r], send1.at[r], recv1.at[r], (z, to))
         copy.start()
         first.append(copy)
+    mix_step(2)
     line(2)
     advance(2)
     sums = tbuf[:, block(e)]
@@ -1022,9 +1020,20 @@
             def _():
                 far[z, place] = total[...]
 
-    for t in range(3, chunks + nz):
+    for t in range(3, max(chunks + nz, mix.steps if with_mix else 0)):
+        mix_step(t)
         line(t)
         advance(t)
+    if with_mix:
+        mix.arrive()
+
+        def finish_output(s, here, span):
+            out_ref[span, :] = (x1_ref[span, :] + mix.rows(s, here)).astype(BF)
+
+        over_rows(mix.half, finish_output)
+        mix.finish()
+    else:
+        out_ref[...] = jnp.zeros_like(out_ref)
     for copy in first:
         copy.wait_send()
 
@@ -1065,7 +1074,7 @@
             copy.wait()
 
 
-def tail(parts, gh1_part, x, gx1, gain_mat, tiny, gain_row, nz, ne, hw, cid):
+def tail(parts, gh1_part, mix, x, x1, gx1, gain_mat, tiny, gain_row, nz, ne, hw, cid):
     width, total_cols = parts.shape
     kinds = total_cols // hw
     count = x.shape[0]
@@ -1075,20 +1084,23 @@
     small_rows, cw = tiny.shape[0], width // ne
     per = ne // nz
     block = (nz, chunks, rows, total_cols)
-    out = pl.pallas_call(
-        functools.partial(tail_kernel, nz, ne, kinds, gain_row),
+    with_mix = mix is not None
+    scratch = TokenScatter.scratch(nz, ne, False, count, width)
+    if with_mix:
+        scratch += TokenScatter.scratch(nz, ne, True, count, width)
+    grad, laid, small, output = pl.pallas_call(
+        functools.partial(tail_kernel, nz, ne, kinds, gain_row, with_mix),
         out_shape=[
             jax.ShapeDtypeStruct((count, width), BF),
             jax.ShapeDtypeStruct((kinds, depth, width), BF),
             jax.ShapeDtypeStruct((per, small_rows, cw), F32),
+            jax.ShapeDtypeStruct((count, width), BF),
         ],
-        in_specs=[ANY, ANY, VMEM, VMEM, VMEM, VMEM],
-        out_specs=[VMEM, ANY, VMEM],
+        in_specs=[ANY, ANY, ANY, VMEM, VMEM, VMEM, VMEM, VMEM],
+        out_specs=[VMEM, ANY, VMEM, VMEM],
         scratch_shapes=[
             pltpu.VMEM(block, BF), pltpu.VMEM(block, BF), pltpu.VMEM(block, BF),
             pltpu.VMEM((chunks, ne, rows, total_cols), BF),
-            pltpu.VMEM((2, ne // 2, count // 2, width), BF),
-            pltpu.VMEM((2, ne - 1, count // 2, width), BF),
             pltpu.VMEM((16, width), F32),
             pltpu.VMEM((small_rows, width), F32),
             pltpu.VMEM((max(ne, nz * per), small_rows, cw), F32),
@@ -1098,17 +1110,17 @@
             DMA((nz, chunks)), DMA((nz, chunks)), DMA((nz, chunks)), DMA((nz, chunks)),
             DMA((nz,)), DMA((nz,)),
             DMA((chunks, 1, 2, ne - 1)), DMA((chunks, 1, 2, ne - 1)), DMA((chunks,)),
-            DMA((2, ne // 2)), DMA((2, ne - 1)), DMA((2, ne - 1)),
             DMA((chunks, ne, kinds)),
             DMA((ne,)), DMA((ne,)), DMA((ne,)), DMA,
+            *scratch,
         ],
         compiler_params=pltpu.CompilerParams(
-            collective_id=cid, has_side_effects=True, vmem_limit_bytes=64_000_000
+            collective_id=cid, has_side_effects=True, vmem_limit_bytes=66_000_000
         ),
         name="tail",
-    )(parts, gh1_part, x, gx1, gain_mat, tiny)
-    *out, small = out
-    return *out, small.transpose(1, 0, 2).reshape(small_rows, per * cw)
+    )(parts, gh1_part, mix if with_mix else gh1_part, x, x1, gx1, gain_mat, tiny)
+    small = small.transpose(1, 0, 2).reshape(small_rows, per * cw)
+    return grad, laid, small, output
 
 
 def add_kernel(x_ref, y_ref, out_ref):
@@ -1656,7 +1668,7 @@
         [w_router.T, gains.T, jnp.zeros((pad, gains.shape[0]), BF)], axis=0
     )
     seg8 = jnp.broadcast_to(segments[:, None, :], (num_seqs, 8, length)).reshape(-1, length)
-    in_all, wq, wo, small, seg_all, cot = start_gather(
+    in_all, wq, wo, small, seg_all, g_all = start_gather(
         inputs, w_qkv.transpose(1, 0, 2), w_out, small, seg8, cotangent, nz, ne, hw, 0
     )
     small = small.transpose(1, 0, 2).reshape(-1, width)
@@ -1665,7 +1677,7 @@
     my_gains = lax.dynamic_slice_in_dim(gain_mat, e * hw, hw, axis=1)
     seg_all = seg_all.reshape(ne * num_seqs, 8, length)
 
-    g_all = lax.all_gather(cot, both, axis=0, tiled=True)
+    g_all = g_all.reshape(-1, width)
     inputs_f = inputs.astype(F32)
     tables = rope_lanes(length)
     *saved, x1_part = attn_fwd(in_all, wq, wo, gain_mat, my_gains, seg_all, tables, 9)
@@ -1708,9 +1720,6 @@
         + gh_sum[:, width + split : width + split + expert_count]
     )
 
-    mix = lax.psum_scatter(mix, both, scatter_dimension=0, tiled=True)
-    output = add_up(x1, mix)
-
     dwin = lax.all_to_all(
         dwin.reshape(nz, width // nz, 2 * per_dev * fl),
         "dp", split_axis=0, concat_axis=0, tiled=True,
@@ -1741,11 +1750,15 @@
         ],
         axis=0,
     )
-    grad_inputs, laid, tiny = tail(
-        parts, gh1_part, inputs, gx1, gain_mat, tiny, expert_count, nz, ne, hw, 5
+    grad_inputs, laid, tiny, output = tail(
+        parts, gh1_part, mix.reshape(-1, count, width) if fits else None, inputs, x1, gx1,
+        gain_mat, tiny, expert_count, nz, ne, hw, 5,
     )
-    laid = laid.astype(F32)
-    grad_w_qkv, grad_w_out = laid[:-1].transpose(1, 0, 2), laid[-1]
+    if not fits:
+        mix = lax.psum_scatter(mix, both, scatter_dimension=0, tiled=True)
+        output = add_up(x1, mix)
+    grad_w_qkv = laid[:-1].astype(F32).transpose(1, 0, 2)
+    grad_w_out = laid[-1].astype(F32)
     grad_w_router = tiny[:expert_count].T
     grad_gains = tiny[expert_count : expert_count + 4].T
     return (

time: 778 us -> 695 us (0.89)
  waiting for transfers between devices: 54.5 us -> 0.01 us
  local copies, waits for them, and re-layouts: 32.1 us -> 17.1 us
  between operations: 14.4 us -> 0.97 us
    pallas_call x1, Pallas kernels: 84.5 us -> 145 us  [start_gather(): pl.pallas_call(functools.partial(start_kernel, nz, ne), out_shape=[jax.Sh...]
    all_gather x1 -> x0, waiting for transfers between devices: 54.5 us -> none  [body(): g_all = lax.all_gather(cot, both, axis=0, tiled=True)]
    pallas_call x2 -> x1, Pallas kernels: 189 us -> 165 us  [tail(): pl.pallas_call(functools.partial(tail_kernel, nz, ne, kinds, gain_row, wi...]
    pallas_call x1, Pallas kernels: 40.4 us -> 22.6 us  [gather_tokens(): pl.pallas_call(functools.partial(gather_kernel, nz, ne, spread), out_shap...]
    pallas_call x1, Pallas kernels: 54.2 us -> 37.8 us  [attn_bwd(): pl.pallas_call(functools.partial(attn_bwd_kernel, ne), out_shape=[jax.Sha...]
    transpose x1 -> x0, local copies, waits for them, and re-layouts: 11.5 us -> none  [body(): grad_w_qkv, grad_w_out = (laid[:-1].transpose(1, 0, 2), laid[-1])]
    pallas_call x1, Pallas kernels: 200 us -> 210 us  [moe_net(): pl.pallas_call(functools.partial(moe_net_kernel, nz, ne, per_dev, slots),...]
    pallas_call x1, Pallas kernels: 38.3 us -> 28.3 us  [scatter_tokens(): pl.pallas_call(functools.partial(scatter_kernel, nz, ne, spread), out_sha...]
  transfers between devices with their start and end apart: 3 -> 1, of which waited for: 1 -> 0; matrix products, arithmetic and copies ran while one was open for 6% -> 4% of each run, Pallas kernels for 46% -> 32%
where the time goes in v8:
time: 695 us; the launch traced here: 693 us
  Pallas kernels  640 us (92%)
  other arithmetic  22 us (3%)
  local copies, waits for them, and re-layouts  17.1 us (2%)
  starting transfers between devices  10.5 us (2%)
    pallas_call x1, Pallas kernels, moe_net(): pl.pallas_call(functools.partial(moe_net_kernel, nz, ne, per_dev, slots),...  210 us
    pallas_call x1, Pallas kernels, tail(): pl.pallas_call(functools.partial(tail_kernel, nz, ne, kinds, gain_row, wi...  165 us
    pallas_call x1, Pallas kernels, start_gather(): pl.pallas_call(functools.partial(start_kernel, nz, ne), out_shape=[jax.Sh...  145 us
    pallas_call x1, Pallas kernels, attn_bwd(): pl.pallas_call(functools.partial(attn_bwd_kernel, ne), out_shape=[jax.Sha...  37.8 us
    pallas_call x1, Pallas kernels, scatter_tokens(): pl.pallas_call(functools.partial(scatter_kernel, nz, ne, spread), out_sha...  28.3 us
    pallas_call x1, Pallas kernels, attn_fwd(): pl.pallas_call(functools.partial(attn_fwd_kernel, ne), out_shape=[jax.Sha...  26.2 us
    pallas_call x1, Pallas kernels, gather_tokens(): pl.pallas_call(functools.partial(gather_kernel, nz, ne, spread), out_shap...  22.6 us
  transfers between devices with their start and end apart: 1, of which 0 were waited for; matrix products, arithmetic and copies ran while one was open for 4% of the time, Pallas kernels for 32%

profile of v8, /device:TPU:0, one launch (start us, length us, event | category | flops | bytes accessed | tf_op | source)
XLA Modules:
  0.0 692.9 jit_solution(1044790276676287817)
XLA Ops:
  0.7 1.4 maximum_maximum_fusion.small_ref
  2.2 1.2 reshape.62.seg_ref
  3.4 145.2 %start_gather.1 = (bf16[8,128,2048]{2,1,0:T(8,128)(2,1)}, bf16[3,2048,256]{2,1,0:T(8,128)(2,1)}, bf16[256,2048]{1,0:T(8,128)(2,1)}, bf16[4,32,512]{2,1,0:T(8,128...) custom-call(bf16[128,2048]{1,0:T(8,128)(2,1)} %x_ref.3, bf16[3,512,2048]{2,1,0:T(8,128)(2,1)} %bitcast.33, ...), custom_call_target="tpu_custom_call" | custom-call | tf_op jit(solution)/shard_map/start_gather/pallas_call | solution.py:543
  149.4 0.9 slice_bitcast_fusion
  151.9 26.2 %attn_fwd.1 = (bf16[1024,2048]{1,0:T(8,128)(2,1)}, f32[1024,256]{1,0:T(8,128)}, f32[1024,256]{1,0:T(8,128)}, bf16[1024,256]{1,0:T(8,128)(2,1)}, bf16[1024,256]{1...) custom-call(bf16[8,128,2048]{2,1,0:T(8,128)(2,1)} %get-tuple-element, ...), custom_call_target="tpu_custom_call" | custom-call | tf_op jit(solution)/shard_map/attn_fwd/pallas_call | solution.py:697
  178.1 28.3 %scatter_tokens.1 = f32[128,2048]{1,0:T(8,128)} custom-call(bf16[8,128,2048]{2,1,0:T(8,128)(2,1)} %get-tuple-element.42.x_ref), custom_call_target="tpu_custom_call" | custom-call | tf_op jit(solution)/shard_map/scatter_tokens/pallas_call | solution.py:357
  206.4 1.5 multiply_reduce_fusion.2
  207.9 0.9 copy-done
  210.2 1.0 concatenate.18.h_ref
  211.1 209.7 %moe_net.1 = (bf16[32,128,2176]{2,1,0:T(8,128)(2,1)}, bf16[32,128,2048]{2,1,0:T(8,128)(2,1)}, f32[128,2176]{1,0:T(8,128)}, bf16[2048,1024]{1,0:T(8,128)(2,1)}, f32[512,2048]{1,0:T(8,128)}) custom-call(bf16[128,2176]{1,0:T(8,128)(2,1)} %concatenate.18.h_ref, bf16[32,128,2048]{2,1,0:T(8,128)(2,1)} %get-tuple-element.43.g_ref, bf16[2,2048,1024]{2,1,0:T(8,128)(2,1)} %wg_ref.1, ...), custom_call_target="tpu_custom_call" | custom-call | tf_op jit(solution)/shard_map/moe_net/pallas_call | solution.py:1632
  420.9 10.5 %all-to-all-start = ((bf16[4,512,1024]{2,1,0:T(8,128)(2,1)}), bf16[4,512,1024]{2,1,0:T(8,128)(2,1)}, u32[]{:S(2)}, u32[]{:S(2)}) async-start(bf16[4,512,1024]{2,1,0:T(8,128)(2,1)} %bitcast.35), calls=%async_computation | async-start | bytes 8388608 | tf_op jit(solution)/shard_map/all_to_all | solution.py:1723
  431.4 1.1 multiply_reduce_fusion.3
  432.5 1.1 multiply_convert_fusion.1
  433.6 1.7 multiply_reduce_fusion
  435.3 1.5 fusion.5
  436.8 22.6 %gather_tokens.1.gab_ref = bf16[8,128,2048]{2,1,0:T(8,128)(2,1)} custom-call(bf16[128,2048]{1,0:T(8,128)(2,1)} %get-tuple-element.67.x_ref), custom_call_target="tpu_custom_call" | custom-call | tf_op jit(solution)/shard_map/gather_tokens/pallas_call | solution.py:191
  459.4 37.8 %attn_bwd.1 = (bf16[8,128,2048]{2,1,0:T(8,128)(2,1)}, bf16[2048,1024]{1,0:T(8,128)(2,1)}, f32[8,256]{1,0:T(8,128)}) custom-call(bf16[8,128,2048]{2,1,0:T(8,128)(2,1)} %gather_tokens.1.gab_ref, bf16[3,2048,256]{2,1,0:T(8,128)(2,1)} %get-tuple-element.38.wq_ref, bf16[256,2048]{1,0:T(8,128)(2,1)} %get-tuple-element.39.wo_ref, ...), custom_call_target="tpu_custom_call" | custom-call | tf_op jit(solution)/shard_map/attn_bwd/pallas_call | solution.py:819
  498.8 1.4 concatenate.19.tiny_ref
  500.2 164.5 %tail.1 = (bf16[128,2048]{1,0:T(8,128)(2,1)}, bf16[4,512,2048]{2,1,0:T(8,128)(2,1)}, f32[2,24,256]{2,1,0:T(8,128)}, bf16[128,2048]{1,0:T(8,128)(2,1)}) custom-call(bf16[2048,1024]{1,0:T(8,128)(2,1)} %get-tuple-element.53.parts_ref, bf16[8,128,2048]{2,1,0:T(8,128)(2,1)} %get-tuple-element.54.gh1_ref, bf16[32,128,2048]{2,1,0:T(8,128)(2,1)} %get-tuple-element.55.mix_ref, ...), custom_call_target="tpu_custom_call" | custom-call | tf_op jit(solution)/shard_map/tail/pallas_call | solution.py:1091
  664.7 1.3 slice.67
  667.4 4.1 bitcast_convert_fusion
  671.6 9.1 %convert_bitcast_fusion = f32[512,3,2048]{2,0,1:T(8,128)} fusion(bf16[4,512,2048]{2,1,0:T(8,128)(2,1)} %get-tuple-element.59), kind=kLoop, calls=%fused_computation | loop fusion | flops 3145728 | bytes 18874368 | tf_op jit(solution)/shard_map/transpose | solution.py:1760
  680.7 6.0 lay_experts.1
  688.2 4.7 copy.46
  (62 shorter events, 8.4 us)
Async XLA Ops:
  149.4 2.5 copy-start.12
  178.1 28.3 %copy-start.2 = (bf16[128,2048]{1,0:T(8,128)(2,1)S(1)}, bf16[128,2048]{1,0:T(8,128)(2,1)}, u32[]{:S(2)}) copy-start(bf16[128,2048]{1,0:T(8,128)(2,1)} %x_ref.3) | copy-start | bytes 1572868
  178.1 31.3 %copy-start.15 = (s32[128,8]{0,1:T(8,128)S(1)}, s32[128,8]{0,1:T(8,128)}, u32[]{:S(2)}) copy-start(s32[128,8]{0,1:T(8,128)} %param.13) | copy-start | bytes 12292
  207.9 1.0 copy-start
  207.9 1.4 copy-start.13
  207.9 1.4 copy-start.8
  209.4 0.6 copy-start.4
  209.5 0.6 copy-start.6
  420.8 10.6 %copy-start.5 = (f32[128,16]{1,0:T(8,128)S(1)}, f32[128,16]{1,0:T(8,128)}, u32[]{:S(2)}) copy-start(f32[128,16]{1,0:T(8,128)} %copy-done.4) | copy-start | bytes 24580
  420.8 10.6 %copy-start.7 = (f32[128,16]{1,0:T(8,128)S(1)}, f32[128,16]{1,0:T(8,128)}, u32[]{:S(2)}) copy-start(f32[128,16]{1,0:T(8,128)} %copy-done.6) | copy-start | bytes 24580
  420.8 12.7 %copy-start.1 = (f32[128,2048]{1,0:T(8,128)S(1)}, f32[128,2048]{1,0:T(8,128)}, u32[]{:S(2)}) copy-start(f32[128,2048]{1,0:T(8,128)} %copy-done) | copy-start | bytes 3145732
  420.8 12.7 %copy-start.9 = (bf16[4,2,8,512]{3,2,0,1:T(8,128)(2,1)S(1)}, bf16[4,2,8,512]{3,2,0,1:T(8,128)(2,1)}, u32[]{:S(2)}) copy-start(bf16[4,2,8,512]{3,2,0,1:T(8,128)(2,1)} %copy-done.8) | copy-start | bytes 196612
  420.8 12.7 %copy-start.14 = (f32[128]{0:T(128)S(1)}, f32[128]{0:T(128)}, u32[]{:S(2)}) copy-start(f32[128]{0:T(128)} %copy-done.13) | copy-start | bytes 1540
  420.8 14.4 %copy-start.3 = (bf16[128,2048]{1,0:T(8,128)(2,1)S(1)}, bf16[128,2048]{1,0:T(8,128)(2,1)}, u32[]{:S(2)}) copy-start(bf16[128,2048]{1,0:T(8,128)(2,1)} %cot_ref.1) | copy-start | bytes 1572868
  420.9 259.8 %all-to-all-start = ((bf16[4,512,1024]{2,1,0:T(8,128)(2,1)}), bf16[4,512,1024]{2,1,0:T(8,128)(2,1)}, u32[]{:S(2)}, u32[]{:S(2)}) async-start(bf16[4,512,1024]{2,1,0:T(8,128)(2,1)} %bitcast.35), calls=%async_computation | async-start | bytes 8388608 | tf_op jit(solution)/shard_map/all_to_all | solution.py:1723
  680.7 6.0 copy-start.11
  680.7 6.8 copy-start.10

commit v9 on v8

--- a/solution.py
+++ b/solution.py
@@ -202,31 +202,31 @@
 def add_rows(dst, src, tile=16):
     def step(i, carry):
         rows = pl.ds(pl.multiple_of(i * tile, tile), tile)
-        dst[rows, :] = (dst[rows, :].astype(F32) + src[rows, :].astype(F32)).astype(dst.dtype)
+        dst[rows, :] = dst[rows, :] + src[rows, :]
         return carry
 
     lax.fori_loop(0, dst.shape[0] // tile, step, 0)
 
 
 class TokenScatter:
-    def __init__(self, nz, ne, z, e, spread, x_ref, acc, got, zgot, loads, send, recv, zsend, zrecv):
-        self.nz, self.ne, self.z, self.e, self.spread = nz, ne, z, e, spread
+    def __init__(self, nz, ne, z, e, ranks, x_ref, acc, got, zgot, loads, send, recv, zsend, zrecv):
+        self.nz, self.ne, self.z, self.e = nz, ne, z, e
         self.x, self.acc, self.got, self.zgot = x_ref, acc, got, zgot
         self.loads, self.send, self.recv, self.zsend, self.zrecv = loads, send, recv, zsend, zrecv
-        self.rounds = nz if spread else 1
+        self.ranks = ranks
         self.stages = ne.bit_length() - 1
-        self.steps = self.rounds + self.stages - 1
+        self.steps = len(ranks) + self.stages - 1
         self.half = acc.shape[3]
         self.orders = bit_orders(ne)
-        self.ranks = list(range(1, self.rounds)) + [0]
         self.first = [0]
         for j in range(self.stages):
             self.first.append(self.first[j] + (ne >> (j + 1)))
-        self.pending, self.arrivals, self.zwait = [], {}, {}
+        self.pending, self.arrivals, self.zwait = [], {}, []
 
     def block(self, r, ee):
-        home = lax.rem(self.z + r, self.nz) * self.ne if self.spread else 0
-        return home + ee
+        if self.ranks[r] is None:
+            return ee
+        return lax.rem(self.z + self.ranks[r], self.nz) * self.ne + ee
 
     def push(self, r, s, j):
         order = self.orders[s]
@@ -248,7 +248,7 @@
             self.arrivals.setdefault((r, s, j), []).append((copy.wait_recv, i, n))
 
     def start(self):
-        for r in self.ranks:
+        for r in range(len(self.ranks)):
             for s in range(2):
                 self.push(r, s, 0)
                 for i, ee in enumerate(flips(self.e, self.orders[s][:0:-1])):
@@ -261,8 +261,8 @@
                     self.arrivals.setdefault((r, s, -1), []).append(copy.wait)
 
     def step(self, t):
-        for place, r in enumerate(self.ranks):
-            j = t - place
+        for r, rank in enumerate(self.ranks):
+            j = t - r
             if not 0 <= j < self.stages:
                 continue
             for s in range(2):
@@ -274,44 +274,54 @@
                     add_rows(self.acc.at[r, s, i], self.got.at[r, s, n])
                 if j + 1 < self.stages:
                     self.push(r, s, j + 1)
-                elif r > 0:
+                elif rank:
                     copy = remote(
                         self.acc.at[r, s, 0], self.zgot.at[r, s],
                         self.zsend.at[r, s], self.zrecv.at[r, s],
-                        (lax.rem(self.z + r, self.nz), self.e),
+                        (lax.rem(self.z + rank, self.nz), self.e),
                     )
                     copy.start()
                     self.pending.append(copy.wait_send)
-                    self.zwait[(r, s)] = copy.wait_recv
+                    self.zwait.append(copy.wait_recv)
 
     def arrive(self):
-        for wait in self.zwait.values():
+        for wait in self.zwait:
             wait()
 
     def rows(self, s, here):
-        total = self.acc[0, s, 0, here, :].astype(F32)
-        for r in range(1, self.rounds):
-            total = total + self.zgot[r, s, here, :].astype(F32)
-        return total
+        parts = [
+            self.zgot[r, s, here, :] if rank else self.acc[r, s, 0, here, :]
+            for r, rank in enumerate(self.ranks)
+        ]
+        return sum(part.astype(F32) for part in parts)
 
     def finish(self):
         for wait in self.pending:
             wait()
 
     @staticmethod
-    def scratch(nz, ne, spread, count, width):
-        rounds = nz if spread else 1
+    def scratch(ne, ranks, count, width):
+        rounds = len(ranks)
         half = count // 2
         return [
             pltpu.VMEM((rounds, 2, ne // 2, half, width), BF),
             pltpu.VMEM((rounds, 2, ne - 1, half, width), BF),
-            pltpu.VMEM((nz if spread else 1, 2, half, width), BF),
+            pltpu.VMEM((rounds, 2, half, width), BF),
             DMA((rounds, 2, ne // 2)),
             DMA((rounds, 2, ne - 1)),
             DMA((rounds, 2, ne - 1)),
-            DMA((nz, 2)),
-            DMA((nz, 2)),
+            DMA((rounds, 2)),
+            DMA((rounds, 2)),
         ]
+
+
+def split_ranks(nz):
+    ranks = scatter_ranks(nz, True)
+    return ranks[: nz // 2], ranks[nz // 2 :]
+
+
+def scatter_ranks(nz, spread):
+    return [*range(1, nz), 0] if spread else [None]
 
 
 def over_rows(half, act, tile=16):
@@ -330,7 +340,7 @@
     out_ref, *rest = refs[-9:]
     z, e = lax.axis_index("dp"), lax.axis_index("expert")
     meet_column_and_plane(nz, ne, z, e, spread)
-    net = TokenScatter(nz, ne, z, e, spread, x_ref, *rest)
+    net = TokenScatter(nz, ne, z, e, scatter_ranks(nz, spread), x_ref, *rest)
     net.start()
     for t in range(net.steps):
         net.step(t)
@@ -360,7 +370,7 @@
         + [jax.ShapeDtypeStruct((count, width), F32)],
         in_specs=[ANY] * (1 + len(more)),
         out_specs=[ANY] * len(more) + [VMEM],
-        scratch_shapes=TokenScatter.scratch(nz, ne, spread, count, width),
+        scratch_shapes=TokenScatter.scratch(ne, scatter_ranks(nz, spread), count, width),
         input_output_aliases={1: 0} if more else {},
         compiler_params=pltpu.CompilerParams(
             collective_id=cid, has_side_effects=True, vmem_limit_bytes=64_000_000
@@ -441,6 +451,7 @@
         remote(seg_ref, seg_out.at[e], seg_send, seg_recv, (z, lax.rem(e + r, ne))).start()
     net = PlaneGather(nz, ne, z, e, False, x_ref, out_ref, zsend, zrecv, send, recv, local)
     net.start_round(0)
+    cot.start_round(0)
 
     columns = pl.ds(e * hw, hw)
     for i in range(per):
@@ -462,10 +473,12 @@
                 def _():
                     give.start()
     net.finish_round(0)
-    cot.start_round(0)
+    for r in range(1, nz):
+        cot.start_round(r)
+        if r + 1 < nz:
+            cot.finish_round(r - 1)
+    left = list(range(max(nz - 2, 0), nz))
     for dist in range(1, nz):
-        cot.start_round(dist)
-        cot.finish_round(dist - 1)
         for j in range(kinds):
 
             @pl.when(z - dist >= 0)
@@ -488,7 +501,10 @@
                     if dist + 1 < nz:
                         hop(j, z + dist, dist + 1, False).start()
 
-    cot.finish_round(nz - 1)
+        if left:
+            cot.finish_round(left.pop(0))
+    for r in left:
+        cot.finish_round(r)
     cot.finish()
     net.finish()
     for keep in keeps:
@@ -720,10 +736,11 @@
 
 
 def attn_bwd_kernel(
-    ne, gab_ref, wq_ref, wo_ref, mine_ref, seg_ref, cos_ref, sin_ref,
-    h1_ref, q_ref, k_ref, rq_ref, rk_ref, v_ref, o_ref, scale_ref,
-    gh1_ref, parts_ref, gain_ref,
+    nz, ne, with_mix, gab_ref, wq_ref, wo_ref, mine_ref, seg_ref, cos_ref, sin_ref,
+    h1_ref, q_ref, k_ref, rq_ref, rk_ref, v_ref, o_ref, scale_ref, x1_ref, mix_ref,
+    gh1_ref, parts_ref, gain_ref, x1m_ref,
     pout, go_ref, gqn_ref, gkn_ref, gp_ref, sums, theirs, means, send, recv, psend, precv,
+    *mix_scratch,
 ):
     z, e = lax.axis_index("dp"), lax.axis_index("expert")
     count, hw = q_ref.shape
@@ -732,7 +749,16 @@
     length = seg_ref.shape[2]
     tile = min(512, count)
     blocks = tile // rows_dev
-    meet_plane(ne, z, e)
+    if with_mix:
+        meet_all(nz, ne, z, e)
+        mix = TokenScatter(nz, ne, z, e, split_ranks(nz)[0], mix_ref, *mix_scratch)
+        mix.start()
+    else:
+        meet_plane(ne, z, e)
+
+    def mix_step(t):
+        if with_mix and t < mix.steps:
+            mix.step(t)
 
     gab = lambda first: gab_ref[first // rows_dev : first // rows_dev + blocks].reshape(tile, width)
     part = dot(o_ref[:tile, :], gab(0), TN)
@@ -753,6 +779,7 @@
         give.start()
         gives.append(give)
     parts_ref[my_rows, last] = pout[:, my_rows]
+    mix_step(0)
 
     cos, sin = cos_ref[...], -sin_ref[...]
     gain_ref[...] = jnp.zeros_like(gain_ref)
@@ -786,8 +813,13 @@
         store_columns(sums, start, [sum_q, sum_k])
         return carry
 
-    lax.fori_loop(0, count // length, sequence, 0)
+    seqs = count // length
+    lax.fori_loop(0, seqs // 2, sequence, 0)
+    mix_step(1)
+    lax.fori_loop(seqs // 2, seqs, sequence, 0)
+    mix_step(2)
     total = plane_totals(ne, z, e, sums, theirs, send, recv)
+    mix_step(3)
     as_columns(total / width, means)
     for first in range(0, count, tile):
         rows = slice(first, first + tile)
@@ -811,20 +843,33 @@
     for give in gives:
         give.wait_send()
         give.wait_recv()
-
-
-def attn_bwd(gab, wq, wo, my_gains, seg, tables, saved, cid):
+    if with_mix:
+        for t in range(4, mix.steps):
+            mix_step(t)
+        mix.arrive()
+
+        def add_part(s, here, span):
+            x1m_ref[span, :] = x1_ref[span, :] + mix.rows(s, here)
+
+        over_rows(mix.half, add_part)
+        mix.finish()
+    else:
+        x1m_ref[...] = x1_ref[...]
+
+
+def attn_bwd(gab, wq, wo, my_gains, seg, tables, saved, x1, mix, nz, cid):
     ne, rows_dev, width = gab.shape
     count, hw = ne * rows_dev, wo.shape[0]
     return pl.pallas_call(
-        functools.partial(attn_bwd_kernel, ne),
+        functools.partial(attn_bwd_kernel, nz, ne, mix is not None),
         out_shape=[
             jax.ShapeDtypeStruct((ne, rows_dev, width), BF),
             jax.ShapeDtypeStruct((width, 4 * hw), BF),
             jax.ShapeDtypeStruct((8, hw), F32),
+            jax.ShapeDtypeStruct((rows_dev, width), F32),
         ],
-        in_specs=[VMEM] * 15,
-        out_specs=[VMEM] * 3,
+        in_specs=[VMEM] * 16 + [ANY],
+        out_specs=[VMEM] * 4,
         scratch_shapes=[
             pltpu.VMEM((hw, width), BF),
             pltpu.VMEM((count, hw), BF),
@@ -835,12 +880,17 @@
             pltpu.VMEM((ne, 8, count), F32),
             pltpu.VMEM((count, 128), F32),
             DMA((ne,)), DMA((ne,)), DMA((ne,)), DMA((ne,)),
-        ],
+        ]
+        + (
+            []
+            if mix is None
+            else TokenScatter.scratch(ne, split_ranks(nz)[0], rows_dev, width)
+        ),
         compiler_params=pltpu.CompilerParams(
             collective_id=cid, has_side_effects=True, vmem_limit_bytes=64_000_000
         ),
         name="attn_bwd",
-    )(gab, wq, wo, my_gains, seg, *tables, *saved)
+    )(gab, wq, wo, my_gains, seg, *tables, *saved, x1, gab if mix is None else mix)
 
 
 def tail_kernel(
@@ -865,10 +915,10 @@
     for copy in loads:
         copy.start()
     meet_all(nz, ne, z, e)
-    mine = TokenScatter(nz, ne, z, e, False, gh1_ref, *nets_scratch[:8])
+    mine = TokenScatter(nz, ne, z, e, [None], gh1_ref, *nets_scratch[:8])
     mine.start()
     if with_mix:
-        mix = TokenScatter(nz, ne, z, e, True, mix_ref, *nets_scratch[8:])
+        mix = TokenScatter(nz, ne, z, e, split_ranks(nz)[1], mix_ref, *nets_scratch[8:])
         mix.start()
     for copy in loads:
         copy.wait()
@@ -1085,9 +1135,9 @@
     per = ne // nz
     block = (nz, chunks, rows, total_cols)
     with_mix = mix is not None
-    scratch = TokenScatter.scratch(nz, ne, False, count, width)
+    scratch = TokenScatter.scratch(ne, [None], count, width)
     if with_mix:
-        scratch += TokenScatter.scratch(nz, ne, True, count, width)
+        scratch += TokenScatter.scratch(ne, split_ranks(nz)[1], count, width)
     grad, laid, small, output = pl.pallas_call(
         functools.partial(tail_kernel, nz, ne, kinds, gain_row, with_mix),
         out_shape=[
@@ -1282,6 +1332,9 @@
     def subset_mask(order, subset):
         return sum(bit for b, bit in enumerate(order) if subset >> b & 1)
 
+    def subset_index(order, mask):
+        return sum(1 << b for b, bit in enumerate(order) if bit & mask)
+
     def pass_on(r, s, stage, subset, own=False):
         order = gather_orders[s]
         dst = hall_ref.at[plane(r) * ne + at[subset_mask(order, subset)], part(s)]
@@ -1399,15 +1452,15 @@
     def settle(r, t):
         for s in range(2):
             order = sum_orders[s]
-            for index in range(1 << (stages - t)):
-                copy = push(r, s, t, index)
-                copy.wait_recv()
+            count = 1 << (stages - t)
+            for index in range(count - 1, -1, -1):
+                push(r, s, t, index).wait_recv()
                 mask = subset_mask(order[t + 1 :], index)
                 add_rows(acc.at[r, mask // 2, part(s)], got.at[r, s, place_of(t, index)])
-            if t < stages:
-                for index in range(1 << (stages - t - 1)):
-                    push(r, s, t + 1, index).start()
-            else:
+                if 2 * index >= count:
+                    keep = subset_index(order[t + 2 :], mask)
+                    push(r, s, t + 1, keep).start()
+            if t == stages:
 
                 @pl.when(r > 0)
                 def _():
@@ -1737,8 +1790,9 @@
     gab = gx1.astype(BF)
 
     gab_all = gather_tokens(gab, nz, ne, False, 4)
-    gh1_part, parts, gain_qk = attn_bwd(
-        gab_all, wq, wo, my_gains, seg_all, tables, saved, 10
+    gh1_part, parts, gain_qk, x1_mix = attn_bwd(
+        gab_all, wq, wo, my_gains, seg_all, tables, saved, x1,
+        mix.reshape(-1, count, width) if fits else None, nz, 10,
     )
     place = lambda part: lax.dynamic_update_slice_in_dim(
         jnp.zeros((1, width), F32), part[None], e * hw, axis=1
@@ -1751,7 +1805,7 @@
         axis=0,
     )
     grad_inputs, laid, tiny, output = tail(
-        parts, gh1_part, mix.reshape(-1, count, width) if fits else None, inputs, x1, gx1,
+        parts, gh1_part, mix.reshape(-1, count, width) if fits else None, inputs, x1_mix, gx1,
         gain_mat, tiny, expert_count, nz, ne, hw, 5,
     )
     if not fits:

time: 695 us -> 725 us (1.043)
  Pallas kernels: 640 us -> 663 us
    pallas_call x1, Pallas kernels: 37.8 us -> 104 us  [attn_bwd(): pl.pallas_call(functools.partial(attn_bwd_kernel, nz, ne, mix is not None...]
    pallas_call x1, Pallas kernels: 165 us -> 124 us  [tail(): pl.pallas_call(functools.partial(tail_kernel, nz, ne, kinds, gain_row, wi...]
    pallas_call x1, Pallas kernels: 210 us -> 201 us  [moe_net(): pl.pallas_call(functools.partial(moe_net_kernel, nz, ne, per_dev, slots),...]
  transfers between devices with their start and end apart: 1 -> 1, of which waited for: 0 -> 0; matrix products, arithmetic and copies ran while one was open for 4% -> 3% of each run, Pallas kernels for 32% -> 35%
where the time goes in v9:
time: 725 us; the launch traced here: 716 us
  Pallas kernels  663 us (91%)
  other arithmetic  22 us (3%)
  local copies, waits for them, and re-layouts  17.1 us (2%)
  starting transfers between devices  10.9 us (2%)
    pallas_call x1, Pallas kernels, moe_net(): pl.pallas_call(functools.partial(moe_net_kernel, nz, ne, per_dev, slots),...  201 us
    pallas_call x1, Pallas kernels, start_gather(): pl.pallas_call(functools.partial(start_kernel, nz, ne), out_shape=[jax.Sh...  152 us
    pallas_call x1, Pallas kernels, tail(): pl.pallas_call(functools.partial(tail_kernel, nz, ne, kinds, gain_row, wi...  124 us
    pallas_call x1, Pallas kernels, attn_bwd(): pl.pallas_call(functools.partial(attn_bwd_kernel, nz, ne, mix is not None...  104 us
    pallas_call x1, Pallas kernels, scatter_tokens(): pl.pallas_call(functools.partial(scatter_kernel, nz, ne, spread), out_sha...  28 us
    pallas_call x1, Pallas kernels, attn_fwd(): pl.pallas_call(functools.partial(attn_fwd_kernel, ne), out_shape=[jax.Sha...  26.2 us
    pallas_call x1, Pallas kernels, gather_tokens(): pl.pallas_call(functools.partial(gather_kernel, nz, ne, spread), out_shap...  22.1 us
  transfers between devices with their start and end apart: 1, of which 0 were waited for; matrix products, arithmetic and copies ran while one was open for 3% of the time, Pallas kernels for 35%

profile of v9, /device:TPU:0, one launch (start us, length us, event | category | flops | bytes accessed | tf_op | source)
XLA Modules:
  0.0 715.9 jit_solution(3591763018222132649)
XLA Ops:
  0.7 1.4 maximum_maximum_fusion.small_ref
  2.2 1.2 reshape.62.seg_ref
  3.4 152.0 %start_gather.1 = (bf16[8,128,2048]{2,1,0:T(8,128)(2,1)}, bf16[3,2048,256]{2,1,0:T(8,128)(2,1)}, bf16[256,2048]{1,0:T(8,128)(2,1)}, bf16[4,32,512]{2,1,0:T(8,128...) custom-call(bf16[128,2048]{1,0:T(8,128)(2,1)} %x_ref.3, bf16[3,512,2048]{2,1,0:T(8,128)(2,1)} %bitcast.33, ...), custom_call_target="tpu_custom_call" | custom-call | tf_op jit(solution)/shard_map/start_gather/pallas_call | solution.py:559
  156.2 0.9 slice_bitcast_fusion
  158.7 26.2 %attn_fwd.1 = (bf16[1024,2048]{1,0:T(8,128)(2,1)}, f32[1024,256]{1,0:T(8,128)}, f32[1024,256]{1,0:T(8,128)}, bf16[1024,256]{1,0:T(8,128)(2,1)}, bf16[1024,256]{1...) custom-call(bf16[8,128,2048]{2,1,0:T(8,128)(2,1)} %get-tuple-element, ...), custom_call_target="tpu_custom_call" | custom-call | tf_op jit(solution)/shard_map/attn_fwd/pallas_call | solution.py:713
  184.9 28.0 %scatter_tokens.1 = f32[128,2048]{1,0:T(8,128)} custom-call(bf16[8,128,2048]{2,1,0:T(8,128)(2,1)} %get-tuple-element.43.x_ref), custom_call_target="tpu_custom_call" | custom-call | tf_op jit(solution)/shard_map/scatter_tokens/pallas_call | solution.py:367
  212.9 1.5 multiply_reduce_fusion.2
  214.4 0.9 copy-done
  216.6 1.0 concatenate.18.h_ref
  217.6 200.9 %moe_net.1 = (bf16[32,128,2176]{2,1,0:T(8,128)(2,1)}, bf16[32,128,2048]{2,1,0:T(8,128)(2,1)}, f32[128,2176]{1,0:T(8,128)}, bf16[2048,1024]{1,0:T(8,128)(2,1)}, f32[512,2048]{1,0:T(8,128)}) custom-call(bf16[128,2176]{1,0:T(8,128)(2,1)} %concatenate.18.h_ref, bf16[32,128,2048]{2,1,0:T(8,128)(2,1)} %get-tuple-element.44.g_ref, bf16[2,2048,1024]{2,1,0:T(8,128)(2,1)} %wg_ref.1, ...), custom_call_target="tpu_custom_call" | custom-call | tf_op jit(solution)/shard_map/moe_net/pallas_call | solution.py:1685
  418.6 10.9 %all-to-all-start = ((bf16[4,512,1024]{2,1,0:T(8,128)(2,1)}), bf16[4,512,1024]{2,1,0:T(8,128)(2,1)}, u32[]{:S(2)}, u32[]{:S(2)}) async-start(bf16[4,512,1024]{2,1,0:T(8,128)(2,1)} %bitcast.35), calls=%async_computation | async-start | bytes 8388608 | tf_op jit(solution)/shard_map/all_to_all | solution.py:1776
  429.4 1.1 multiply_reduce_fusion.3
  430.5 1.1 multiply_convert_fusion.1
  431.6 1.7 multiply_reduce_fusion
  433.4 1.5 fusion.5
  434.8 22.1 %gather_tokens.1.gab_ref = bf16[8,128,2048]{2,1,0:T(8,128)(2,1)} custom-call(bf16[128,2048]{1,0:T(8,128)(2,1)} %get-tuple-element.69.x_ref), custom_call_target="tpu_custom_call" | custom-call | tf_op jit(solution)/shard_map/gather_tokens/pallas_call | solution.py:191
  457.0 104.0 %attn_bwd.1 = (bf16[8,128,2048]{2,1,0:T(8,128)(2,1)}, bf16[2048,1024]{1,0:T(8,128)(2,1)}, f32[8,256]{1,0:T(8,128)}, f32[128,2048]{1,0:T(8,128)}) custom-call(bf16[8,128,2048]{2,1,0:T(8,128)(2,1)} %gather_tokens.1.gab_ref, bf16[3,2048,256]{2,1,0:T(8,128)(2,1)} %get-tuple-element.39.wq_ref, bf16[256,2048]{1,0:T(8,128)(2,1)} %get-tuple-element.40.wo_ref, ...), custom_call_target="tpu_custom_call" | custom-call | tf_op jit(solution)/shard_map/attn_bwd/pallas_call | solution.py:863
  562.6 1.4 concatenate.19.tiny_ref
  564.0 123.7 %tail.1 = (bf16[128,2048]{1,0:T(8,128)(2,1)}, bf16[4,512,2048]{2,1,0:T(8,128)(2,1)}, f32[2,24,256]{2,1,0:T(8,128)}, bf16[128,2048]{1,0:T(8,128)(2,1)}) custom-call(bf16[2048,1024]{1,0:T(8,128)(2,1)} %get-tuple-element.55.parts_ref, bf16[8,128,2048]{2,1,0:T(8,128)(2,1)} %get-tuple-element.56.gh1_ref, bf16[32,128,2048]{2,1,0:T(8,128)(2,1)} %get-tuple-element.54.mix_ref, ...), custom_call_target="tpu_custom_call" | custom-call | tf_op jit(solution)/shard_map/tail/pallas_call | solution.py:1141
  687.7 1.3 slice.67
  690.4 4.1 bitcast_convert_fusion
  694.6 9.1 %convert_bitcast_fusion = f32[512,3,2048]{2,0,1:T(8,128)} fusion(bf16[4,512,2048]{2,1,0:T(8,128)(2,1)} %get-tuple-element.61), kind=kLoop, calls=%fused_computation | loop fusion | flops 3145728 | bytes 18874368 | tf_op jit(solution)/shard_map/transpose | solution.py:1814
  703.7 6.0 lay_experts.1
  711.2 4.7 copy.46
  (62 shorter events, 8.4 us)
Async XLA Ops:
  156.1 2.5 copy-start.12
  184.9 28.0 %copy-start.2 = (bf16[128,2048]{1,0:T(8,128)(2,1)S(1)}, bf16[128,2048]{1,0:T(8,128)(2,1)}, u32[]{:S(2)}) copy-start(bf16[128,2048]{1,0:T(8,128)(2,1)} %x_ref.3) | copy-start | bytes 1572868
  184.9 31.0 %copy-start.15 = (s32[128,8]{0,1:T(8,128)S(1)}, s32[128,8]{0,1:T(8,128)}, u32[]{:S(2)}) copy-start(s32[128,8]{0,1:T(8,128)} %param.13) | copy-start | bytes 12292
  214.3 1.0 copy-start
  214.4 1.4 copy-start.13
  214.4 1.4 copy-start.8
  215.9 0.6 copy-start.4
  216.0 0.6 copy-start.6
  418.5 10.9 %copy-start.5 = (f32[128,16]{1,0:T(8,128)S(1)}, f32[128,16]{1,0:T(8,128)}, u32[]{:S(2)}) copy-start(f32[128,16]{1,0:T(8,128)} %copy-done.4) | copy-start | bytes 24580
  418.5 10.9 %copy-start.7 = (f32[128,16]{1,0:T(8,128)S(1)}, f32[128,16]{1,0:T(8,128)}, u32[]{:S(2)}) copy-start(f32[128,16]{1,0:T(8,128)} %copy-done.6) | copy-start | bytes 24580
  418.5 13.1 %copy-start.1 = (f32[128,2048]{1,0:T(8,128)S(1)}, f32[128,2048]{1,0:T(8,128)}, u32[]{:S(2)}) copy-start(f32[128,2048]{1,0:T(8,128)} %copy-done) | copy-start | bytes 3145732
  418.5 13.1 %copy-start.9 = (bf16[4,2,8,512]{3,2,0,1:T(8,128)(2,1)S(1)}, bf16[4,2,8,512]{3,2,0,1:T(8,128)(2,1)}, u32[]{:S(2)}) copy-start(bf16[4,2,8,512]{3,2,0,1:T(8,128)(2,1)} %copy-done.8) | copy-start | bytes 196612
  418.5 13.1 %copy-start.14 = (f32[128]{0:T(128)S(1)}, f32[128]{0:T(128)}, u32[]{:S(2)}) copy-start(f32[128]{0:T(128)} %copy-done.13) | copy-start | bytes 1540
  418.5 14.8 %copy-start.3 = (bf16[128,2048]{1,0:T(8,128)(2,1)S(1)}, bf16[128,2048]{1,0:T(8,128)(2,1)}, u32[]{:S(2)}) copy-start(bf16[128,2048]{1,0:T(8,128)(2,1)} %cot_ref.1) | copy-start | bytes 1572868
  418.6 285.1 %all-to-all-start = ((bf16[4,512,1024]{2,1,0:T(8,128)(2,1)}), bf16[4,512,1024]{2,1,0:T(8,128)(2,1)}, u32[]{:S(2)}, u32[]{:S(2)}) async-start(bf16[4,512,1024]{2,1,0:T(8,128)(2,1)} %bitcast.35), calls=%async_computation | async-start | bytes 8388608 | tf_op jit(solution)/shard_map/all_to_all | solution.py:1776
  703.7 6.0 copy-start.11
  703.7 6.8 copy-start.10

commit v10 on v9

--- a/solution.py
+++ b/solution.py
@@ -179,10 +179,10 @@
     net = PlaneGather(nz, ne, z, e, spread, x_ref, out_ref, *sems)
     net.spread_own()
     net.start_round(0)
+    net.finish_round(0)
     for r in range(1, net.rounds):
         net.start_round(r)
-        net.finish_round(r - 1)
-    net.finish_round(net.rounds - 1)
+        net.finish_round(r)
     net.finish()
 
 
@@ -316,8 +316,7 @@
 
 
 def split_ranks(nz):
-    ranks = scatter_ranks(nz, True)
-    return ranks[: nz // 2], ranks[nz // 2 :]
+    return [], scatter_ranks(nz, True)
 
 
 def scatter_ranks(nz, spread):
@@ -473,12 +472,9 @@
                 def _():
                     give.start()
     net.finish_round(0)
-    for r in range(1, nz):
-        cot.start_round(r)
-        if r + 1 < nz:
-            cot.finish_round(r - 1)
-    left = list(range(max(nz - 2, 0), nz))
     for dist in range(1, nz):
+        cot.start_round(dist)
+        cot.finish_round(dist - 1)
         for j in range(kinds):
 
             @pl.when(z - dist >= 0)
@@ -501,10 +497,7 @@
                     if dist + 1 < nz:
                         hop(j, z + dist, dist + 1, False).start()
 
-        if left:
-            cot.finish_round(left.pop(0))
-    for r in left:
-        cot.finish_round(r)
+    cot.finish_round(nz - 1)
     cot.finish()
     net.finish()
     for keep in keeps:
@@ -1533,7 +1526,7 @@
 
         for r1 in range(1, nz):
 
-            @pl.when(k == (r1 - 1) * (pairs - 1) + 1)
+            @pl.when(k == (r1 - 1) * pairs + 2)
             def _():
                 start_round(r1)
 
@@ -1792,7 +1785,7 @@
     gab_all = gather_tokens(gab, nz, ne, False, 4)
     gh1_part, parts, gain_qk, x1_mix = attn_bwd(
         gab_all, wq, wo, my_gains, seg_all, tables, saved, x1,
-        mix.reshape(-1, count, width) if fits else None, nz, 10,
+        mix.reshape(-1, count, width) if fits and split_ranks(nz)[0] else None, nz, 10,
     )
     place = lambda part: lax.dynamic_update_slice_in_dim(
         jnp.zeros((1, width), F32), part[None], e * hw, axis=1

time: 725 us -> 685 us (0.945)
  Pallas kernels: 663 us -> 627 us
    pallas_call x1, Pallas kernels: 104 us -> 38.5 us  [attn_bwd(): pl.pallas_call(functools.partial(attn_bwd_kernel, nz, ne, mix is not None...]
    pallas_call x1, Pallas kernels: 124 us -> 164 us  [tail(): pl.pallas_call(functools.partial(tail_kernel, nz, ne, kinds, gain_row, wi...]
  transfers between devices with their start and end apart: 1 -> 1, of which waited for: 0 -> 0; matrix products, arithmetic and copies ran while one was open for 3% -> 4% of each run, Pallas kernels for 35% -> 33%
where the time goes in v10:
time: 685 us; the launch traced here: 683 us
  Pallas kernels  627 us (92%)
  other arithmetic  22 us (3%)
  local copies, waits for them, and re-layouts  17.1 us (2%)
  starting transfers between devices  13.6 us (2%)
    pallas_call x1, Pallas kernels, moe_net(): pl.pallas_call(functools.partial(moe_net_kernel, nz, ne, per_dev, slots),...  196 us
    pallas_call x1, Pallas kernels, tail(): pl.pallas_call(functools.partial(tail_kernel, nz, ne, kinds, gain_row, wi...  164 us
    pallas_call x1, Pallas kernels, start_gather(): pl.pallas_call(functools.partial(start_kernel, nz, ne), out_shape=[jax.Sh...  145 us
    pallas_call x1, Pallas kernels, attn_bwd(): pl.pallas_call(functools.partial(attn_bwd_kernel, nz, ne, mix is not None...  38.5 us
    pallas_call x1, Pallas kernels, scatter_tokens(): pl.pallas_call(functools.partial(scatter_kernel, nz, ne, spread), out_sha...  28 us
    pallas_call x1, Pallas kernels, attn_fwd(): pl.pallas_call(functools.partial(attn_fwd_kernel, ne), out_shape=[jax.Sha...  26.2 us
    pallas_call x1, Pallas kernels, gather_tokens(): pl.pallas_call(functools.partial(gather_kernel, nz, ne, spread), out_shap...  22.9 us
  transfers between devices with their start and end apart: 1, of which 0 were waited for; matrix products, arithmetic and copies ran while one was open for 4% of the time, Pallas kernels for 33%

profile of v10, /device:TPU:0, one launch (start us, length us, event | category | flops | bytes accessed | tf_op | source)
XLA Modules:
  0.0 683.1 jit_solution(14692590460063373094)
XLA Ops:
  0.7 1.4 maximum_maximum_fusion.small_ref
  2.2 1.2 reshape.62.seg_ref
  3.4 145.2 %start_gather.1 = (bf16[8,128,2048]{2,1,0:T(8,128)(2,1)}, bf16[3,2048,256]{2,1,0:T(8,128)(2,1)}, bf16[256,2048]{1,0:T(8,128)(2,1)}, bf16[4,32,512]{2,1,0:T(8,128...) custom-call(bf16[128,2048]{1,0:T(8,128)(2,1)} %x_ref.3, bf16[3,512,2048]{2,1,0:T(8,128)(2,1)} %bitcast.33, ...), custom_call_target="tpu_custom_call" | custom-call | tf_op jit(solution)/shard_map/start_gather/pallas_call | solution.py:552
  149.4 0.9 slice_bitcast_fusion
  151.9 26.2 %attn_fwd.1 = (bf16[1024,2048]{1,0:T(8,128)(2,1)}, f32[1024,256]{1,0:T(8,128)}, f32[1024,256]{1,0:T(8,128)}, bf16[1024,256]{1,0:T(8,128)(2,1)}, bf16[1024,256]{1...) custom-call(bf16[8,128,2048]{2,1,0:T(8,128)(2,1)} %get-tuple-element, ...), custom_call_target="tpu_custom_call" | custom-call | tf_op jit(solution)/shard_map/attn_fwd/pallas_call | solution.py:706
  178.1 28.0 %scatter_tokens.1 = f32[128,2048]{1,0:T(8,128)} custom-call(bf16[8,128,2048]{2,1,0:T(8,128)(2,1)} %get-tuple-element.43.x_ref), custom_call_target="tpu_custom_call" | custom-call | tf_op jit(solution)/shard_map/scatter_tokens/pallas_call | solution.py:366
  206.2 1.5 multiply_reduce_fusion.2
  207.7 0.9 copy-done
  209.9 1.0 concatenate.18.h_ref
  210.9 196.3 %moe_net.1 = (bf16[32,128,2176]{2,1,0:T(8,128)(2,1)}, bf16[32,128,2048]{2,1,0:T(8,128)(2,1)}, f32[128,2176]{1,0:T(8,128)}, bf16[2048,1024]{1,0:T(8,128)(2,1)}, f32[512,2048]{1,0:T(8,128)}) custom-call(bf16[128,2176]{1,0:T(8,128)(2,1)} %concatenate.18.h_ref, bf16[32,128,2048]{2,1,0:T(8,128)(2,1)} %get-tuple-element.44.g_ref, bf16[2,2048,1024]{2,1,0:T(8,128)(2,1)} %wg_ref.1, ...), custom_call_target="tpu_custom_call" | custom-call | tf_op jit(solution)/shard_map/moe_net/pallas_call | solution.py:1678
  407.3 13.6 %all-to-all-start = ((bf16[4,512,1024]{2,1,0:T(8,128)(2,1)}), bf16[4,512,1024]{2,1,0:T(8,128)(2,1)}, u32[]{:S(2)}, u32[]{:S(2)}) async-start(bf16[4,512,1024]{2,1,0:T(8,128)(2,1)} %bitcast.35), calls=%async_computation | async-start | bytes 8388608 | tf_op jit(solution)/shard_map/all_to_all | solution.py:1769
  420.8 1.1 multiply_reduce_fusion.3
  421.9 1.1 multiply_convert_fusion.1
  423.0 1.7 multiply_reduce_fusion
  424.7 1.5 fusion.5
  426.2 22.9 %gather_tokens.1.gab_ref.mix_ref = bf16[8,128,2048]{2,1,0:T(8,128)(2,1)} custom-call(bf16[128,2048]{1,0:T(8,128)(2,1)} %get-tuple-element.69.x_ref), custom_call_target="tpu_custom_call" | custom-call | tf_op jit(solution)/shard_map/gather_tokens/pallas_call | solution.py:191
  449.1 38.5 %attn_bwd.1 = (bf16[8,128,2048]{2,1,0:T(8,128)(2,1)}, bf16[2048,1024]{1,0:T(8,128)(2,1)}, f32[8,256]{1,0:T(8,128)}, f32[128,2048]{1,0:T(8,128)}) custom-call(bf16[8,128,2048]{2,1,0:T(8,128)(2,1)} %gather_tokens.1.gab_ref.mix_ref, bf16[3,2048,256]{2,1,0:T(8,128)(2,1)} %get-tuple-element.39.wq_ref, bf16[256,2048]{1,0:T(8,128)(2,1)} %get-tuple-element.40.wo_ref, ...), custom_call_target="tpu_custom_call" | custom-call | tf_op jit(solution)/shard_map/attn_bwd/pallas_call | solution.py:856
  489.3 1.4 concatenate.19.tiny_ref
  490.6 164.3 %tail.1 = (bf16[128,2048]{1,0:T(8,128)(2,1)}, bf16[4,512,2048]{2,1,0:T(8,128)(2,1)}, f32[2,24,256]{2,1,0:T(8,128)}, bf16[128,2048]{1,0:T(8,128)(2,1)}) custom-call(bf16[2048,1024]{1,0:T(8,128)(2,1)} %get-tuple-element.54.parts_ref, bf16[8,128,2048]{2,1,0:T(8,128)(2,1)} %get-tuple-element.55.gh1_ref, bf16[32,128,2048]{2,1,0:T(8,128)(2,1)} %get-tuple-element.56.mix_ref, ...), custom_call_target="tpu_custom_call" | custom-call | tf_op jit(solution)/shard_map/tail/pallas_call | solution.py:1134
  655.0 1.3 slice.67
  657.7 4.1 bitcast_convert_fusion
  661.8 9.1 %convert_bitcast_fusion = f32[512,3,2048]{2,0,1:T(8,128)} fusion(bf16[4,512,2048]{2,1,0:T(8,128)(2,1)} %get-tuple-element.61), kind=kLoop, calls=%fused_computation | loop fusion | flops 3145728 | bytes 18874368 | tf_op jit(solution)/shard_map/transpose | solution.py:1807
  670.9 6.0 lay_experts.1
  678.5 4.7 copy.46
  (62 shorter events, 8.4 us)
Async XLA Ops:
  149.4 2.5 copy-start.12
  178.1 28.1 %copy-start.2 = (bf16[128,2048]{1,0:T(8,128)(2,1)S(1)}, bf16[128,2048]{1,0:T(8,128)(2,1)}, u32[]{:S(2)}) copy-start(bf16[128,2048]{1,0:T(8,128)(2,1)} %x_ref.3) | copy-start | bytes 1572868
  178.1 31.0 %copy-start.15 = (s32[128,8]{0,1:T(8,128)S(1)}, s32[128,8]{0,1:T(8,128)}, u32[]{:S(2)}) copy-start(s32[128,8]{0,1:T(8,128)} %param.13) | copy-start | bytes 12292
  207.6 1.0 copy-start
  207.7 1.4 copy-start.13
  207.7 1.4 copy-start.8
  209.2 0.6 copy-start.4
  209.3 0.6 copy-start.6
  407.2 13.6 %copy-start.5 = (f32[128,16]{1,0:T(8,128)S(1)}, f32[128,16]{1,0:T(8,128)}, u32[]{:S(2)}) copy-start(f32[128,16]{1,0:T(8,128)} %copy-done.4) | copy-start | bytes 24580
  407.2 13.6 %copy-start.7 = (f32[128,16]{1,0:T(8,128)S(1)}, f32[128,16]{1,0:T(8,128)}, u32[]{:S(2)}) copy-start(f32[128,16]{1,0:T(8,128)} %copy-done.6) | copy-start | bytes 24580
  407.2 15.8 %copy-start.1 = (f32[128,2048]{1,0:T(8,128)S(1)}, f32[128,2048]{1,0:T(8,128)}, u32[]{:S(2)}) copy-start(f32[128,2048]{1,0:T(8,128)} %copy-done) | copy-start | bytes 3145732
  407.2 15.8 %copy-start.9 = (bf16[4,2,8,512]{3,2,0,1:T(8,128)(2,1)S(1)}, bf16[4,2,8,512]{3,2,0,1:T(8,128)(2,1)}, u32[]{:S(2)}) copy-start(bf16[4,2,8,512]{3,2,0,1:T(8,128)(2,1)} %copy-done.8) | copy-start | bytes 196612
  407.2 15.8 %copy-start.14 = (f32[128]{0:T(128)S(1)}, f32[128]{0:T(128)}, u32[]{:S(2)}) copy-start(f32[128]{0:T(128)} %copy-done.13) | copy-start | bytes 1540
  407.2 17.5 %copy-start.3 = (bf16[128,2048]{1,0:T(8,128)(2,1)S(1)}, bf16[128,2048]{1,0:T(8,128)(2,1)}, u32[]{:S(2)}) copy-start(bf16[128,2048]{1,0:T(8,128)(2,1)} %cot_ref.1) | copy-start | bytes 1572868
  407.3 263.6 %all-to-all-start = ((bf16[4,512,1024]{2,1,0:T(8,128)(2,1)}), bf16[4,512,1024]{2,1,0:T(8,128)(2,1)}, u32[]{:S(2)}, u32[]{:S(2)}) async-start(bf16[4,512,1024]{2,1,0:T(8,128)(2,1)} %bitcast.35), calls=%async_computation | async-start | bytes 8388608 | tf_op jit(solution)/shard_map/all_to_all | solution.py:1769
  670.9 6.0 copy-start.11
  670.9 6.8 copy-start.10
